TPU v7x, 32 devices: a whole 2x2x4 slice. The times are simulated.
32 devices in a mesh: dp: 8 (over z, x), tensor: 4 (over y, core).
Axes of the slice: x: 2, y: 2, z: 4, core: 2. Of those that a mesh axis runs over, the one named last changes fastest.
Arguments:
- tokens: bfloat16 [64, 258, 768], P('dp'), may hold values from -6 to 6
- metadata: int32 [64], P('dp'), may hold values 0 or 1
- cotangent: bfloat16 [64, 258, 768], P('dp'), may hold values from -6 to 6
- w_query: bfloat16 [768, 768], P(None, 'tensor'), may hold values from -0.21875 to 0.21875
- w_key: bfloat16 [768, 768], P(None, 'tensor'), may hold values from -0.21875 to 0.21875
- w_value: bfloat16 [768, 768], P(None, 'tensor'), may hold values from -0.21875 to 0.21875
- w_out: bfloat16 [768, 768], P('tensor'), may hold values from -1.75 to 1.75
- b_query: float32 [768], P('tensor'), may hold values from -1.5 to 1.5
- b_value: float32 [768], P('tensor'), may hold values from -1.5 to 1.5
- b_out: float32 [768], replicated, may hold values from -1.5 to 1.5
- w_up: bfloat16 [768, 3072], P(None, 'tensor'), may hold values from -0.21875 to 0.21875
- b_up: float32 [3072], P('tensor'), may hold values from -1.5 to 1.5
- w_down: bfloat16 [3072, 768], P('tensor'), may hold values from -0.21875 to 0.21875
- b_down: float32 [768], replicated, may hold values from -1.5 to 1.5
- gain_one: float32 [768], replicated, may hold values from 0.25 to 1.75
- shift_one: float32 [768], replicated, may hold values from -1.5 to 1.5
- gain_two: float32 [768], replicated, may hold values from 0.25 to 1.75
- shift_two: float32 [768], replicated, may hold values from -1.5 to 1.5
Outputs:
- layer_out: bfloat16 [64, 258, 768], P('dp')
- grad_tokens: float32 [64, 258, 768], P('dp')
- grad_w_query: float32 [768, 768], P(None, 'tensor')
- grad_w_key: float32 [768, 768], P(None, 'tensor')
- grad_w_value: float32 [768, 768], P(None, 'tensor')
- grad_w_out: float32 [768, 768], P('tensor')
- grad_b_query: float32 [768], P('tensor')
- grad_b_value: float32 [768], P('tensor')
- grad_b_out: float32 [768], replicated
- grad_w_up: float32 [768, 3072], P(None, 'tensor')
- grad_b_up: float32 [3072], P('tensor')
- grad_w_down: float32 [3072, 768], P('tensor')
- grad_b_down: float32 [768], replicated
- grad_gain_one: float32 [768], replicated
- grad_shift_one: float32 [768], replicated
- grad_gain_two: float32 [768], replicated
- grad_shift_two: float32 [768], replicated
All inputs are finite; a program needn't handle non-finite values. No bound on the sum of `metadata` on one device may be relied on, other than what follows from the above.
Results may differ from a plain program's by a relative error of at most 0.012.
Values sent between devices are 32-bit elements; how exact they have to be, the bound alone decides.
A program may use at most 192 MiB of HBM per device.

v0:
```python
import math

import jax
import jax.numpy as jnp
from jax import lax
from jax.sharding import PartitionSpec as P

HEAD_DIM = 64


NORM_EPSILON = 1e-05


def layer_norm(source_tokens, gain, shift):
    average = jnp.mean(source_tokens, -1, keepdims=True)
    mean_removed = source_tokens - average
    variance = jnp.mean(mean_removed * mean_removed, -1, keepdims=True)
    return mean_removed * lax.rsqrt(variance + NORM_EPSILON) * gain + shift


def gelu_exact(source_tokens):
    return jax.nn.gelu(source_tokens, approximate=False)


def multiply(left_mat, right_mat):
    return jnp.dot(left_mat, right_mat, preferred_element_type=jnp.float32)


def contract_rows(left_mat, right_mat):
    return lax.dot_general(
        left_mat, right_mat, (((0,), (0,)), ((), ())), preferred_element_type=jnp.float32
    )


def contract_cols(left_mat, right_mat):
    return lax.dot_general(
        left_mat, right_mat, (((1,), (1,)), ((), ())), preferred_element_type=jnp.float32
    )


def column_sums(matrix):
    return jnp.sum(matrix.astype(jnp.float32), 0)


def shards(
    tokens,
    metadata,
    cotangent,
    w_query,
    w_key,
    w_value,
    w_out,
    b_query,
    b_value,
    b_out,
    w_up,
    b_up,
    w_down,
    b_down,
    gain_one,
    shift_one,
    gain_two,
    shift_two,
):
    samples, length, model_width = tokens.shape
    row_count = samples * length
    local_width = w_query.shape[1]
    local_heads = local_width // HEAD_DIM
    score_scale = 1.0 / math.sqrt(HEAD_DIM)
    position = lax.broadcasted_iota(jnp.int32, (samples, length), 1)
    keep_mask = jnp.where(
        position == 1, metadata[:, None].astype(jnp.float32), jnp.float32(1.0)
    ).reshape(row_count, 1)
    inputs = tokens.reshape(row_count, model_width).astype(jnp.float32) * keep_mask

    def split_heads(matrix):
        return matrix.reshape(samples, length, local_heads, HEAD_DIM)

    normed, first_norm_backward = jax.vjp(layer_norm, inputs, gain_one, shift_one)
    normed_low = normed.astype(jnp.bfloat16)
    queries = (multiply(normed_low, w_query) + b_query).astype(jnp.bfloat16)
    key_rows = multiply(normed_low, w_key).astype(jnp.bfloat16)
    values = (multiply(normed_low, w_value) + b_value).astype(jnp.bfloat16)
    head_queries = split_heads(queries)
    head_keys = split_heads(key_rows)
    head_values = split_heads(values)
    scores = (
        jnp.einsum("sqhc,skhc->shqk", head_queries, head_keys, preferred_element_type=jnp.float32)
        * score_scale
    )
    row_max = jnp.max(scores, -1, keepdims=True)
    row_total = jnp.sum(jnp.exp(scores - row_max), -1, keepdims=True)
    logsum = row_max + jnp.log(row_total)
    probs_low = jnp.exp(scores - logsum).astype(jnp.bfloat16)
    mixture = jnp.einsum(
        "shqk,skhc->sqhc", probs_low, head_values, preferred_element_type=jnp.float32
    )
    mixture = mixture.reshape(row_count, local_width).astype(jnp.bfloat16)
    branch = lax.psum(multiply(mixture, w_out), "tensor") + b_out
    middle = inputs + branch
    normed_two, norm_two_back = jax.vjp(layer_norm, middle, gain_two, shift_two)
    normed_two_low = normed_two.astype(jnp.bfloat16)
    hidden = multiply(normed_two_low, w_up) + b_up
    active, gelu_back = jax.vjp(gelu_exact, hidden)
    active_reduced = active.astype(jnp.bfloat16)
    branch_two = lax.psum(multiply(active_reduced, w_down), "tensor") + b_down
    layer_out = (middle + branch_two).astype(jnp.bfloat16).reshape(samples, length, model_width)
    grad_out = cotangent.reshape(row_count, model_width).astype(jnp.float32)
    grad_out_low = grad_out.astype(jnp.bfloat16)
    grad_b_down = column_sums(grad_out_low)
    grad_w_down = contract_rows(active_reduced, grad_out_low)
    grad_active = contract_cols(grad_out_low, w_down)
    grad_hidden = gelu_back(grad_active)[0].astype(jnp.bfloat16)
    grad_b_up = column_sums(grad_hidden)
    grad_w_up = contract_rows(normed_two_low, grad_hidden)
    grad_normed_two = lax.psum(contract_cols(grad_hidden, w_up), "tensor")
    grad_mid_part, grad_gain_two, grad_shift_two = norm_two_back(grad_normed_two)
    grad_middle = grad_out + grad_mid_part
    mlp_group = (grad_w_up, grad_b_up, grad_w_down, grad_b_down, grad_gain_two, grad_shift_two)
    grad_mid_low = grad_middle.astype(jnp.bfloat16)
    grad_b_out = column_sums(grad_mid_low)
    grad_w_out = contract_rows(mixture, grad_mid_low)
    grad_mixture = split_heads(contract_cols(grad_mid_low, w_out).astype(jnp.bfloat16))
    scores_again = (
        jnp.einsum("sqhc,skhc->shqk", head_queries, head_keys, preferred_element_type=jnp.float32)
        * score_scale
    )
    attn_probs = jnp.exp(scores_again - logsum)
    probs_again = attn_probs.astype(jnp.bfloat16)
    grad_values = jnp.einsum(
        "shqk,sqhc->skhc", probs_again, grad_mixture, preferred_element_type=jnp.float32
    )
    grad_values = grad_values.reshape(row_count, local_width).astype(jnp.bfloat16)
    grad_probs = jnp.einsum(
        "sqhc,skhc->shqk", grad_mixture, head_values, preferred_element_type=jnp.float32
    )
    grad_scores = attn_probs * (grad_probs - jnp.sum(attn_probs * grad_probs, -1, keepdims=True))
    grad_scores = grad_scores.astype(jnp.bfloat16)
    grad_queries = (
        jnp.einsum("shqk,skhc->sqhc", grad_scores, head_keys, preferred_element_type=jnp.float32)
        * score_scale
    )
    grad_queries = grad_queries.reshape(row_count, local_width).astype(jnp.bfloat16)
    grad_keys = (
        jnp.einsum("shqk,sqhc->skhc", grad_scores, head_queries, preferred_element_type=jnp.float32)
        * score_scale
    )
    grad_keys = grad_keys.reshape(row_count, local_width).astype(jnp.bfloat16)
    grad_w_query = contract_rows(normed_low, grad_queries)
    grad_w_key = contract_rows(normed_low, grad_keys)
    grad_w_value = contract_rows(normed_low, grad_values)
    grad_b_query = column_sums(grad_queries)
    grad_b_value = column_sums(grad_values)
    grad_normalized_piece = (
        contract_cols(grad_queries, w_query)
        + contract_cols(grad_keys, w_key)
        + contract_cols(grad_values, w_value)
    )
    grad_normed = lax.psum(grad_normalized_piece, "tensor")
    grad_in_part, grad_gain_one, grad_shift_one = first_norm_backward(grad_normed)
    grad_tokens = ((grad_middle + grad_in_part) * keep_mask).reshape(samples, length, model_width)
    attn_group = (
        grad_w_query,
        grad_w_key,
        grad_w_value,
        grad_w_out,
        grad_b_query,
        grad_b_value,
        grad_b_out,
        grad_gain_one,
        grad_shift_one,
    )
    summed = lax.psum(mlp_group + attn_group, "dp")
    mlp_group = summed[:6]
    attn_group = summed[6:]
    return (
        layer_out,
        grad_tokens,
        attn_group[0],
        attn_group[1],
        attn_group[2],
        attn_group[3],
        attn_group[4],
        attn_group[5],
        attn_group[6],
        mlp_group[0],
        mlp_group[1],
        mlp_group[2],
        mlp_group[3],
        attn_group[7],
        attn_group[8],
        mlp_group[4],
        mlp_group[5],
    )


def solution(mesh):
    return jax.shard_map(
        shards,
        mesh=mesh,
        in_specs=(
            P("dp", None, None),
            P("dp"),
            P("dp", None, None),
            P(None, "tensor"),
            P(None, "tensor"),
            P(None, "tensor"),
            P("tensor", None),
            P("tensor"),
            P("tensor"),
            P(),
            P(None, "tensor"),
            P("tensor"),
            P("tensor", None),
            P(),
            P(),
            P(),
            P(),
            P(),
        ),
        out_specs=(
            P("dp", None, None),
            P("dp", None, None),
            P(None, "tensor"),
            P(None, "tensor"),
            P(None, "tensor"),
            P("tensor", None),
            P("tensor"),
            P("tensor"),
            P(),
            P(None, "tensor"),
            P("tensor"),
            P("tensor", None),
            P(),
            P(),
            P(),
            P(),
            P(),
        ),
        check_vma=False,
    )
```

profile of v0, /device:TPU:0, one launch (start us, length us, event | category | flops | bytes accessed | tf_op | source)
XLA Modules:
  0.0 897.5 jit_solution(9342128070286131994)
XLA Ops:
  11.4 5.4 copy.99
  19.3 5.0 reshape.276
  38.4 4.0 fusion.9
  59.0 4.2 copy.109
  63.2 3.8 reshape.273
  67.0 115.3 %all-reduce.8.cloned.1.call-done = f32[2064,768]{1,0:T(8,128)} async-done(((f32[2064,768]{1,0:T(8,128)}), f32[2064,768]{1,0:T(8,128)}) %all-reduce.8.cloned.1.call-update) | async-done | bytes 6340624 | tf_op jit(solution)/shard_map/psum | solution.py:99
  182.3 5.8 fusion.34
  194.3 18.7 %convert_reduce_fusion.1 = (f32[768]{0:T(1024)}, bf16[2064,768]{1,0:T(8,128)(2,1)S(1)}, f32[2064,768]{1,0:T(8,128)}) fusion(f32[2064,768]{1,0:T(8,128)S(1)} %convolution_add_fusion, bf16[2064,768]{1,0:T(8,128)(2,1)S(1)} %copy-done.8, bf16[768,768]{1,0:T(8,128)(2,1)S(1)} %copy-done), kind=kOutput, calls=%fused_computation.12 | convolution fusion | flops 2552093952 | bytes 20204544 | tf_op jit(solution)/shard_map/dot_general | solution.py:36
  214.7 4.6 fusion.37
  219.4 5.5 multiply_convert_fusion.1
  226.6 5.0 fusion.36
  231.5 108.7 %all-reduce.10.cloned.1.call-done = f32[2064,768]{1,0:T(8,128)} async-done(((f32[2064,768]{1,0:T(8,128)}), f32[2064,768]{1,0:T(8,128)}) %all-reduce.10.cloned.1.call-update) | async-done | bytes 6340624 | tf_op jit(solution)/shard_map/psum | solution.py:116
  340.2 6.5 multiply_reduce_fusion.2
  346.7 6.8 fusion.33
  360.6 6.8 convert_reduce_fusion.3
  367.3 7.6 multiply_reduce_fusion
  375.0 10.9 %multiply_convert_fusion = bf16[8,3,258,258]{2,3,1,0:T(8,128)(2,1)} fusion(f32[8,3,258,258]{2,3,1,0:T(8,128)} %get-tuple-element.124, f32[8,3,258,258]{2,3,1,0:T(8,128)} %copy-done.2, f32[8,3,258]{2,1,0:T(4,128)S(1)} %get-tuple-element.123, f32[8,3,258]{2,1,0:T(4,128)S(1)} %log_add_fusion), kind=kLoop, calls=%fused_computation | loop fusion | flops 7987680 | bytes 16024896 | tf_op jit(solution)/shard_map/convert_element_type | solution.py:138
  385.9 5.5 fusion.13
  407.9 3.7 add_add_fusion.2
  422.1 7.4 fusion.41
  429.5 4.4 fusion.42
  443.4 191.5 %all-reduce.14.cloned.1.call-done = (f32[2064,768]{1,0:T(8,128)}, f32[2064,768]{1,0:T(8,128)}) async-done(((f32[2064,768]{1,0:T(8,128)}, f32[2064,768]{1,0:T(8,128)}), (f32[2064,768]{1,0:T(8,128)}, f32[2064,768]{1,0:T(8,128)})) %all-reduce.14.cloned.1.call-update) | async-done | bytes 12681232 | tf_op jit(solution)/shard_map/psum | solution.py:106
  634.9 7.2 add_convert_fusion.2
  642.2 3.8 reshape.272
  646.0 5.1 copy.123
  651.1 7.1 multiply_reduce_fusion.3
  658.3 7.8 fusion.32
  666.0 7.5 add_multiply_fusion
  673.5 5.1 reshape.275
  678.6 7.7 copy.124
  686.3 39.8 %all-reduce = (f32[192]{0:T(256)}, f32[192]{0:T(256)}, f32[768]{0:T(1024)}, f32[768]{0:T(1024)}, f32[768]{0:T(1024)}, /*index=5*/f32[768]{0:T(1024)}, f32[768]{0:T(1024)}, f32[768]{0:T(1024)}, f32[768]{0:T(1024)}) all-reduce(f32[192]{0:T(256)S(1)} %reduce_sum.218, ...), channel_id=1, replica_groups=mesh['dp'=8,'tensor'=4] {'dp'}, use_global_device_ids=true, to_apply=%region_20.21 | all-reduce | flops 5760 | bytes 46080 | tf_op jit(solution)/shard_map/psum | solution.py:173
  726.1 153.7 %all-reduce.12.cloned.1.call-done = (f32[768,192]{0,1:T(8,128)}, f32[768,192]{0,1:T(8,128)}, f32[768,192]{0,1:T(8,128)}, f32[192,768]{1,0:T(8,128)}, f32[768,768]{1,0:T(8,128)}, /*index=5*/f32[768,768]{1,0:T(8,128)}) async-done(((f32[768,192]{0,1:T(8,128)}, f32[768,192]{0,1:T(8,128)}, f32[768,192]{0,1:T(8,128)}, f32[192,768]{1,0:T(8,128)}, f32[768,768]{1,0:T(8,128)}, /*index=5*/f32[768,768]{1,0:T(8,128)}), ...) | async-done | bytes 7077904 | tf_op jit(solution)/shard_map/psum | solution.py:173
  (211 shorter events, 100.6 us)
Async XLA Ops:
  7.2 186.8 %copy-start = (bf16[768,768]{1,0:T(8,128)(2,1)S(1)}, bf16[768,768]{1,0:T(8,128)(2,1)}, u32[]{:S(2)}) copy-start(bf16[768,768]{1,0:T(8,128)(2,1)} %param.30) | copy-start | bytes 3538948
  7.2 175.1 %all-reduce.8.cloned.1.call-start = ((), (), s32[]{:S(2)}) async-start(), calls=%async_computation | async-start | bytes 12681216 | tf_op jit(solution)/shard_map/psum | solution.py:99
  8.2 174.1 %copy-start.35 = (f32[2064]{0:T(1024)}, f32[2064]{0:T(1024)S(1)}, u32[]{:S(2)}) copy-start(f32[2064]{0:T(1024)S(1)} %select_n.13) | copy-start | bytes 24772
  8.3 8.5 copy-start.31
  11.3 13.1 %copy-start.43 = (f32[2064]{0:T(1024)}, f32[2064]{0:T(1024)S(1)}, u32[]{:S(2)}) copy-start(f32[2064]{0:T(1024)S(1)} %div.39) | copy-start | bytes 24772
  31.0 7.4 copy-start.38
  31.0 7.4 copy-start.64
  32.4 12.7 %copy-start.12 = (bf16[8,258,3,64]{1,0,3,2:T(8,128)(2,1)}, bf16[8,258,3,64]{1,0,3,2:T(8,128)(2,1)S(1)}, u32[]{:S(2)}) copy-start(bf16[8,258,3,64]{1,0,3,2:T(8,128)(2,1)S(1)} %reshape.271) | copy-start | bytes 2377732
  58.9 123.4 %copy-start.57 = (f32[768]{0:T(1024)S(1)}, f32[768]{0:T(1024)}, u32[]{:S(2)}) copy-start(f32[768]{0:T(1024)} %param.27) | copy-start | bytes 9220
  58.9 281.3 %all-reduce.10.cloned.1.call-start = ((), (), s32[]{:S(2)}) async-start(), calls=%async_computation.1 | async-start | bytes 12681216 | tf_op jit(solution)/shard_map/psum | solution.py:116
  194.3 18.7 %copy-start.23 = (f32[2064,768]{1,0:T(8,128)}, f32[2064,768]{1,0:T(8,128)S(1)}, u32[]{:S(2)}) copy-start(f32[2064,768]{1,0:T(8,128)S(1)} %convolution_add_fusion) | copy-start | bytes 19021828
  219.4 415.6 %all-reduce.14.cloned.1.call-start = ((), (), s32[]{:S(2)}) async-start(), calls=%async_computation.3 | async-start | bytes 25362432 | tf_op jit(solution)/shard_map/psum | solution.py:106
  374.9 10.9 %copy-start.15 = (bf16[8,258,3,64]{1,0,3,2:T(8,128)(2,1)S(1)}, bf16[8,258,3,64]{1,0,3,2:T(8,128)(2,1)}, u32[]{:S(2)}) copy-start(bf16[8,258,3,64]{1,0,3,2:T(8,128)(2,1)} %copy-done.14) | copy-start | bytes 2377732
  392.8 13.0 %copy-start.39 = (bf16[768,192]{0,1:T(8,128)(2,1)S(1)}, bf16[768,192]{0,1:T(8,128)(2,1)}, u32[]{:S(2)}) copy-start(bf16[768,192]{0,1:T(8,128)(2,1)} %param.21) | copy-start | bytes 884740
  396.6 11.3 %copy-start.21 = (bf16[2064,192]{0,1:T(8,128)(2,1)}, bf16[2064,192]{0,1:T(8,128)(2,1)S(1)}, u32[]{:S(2)}) copy-start(bf16[2064,192]{0,1:T(8,128)(2,1)S(1)} %convert_element_type.155) | copy-start | bytes 2377732
  411.7 468.1 %all-reduce.12.cloned.1.call-start = ((), (), s32[]{:S(2)}) async-start(), calls=%async_computation.2 | async-start | bytes 14155776 | tf_op jit(solution)/shard_map/psum | solution.py:173
  422.1 7.4 copy-start.10
  422.1 7.4 copy-start.27
  439.1 195.8 %copy-start.59 = (f32[768]{0:T(1024)S(1)}, f32[768]{0:T(1024)}, u32[]{:S(2)}) copy-start(f32[768]{0:T(1024)} %param.31) | copy-start | bytes 9220
  642.2 8.9 copy-start.36
  642.2 8.9 copy-start.44
  642.2 8.9 copy-start.46
  646.0 12.2 %slice-start = ((s8[6340608]{0:T(1024)(128)(4,1)}), s8[4194304]{0:T(1024)(128)(4,1)S(1)}, s32[]{:S(2)}) async-start(s8[6340608]{0:T(1024)(128)(4,1)} %bitcast.70), calls=%async_computation.4 | async-start | bytes 8388608
  651.1 7.1 copy-start.48
  651.1 7.2 slice-start.1
  658.2 7.8 copy-start.11
  678.6 7.7 copy-start.53
  678.6 7.7 copy-start.54
  678.6 7.7 copy-start.60
  879.8 7.9 copy-start.30
  879.8 9.3 %copy-start.29 = (f32[768,768]{1,0:T(8,128)S(1)}, f32[768,768]{1,0:T(8,128)}, u32[]{:S(2)}) copy-start(f32[768,768]{1,0:T(8,128)} %get-tuple-element.140) | copy-start | bytes 7077892
  879.8 10.7 %copy-start.1 = (bf16[768,768]{1,0:T(8,128)(2,1)S(1)}, bf16[768,768]{1,0:T(8,128)(2,1)}, u32[]{:S(2)}) copy-start(bf16[768,768]{1,0:T(8,128)(2,1)} %param.30) | copy-start | bytes 3538948
  (40 other events, 132.0 us)
Sparse Core Ops, SparseCore 0:
  59.0 123.2 all-reduce.7
  219.5 120.6 all-reduce.9
  411.8 223.0 all-reduce.13
  641.8 237.9 all-reduce.11
where the time goes:
time: 906 us; the launch traced here: 897 us
  waiting for transfers between devices  569 us (63%)
  matrix products  94.5 us (10%)
  local copies, waits for them, and re-layouts  91.9 us (10%)
  other arithmetic  86.9 us (10%)
  blocking collectives  39.8 us (4%)
  between operations  15 us (2%)
    psum x1, waiting for transfers between devices, shards(): branch_two = lax.psum(multiply(active_reduced, w_down), 'tensor') + b_down  192 us
    psum x1, waiting for transfers between devices, shards(): summed = lax.psum(mlp_group + attn_group, 'dp')  154 us
    psum x1, waiting for transfers between devices, shards(): branch = lax.psum(multiply(mixture, w_out), 'tensor') + b_out  115 us
    psum x1, waiting for transfers between devices, shards(): grad_normed_two = lax.psum(contract_cols(grad_hidden, w_up), 'tensor')  109 us
    psum x1, blocking collectives, shards(): summed = lax.psum(mlp_group + attn_group, 'dp')  39.8 us
    unnamed x145, local copies, waits for them, and re-layouts  37.1 us
    dot_general x6, matrix products, contract_cols(): lax.dot_general(left_mat, right_mat, (((1,), (1,)), ((), ())), preferred_...  30.3 us
    dot_general x6, matrix products, multiply(): return jnp.dot(left_mat, right_mat, preferred_element_type=jnp.float32)  20.2 us
  transfers between devices with their start and end apart: 4, of which 4 were waited for; matrix products, arithmetic and copies ran while one was open for 11% of the time, Pallas kernels for 0%

commit v1 on v0

v1 whole, which is shorter than its diff:
```python
import math

import jax
import jax.numpy as jnp
from jax import lax
from jax.experimental import pallas as pl
from jax.experimental.pallas import tpu as pltpu
from jax.sharding import PartitionSpec as P

HEAD_DIM = 64
EPS = 1e-05
MESH = pl.DeviceIdType.MESH
f32 = jnp.float32
bf16 = jnp.bfloat16
VMEM_LIMIT = 61 << 20
TAIL_P = 0.24
TAIL = (
    0.08952743306829739,
    0.15551359433427508,
    -0.15404885518029288,
    0.6255903019940591,
    -0.6460706945688248,
    0.5545739487327468,
    -0.12508572868970558,
)
INV_SQRT_2PI = 1.0 / math.sqrt(2.0 * math.pi)
HALF_LOG2E = -0.5 / math.log(2.0)


def mm(a, b):
    return lax.dot_general(a, b, (((1,), (0,)), ((), ())), preferred_element_type=f32)


def mmt(a, b):
    return lax.dot_general(a, b, (((1,), (1,)), ((), ())), preferred_element_type=f32)


def tmm(a, b):
    return lax.dot_general(a, b, (((0,), (0,)), ((), ())), preferred_element_type=f32)


def loop(n, fn):
    def body(i, carry):
        fn(i)
        return carry

    lax.fori_loop(0, n, body, 0)


def al(i, step):
    return pl.ds(pl.multiple_of(i * step, step), step)


def centred(x):
    d = x.shape[-1]
    mu = jnp.sum(x, -1, keepdims=True) * (1.0 / d)
    xm = x - mu
    var = jnp.sum(xm * xm, -1, keepdims=True) * (1.0 / d)
    r = lax.rsqrt(var + EPS)
    return xm * r, r


def gelu_pair(v):
    d = 1.0 + TAIL_P * jnp.abs(v)
    t = pltpu.reciprocal(d, approx=True)
    t = t * (2.0 - d * t)
    e = jnp.exp2(HALF_LOG2E * (v * v))
    acc = TAIL[6] * t + TAIL[5]
    for k in range(4, -1, -1):
        acc = acc * t + TAIL[k]
    q = (acc * t) * e
    cdf = jnp.where(v < 0, q, 1.0 - q)
    return v * cdf, cdf + (v * e) * INV_SQRT_2PI


def fold8(x):
    return jnp.sum(x.reshape(x.shape[0] // 8, 8, x.shape[1]), 0)


class Dims:
    def __init__(self, tokens, w_up, n_t):
        self.samples, self.length, self.d = tokens.shape
        self.ns = self.samples // 2
        self.r = -(-self.length // 16) * 16
        self.rows = self.ns * self.r
        self.f = w_up.shape[1]
        self.ff = self.f * n_t
        self.n_t = n_t
        self.heads = self.d // HEAD_DIM
        self.pairs = self.heads // 2
        self.hw = self.d // n_t


def masked_input(tok, meta, r0, ch, R):
    x = tok[pl.ds(r0, ch), :].astype(f32)
    samp = (r0 + (ch - 2)) // R
    rows = lax.broadcasted_iota(jnp.int32, (ch, 1), 0) + r0
    keep = jnp.where(rows == samp * R + 1, meta[samp].astype(f32), 1.0)
    return x, keep


CH = 64


def forward_body(dm, y, meta, tok, cot, wqkv, wo, wup, wdn, vec, p_hbm, normed, q8, kk, vv, mixt, n2, gp, mid, lout, dwd, act, pbuf, psem):
    R, D, NS = dm.r, dm.d, dm.ns
    g1, s1, g2, s2 = (vec[i : i + 1, :] for i in range(4))
    bo, bd, bq, bv = (vec[i : i + 1, :] for i in range(4, 8))
    nt = D // 256

    def ln1(i):
        r0 = pl.multiple_of(i * CH, CH)
        x, keep = masked_input(tok, meta, r0, CH, R)
        xh, _ = centred(x * keep)
        normed[pl.ds(r0, CH), :] = (xh * g1 + s1).astype(bf16)

    loop(dm.rows // CH, ln1)

    def qkv(s):
        rs = al(s, R)
        n = normed[rs, :]
        for j in range(nt):
            c = slice(j * 256, j * 256 + 256)
            q8[rs, c] = (mmt(n, wqkv[c, :]) + bq[:, c]).astype(bf16) * jnp.bfloat16(0.125)
            kk[rs, c] = mmt(n, wqkv[D + j * 256 : D + j * 256 + 256, :]).astype(bf16)
            vv[rs, c] = (mmt(n, wqkv[2 * D + j * 256 : 2 * D + j * 256 + 256, :]) + bv[:, c]).astype(bf16)

    loop(NS, qkv)
    lane = lax.broadcasted_iota(jnp.int32, (1, 128), 1)
    masks = (lane < HEAD_DIM, lane >= HEAD_DIM)
    tail = R - 16
    live = lax.broadcasted_iota(jnp.int32, (16, 1), 0) < dm.length - tail

    def p_copy(i):
        slot = lax.rem(i, 2)
        return pltpu.make_async_copy(pbuf.at[slot], p_hbm.at[i], psem.at[slot])

    def attn(i):
        s, p = i // dm.pairs, lax.rem(i, dm.pairs)
        slot = lax.rem(i, 2)
        rs, cs = al(s, R), al(p, 128)

        @pl.when(i >= 2)
        def _():
            p_copy(i - 2).wait()

        q, k, v = q8[rs, cs], kk[rs, cs], vv[rs, cs]
        for h in range(2):
            st = mmt(jnp.where(masks[h], k, jnp.bfloat16(0)), q)
            sa = st[:tail]
            sb = jnp.where(live, st[tail:], -1e30)
            m = jnp.maximum(jnp.max(sa, 0, keepdims=True), jnp.max(sb, 0, keepdims=True))
            ea, eb = jnp.exp(sa - m), jnp.exp(sb - m)
            inv = 1.0 / (jnp.sum(ea, 0, keepdims=True) + jnp.sum(eb, 0, keepdims=True))
            pbuf[slot, h, :tail, :] = (ea * inv).astype(bf16)
            pbuf[slot, h, tail:, :] = (eb * inv).astype(bf16)
            o = tmm(v, pbuf[slot, h])
            hr = pl.ds(pl.multiple_of(p * 128 + h * HEAD_DIM, HEAD_DIM), HEAD_DIM)
            mixt[s, hr, :] = o[h * HEAD_DIM : (h + 1) * HEAD_DIM].astype(bf16)
        p_copy(i).start()

    total = NS * dm.pairs
    loop(total, attn)
    p_copy(total - 2).wait()
    p_copy(total - 1).wait()

    def outp(s):
        rs = al(s, R)
        a = mixt[s]
        for j in range(nt):
            c = slice(j * 256, j * 256 + 256)
            mid[rs, c] = tmm(a, wo[:, c])

    loop(NS, outp)

    def ln2(i):
        r0 = pl.multiple_of(i * CH, CH)
        x, keep = masked_input(tok, meta, r0, CH, R)
        m = x * keep + (mid[pl.ds(r0, CH), :] + bo)
        mid[pl.ds(r0, CH), :] = m
        xh, _ = centred(m)
        n2[pl.ds(r0, CH), :] = (xh * g2 + s2).astype(bf16)

    loop(dm.rows // CH, ln2)
    ft = dm.f // 256

    def mlp(i):
        s, j = i // (dm.ff // 256), lax.rem(i, dm.ff // 256)
        rs = al(s, R)
        sh, cs = j // ft, al(lax.rem(j, ft), 256)
        h = mm(n2[rs, :], wup[sh, :, cs]) + vec[pl.ds(8 + sh, 1), cs]
        a, g = gelu_pair(h)
        act[rs, al(j, 256)] = a.astype(bf16)
        gp[rs, al(j, 256)] = g.astype(bf16)

    loop(NS * (dm.ff // 256), mlp)

    def dwdn(i):
        sh, j = i // ft, lax.rem(i, ft)
        for n in range(nt):
            c = slice(n * 256, n * 256 + 256)
            dwd[sh, al(j, 256), c] = tmm(act[:, al(2 * y * ft + i, 256)], cot[:, c])

    loop(2 * ft, dwdn)

    def mlp2(s):
        rs = al(s, R)
        for j in range(nt):
            c = slice(j * 256, j * 256 + 256)
            lout[rs, c] = mid[rs, c] + (mm(act[rs, :], wdn[:, c]) + bd[:, c])

    loop(NS, mlp2)


def backward_body(dm, y, meta, tok, cot, wqkv, wo, wup, wdn, vec, p_hbm, normed, q8, kk, vv, mixt, n2, gp, mid, gml, gmix, dqt, gn, dwu, dwa, acc, pbuf, psem):
    R, D, NS = dm.r, dm.d, dm.ns
    nt, ft = D // 256, dm.f // 256
    g1, g2 = vec[0:1, :], vec[2:3, :]
    acc[...] = jnp.zeros_like(acc)

    def ghid(i):
        s, j = i // (dm.ff // 256), lax.rem(i, dm.ff // 256)
        rs, cs = al(s, R), al(j, 256)
        ga = mmt(cot[rs, :], wdn[cs, :])
        gp[rs, cs] = (ga * gp[rs, cs].astype(f32)).astype(bf16)

    loop(NS * (dm.ff // 256), ghid)

    def gnorm2(s):
        rs = al(s, R)
        for j in range(nt):
            c = slice(j * 256, j * 256 + 256)
            tot = None
            for sh in range(dm.n_t):
                t = mmt(gp[rs, sh * dm.f : (sh + 1) * dm.f], wup[sh, c, :])
                tot = t if tot is None else tot + t
            gn[rs, c] = tot

    loop(NS, gnorm2)

    def ln2b(i):
        rs = pl.ds(pl.multiple_of(i * CH, CH), CH)
        xh, r = centred(mid[rs, :])
        go = gn[rs, :]
        co = cot[rs, :].astype(f32)
        g = go * g2
        gx = g * xh
        gm = co + r * (g - jnp.sum(g, -1, keepdims=True) * (1.0 / D) - xh * (jnp.sum(gx, -1, keepdims=True) * (1.0 / D)))
        mid[rs, :] = gm
        gl = gm.astype(bf16)
        gml[rs, :] = gl
        acc[0] += fold8(co)
        acc[1] += fold8(gl.astype(f32))
        acc[4] += fold8(go * xh)
        acc[5] += fold8(go)

    loop(dm.rows // CH, ln2b)

    def gmixf(s):
        rs = al(s, R)
        for j in range(nt):
            c = slice(j * 256, j * 256 + 256)
            gmix[rs, c] = mmt(gml[rs, :], wo[c, :]).astype(bf16)

    loop(NS, gmixf)

    def dwup(i):
        sh, j = i // nt, lax.rem(i, nt)
        for n in range(ft):
            dwu[sh, al(j, 256), n * 256 : n * 256 + 256] = tmm(n2[:, al(j, 256)], gp[:, al((2 * y + sh) * ft + n, 256)])

    loop(2 * nt, dwup)
    ones = jnp.ones((8, dm.rows), bf16)
    for sh in range(2):
        acc[6 + sh, :, : dm.f] = mm(ones, gp[:, al(2 * y + sh, dm.f)]) * 0.125
    hw = dm.hw
    own = al(y, 2 * hw)

    def over_samples(fn):
        tot = None
        for s in range(NS):
            t = fn(s)
            tot = t if tot is None else tot + t
        return tot

    for n in range(nt):
        c = slice(n * 256, n * 256 + 256)
        t = over_samples(lambda s: mm(mixt[s, own, :], gml[s * R : s * R + R, c]))
        for sh in range(2):
            dwa[sh, 3 * hw : 4 * hw, c] = t[sh * hw : (sh + 1) * hw]

    lane = lax.broadcasted_iota(jnp.int32, (1, 128), 1)
    masks = (lane < HEAD_DIM, lane >= HEAD_DIM)
    total = NS * dm.pairs

    def p_copy(i):
        slot = lax.rem(i, 2)
        return pltpu.make_async_copy(p_hbm.at[i], pbuf.at[slot], psem.at[slot])

    p_copy(0).start()

    def attn(i):
        s, p = i // dm.pairs, lax.rem(i, dm.pairs)
        slot = lax.rem(i, 2)
        rs, cs = al(s, R), al(p, 128)

        @pl.when(i + 1 < total)
        def _():
            p_copy(i + 1).start()

        p_copy(i).wait()
        q, k, v, do = q8[rs, cs], kk[rs, cs], vv[rs, cs], gmix[rs, cs]
        dv, dk = [], []
        for h in range(2):
            pt = pbuf[slot, h]
            pf = pt.astype(f32)
            dp = mmt(jnp.where(masks[h], v, jnp.bfloat16(0)), do)
            dsum = jnp.sum(pf * dp, 0, keepdims=True)
            ds = (pf * (dp - dsum)).astype(bf16)
            dv.append(mm(pt, do))
            dk.append(mm(ds, q))
            o = tmm(k, ds)
            hr = pl.ds(pl.multiple_of(p * 128 + h * HEAD_DIM, HEAD_DIM), HEAD_DIM)
            dqt[s, hr, :] = (o[h * HEAD_DIM : (h + 1) * HEAD_DIM] * 0.125).astype(bf16)
        kk[rs, cs] = jnp.where(masks[0], dk[0], dk[1]).astype(bf16)
        vv[rs, cs] = jnp.where(masks[0], dv[0], dv[1]).astype(bf16)

    loop(total, attn)

    for n in range(nt):
        c = slice(n * 256, n * 256 + 256)
        t = over_samples(lambda s: mm(dqt[s, own, :], normed[s * R : s * R + R, c]))
        tk = tmm(kk[:, own], normed[:, c])
        tv = tmm(vv[:, own], normed[:, c])
        for sh in range(2):
            h = slice(sh * hw, (sh + 1) * hw)
            dwa[sh, 0:hw, c] = t[h]
            dwa[sh, hw : 2 * hw, c] = tk[h]
            dwa[sh, 2 * hw : 3 * hw, c] = tv[h]
    onesr = jnp.ones((8, R), bf16)
    acc[8, :, 0 : 2 * hw] = over_samples(lambda s: mmt(onesr, dqt[s, own, :])) * 0.125
    acc[9, :, 0 : 2 * hw] = mm(ones, vv[:, own]) * 0.125

    def gnorm1(s):
        rs = al(s, R)
        for j in range(nt):
            c = slice(j * 256, j * 256 + 256)
            gn[rs, c] = tmm(dqt[s], wqkv[0:D, c]) + mm(kk[rs, :], wqkv[D : 2 * D, c]) + mm(vv[rs, :], wqkv[2 * D : 3 * D, c])

    loop(NS, gnorm1)

    def ln1b(i):
        r0 = pl.multiple_of(i * CH, CH)
        rs = pl.ds(r0, CH)
        x, keep = masked_input(tok, meta, r0, CH, R)
        xh, r = centred(x * keep)
        go = gn[rs, :]
        g = go * g1
        gx = g * xh
        gi = r * (g - jnp.sum(g, -1, keepdims=True) * (1.0 / D) - xh * (jnp.sum(gx, -1, keepdims=True) * (1.0 / D)))
        mid[rs, :] = (mid[rs, :] + gi) * keep
        acc[2] += fold8(go * xh)
        acc[3] += fold8(go)

    loop(dm.rows // CH, ln1b)
    tot = jnp.sum(acc[...], 1)
    for sh in range(2):
        dwa[sh, D : D + 6, :] = tot[0:6]
        dwa[sh, D + 6 : D + 7, :] = tot[6 + sh : 7 + sh]
        dwa[sh, D + 7 : D + 8, 0:hw] = tot[8:9, sh * hw : (sh + 1) * hw]
        dwa[sh, D + 7 : D + 8, hw : 2 * hw] = tot[9:10, sh * hw : (sh + 1) * hw]


V = pl.BlockSpec(memory_space=pltpu.VMEM)
ANY = pl.BlockSpec(memory_space=pl.ANY)
SM = pl.BlockSpec(memory_space=pltpu.SMEM)


def forward_call(dm, meta, tok, cot, wqkv, wo, wup, wdn, vec):
    M, D = dm.rows, dm.d
    sds = jax.ShapeDtypeStruct
    total = dm.ns * dm.pairs

    def kern(meta, tok, cot, wqkv, wo, wup, wdn, vec, p_hbm, normed, q8, kk, vv, mixt, n2, gp, mid, lout, dwd, act, pbuf, psem):
        y = lax.axis_index("tensor") // 2
        forward_body(dm, y, meta, tok, cot, wqkv, wo, wup, wdn, vec, p_hbm, normed, q8, kk, vv, mixt, n2, gp, mid, lout, dwd, act, pbuf, psem)

    row = sds((M, D), bf16)
    return pl.pallas_call(
        kern,
        out_shape=[sds((total, 2, dm.r, dm.r), bf16), row, row, row, row, sds((dm.ns, D, dm.r), bf16), row, sds((M, dm.ff), bf16), sds((M, D), f32), sds((M, D), f32), sds((2, dm.f, D), f32)],
        in_specs=[SM] + [V] * 7,
        out_specs=[ANY] + [V] * 10,
        scratch_shapes=[pltpu.VMEM((M, dm.ff), bf16), pltpu.VMEM((2, 2, dm.r, dm.r), bf16), pltpu.SemaphoreType.DMA((2,))],
        compiler_params=pltpu.CompilerParams(vmem_limit_bytes=VMEM_LIMIT),
        name="forward",
    )(meta, tok, cot, wqkv, wo, wup, wdn, vec)


def backward_call(dm, meta, tok, cot, wqkv, wo, wup, wdn, vec, saved):
    M, D = dm.rows, dm.d
    sds = jax.ShapeDtypeStruct
    p_hbm, normed, q8, kk, vv, mixt, n2, gp, mid = saved

    def kern(meta, tok, cot, wqkv, wo, wup, wdn, vec, normed, q8, mixt, n2, p_hbm, kk_h, vv_h, gp_h, mid_h, gtok, dwu, dwa, kk, vv, gp, gml, gmix, dqt, gn, acc, pbuf, psem, lsem):
        y = lax.axis_index("tensor") // 2
        cps = [pltpu.make_async_copy(a, b, lsem.at[i]) for i, (a, b) in enumerate(((gp_h, gp), (kk_h, kk), (vv_h, vv), (mid_h, gtok)))]
        for c in cps:
            c.start()
        for c in cps:
            c.wait()
        backward_body(dm, y, meta, tok, cot, wqkv, wo, wup, wdn, vec, p_hbm, normed, q8, kk, vv, mixt, n2, gp, gtok, gml, gmix, dqt, gn, dwu, dwa, acc, pbuf, psem)

    row = pltpu.VMEM((M, D), bf16)
    return pl.pallas_call(
        kern,
        out_shape=[sds((M, D), f32), sds((2, D, dm.f), f32), sds((2, D + 16, D), f32)],
        in_specs=[SM] + [V] * 11 + [ANY] * 5,
        out_specs=[V] * 3,
        scratch_shapes=[row, row, pltpu.VMEM((M, dm.ff), bf16), row, row, pltpu.VMEM((dm.ns, D, dm.r), bf16), pltpu.VMEM((M, D), f32), pltpu.VMEM((10, 8, D), f32), pltpu.VMEM((2, 2, dm.r, dm.r), bf16), pltpu.SemaphoreType.DMA((2,)), pltpu.SemaphoreType.DMA((4,))],
        compiler_params=pltpu.CompilerParams(vmem_limit_bytes=VMEM_LIMIT),
        name="backward",
    )(meta, tok, cot, wqkv, wo, wup, wdn, vec, normed, q8, mixt, n2, p_hbm, kk, vv, gp, mid)


def shards(tokens, metadata, cotangent, w_query, w_key, w_value, w_out, b_query, b_value, b_out, w_up, b_up, w_down, b_down, gain_one, shift_one, gain_two, shift_two, n_dp, n_t):
    dm = Dims(tokens, w_up, n_t)
    D, hw = dm.d, dm.hw
    core = lax.rem(lax.axis_index("tensor"), 2)
    y = lax.axis_index("tensor") // 2
    mine = core * dm.ns

    def take(a):
        a = lax.dynamic_slice_in_dim(a, mine, dm.ns, 0)
        return jnp.pad(a, ((0, 0), (0, dm.r - dm.length), (0, 0))).reshape(dm.rows, D)

    tok, cot = take(tokens), take(cotangent)
    meta = lax.dynamic_slice_in_dim(metadata, mine, dm.ns, 0)
    bias = jnp.zeros((16, D), f32).at[0, : dm.f].set(b_up).at[1, :hw].set(b_query).at[1, hw : 2 * hw].set(b_value)
    own = jnp.concatenate([w_query.T.astype(f32), w_key.T.astype(f32), w_value.T.astype(f32), w_out.astype(f32), w_up.astype(f32), w_down.astype(f32), bias])
    g = lax.all_gather(own, "tensor")
    wq, wk, wv, wo = (g[:, i * hw : (i + 1) * hw].reshape(D, D).astype(bf16) for i in range(4))
    wqkv = jnp.concatenate([wq, wk, wv])
    wup = g[:, D : 2 * D].astype(bf16)
    wdn = g[:, 2 * D : 3 * D].reshape(dm.ff, D).astype(bf16)
    gb = g[:, 3 * D :]
    vec = jnp.concatenate([jnp.stack([gain_one, shift_one, gain_two, shift_two, b_out, b_down, gb[:, 1, :hw].reshape(D), gb[:, 1, hw : 2 * hw].reshape(D)]), gb[:, 0]])
    *saved, lout, dwd = forward_call(dm, meta, tok, cot, wqkv, wo, wup, wdn, vec)
    gtok, dwu, dwa = backward_call(dm, meta, tok, cot, wqkv, wo, wup, wdn, vec, saved)

    nt2 = n_t // 2
    sib = [[2 * i, 2 * i + 1] for i in range(nt2)]
    out2 = lax.all_gather(jnp.stack([lout, gtok]), "tensor", axis_index_groups=sib)
    lo, gt = (out2[:, i].reshape(dm.samples, dm.r, D)[:, : dm.length] for i in range(2))
    dw = jnp.concatenate([dwd, dwu, dwa], 1)
    dw = lax.psum_scatter(dw, "tensor", axis_index_groups=sib, scatter_dimension=0)
    dw = lax.psum(dw[...], "dp")
    dw = dw.reshape(3 * D + 16, D)
    d_, u_, a_ = dw[:D], dw[D : 2 * D], dw[2 * D :]
    sm = a_[D:]
    return (
        lo.astype(bf16),
        gt,
        a_[0:hw].T,
        a_[hw : 2 * hw].T,
        a_[2 * hw : 3 * hw].T,
        a_[3 * hw : 4 * hw],
        sm[7, :hw],
        sm[7, hw : 2 * hw],
        sm[1],
        u_,
        sm[6],
        d_,
        sm[0],
        sm[2],
        sm[3],
        sm[4],
        sm[5],
    )


def solution(mesh):
    n_dp, n_t = mesh.shape["dp"], mesh.shape["tensor"]
    rows, cols, vec, rep = P("dp", None, None), P(None, "tensor"), P("tensor"), P()
    srow = P("tensor", None)

    def run(*args):
        return shards(*args, n_dp=n_dp, n_t=n_t)

    return jax.shard_map(
        run,
        mesh=mesh,
        in_specs=(rows, P("dp"), rows, cols, cols, cols, srow, vec, vec, rep, cols, vec, srow, rep, rep, rep, rep, rep),
        out_specs=(rows, rows, cols, cols, cols, srow, vec, vec, rep, cols, vec, srow, rep, rep, rep, rep, rep),
        check_vma=False,
    )
```

time: 906 us -> 732 us (0.81)
  Pallas kernels: 0 us -> 178 us
  waiting for transfers between devices: 569 us -> 437 us
  matrix products: 94.5 us -> 0 us
  other arithmetic: 86.9 us -> 40 us
  blocking collectives: 39.8 us -> 0 us
  local copies, waits for them, and re-layouts: 91.9 us -> 61.7 us
    psum x4 -> x1, waiting for transfers between devices: 569 us -> 227 us  [shards(): dw = lax.psum(dw[...], 'dp')]
    all_gather x0 -> x2, waiting for transfers between devices: none -> 194 us  [the longest x1 165 us: shards(): g = lax.all_gather(own, 'tensor')]
    pallas_call x0 -> x2, Pallas kernels: none -> 178 us  [the longest x1 89.1 us: backward_call(): pl.pallas_call(kern, out_shape=[sds((M, D), f32), sds((2, D, dm.f), f32),...]
    dot_general x24 -> x0, matrix products: 94.5 us -> none  [the longest x6 30.3 us: contract_cols(): lax.dot_general(left_mat, right_mat, (((1,), (1,)), ((), ())), preferred_...]
    reduce_sum x11 -> x0, other arithmetic: 46 us -> none  [the longest x2 14.6 us: layer_norm(): mean_removed = source_tokens - average]
    psum x1 -> x0, blocking collectives: 39.8 us -> none  [shards(): summed = lax.psum(mlp_group + attn_group, 'dp')]
    convert_element_type x12 -> x0, local copies, waits for them, and re-layouts: 33.4 us -> none  [the longest x2 10.4 us: shards(): tokens.reshape(row_count, model_width).astype(jnp.float32) * keep_mask]
    convert_element_type x7 -> x0, other arithmetic: 32.5 us -> none  [the longest x1 10.9 us: shards(): grad_scores = grad_scores.astype(jnp.bfloat16)]
  transfers between devices with their start and end apart: 4 -> 4, of which waited for: 4 -> 4; matrix products, arithmetic and copies ran while one was open for 11% -> 4% of each run, Pallas kernels for 0% -> 0%
where the time goes in v1:
time: 732 us; the launch traced here: 731 us
  waiting for transfers between devices  437 us (60%)
  Pallas kernels  178 us (24%)
  local copies, waits for them, and re-layouts  61.7 us (8%)
  other arithmetic  40 us (5%)
  between operations  14 us (2%)
    psum x1, waiting for transfers between devices, shards(): dw = lax.psum(dw[...], 'dp')  227 us
    all_gather x1, waiting for transfers between devices, shards(): g = lax.all_gather(own, 'tensor')  165 us
    pallas_call x1, Pallas kernels, backward_call(): pl.pallas_call(kern, out_shape=[sds((M, D), f32), sds((2, D, dm.f), f32),...  89.1 us
    pallas_call x1, Pallas kernels, forward_call(): pl.pallas_call(kern, out_shape=[sds((total, 2, dm.r, dm.r), bf16), row, r...  88.7 us
    all_gather x1, waiting for transfers between devices, shards(): lax.all_gather(jnp.stack([lout, gtok]), 'tensor', axis_index_groups=sib)  28.6 us
    reduce_scatter x1, waiting for transfers between devices, shards(): lax.psum_scatter(dw, 'tensor', axis_index_groups=sib, scatter_dimension=0)  15.8 us
    unnamed x35, local copies, waits for them, and re-layouts  15.2 us
  transfers between devices with their start and end apart: 4, of which 4 were waited for; matrix products, arithmetic and copies ran while one was open for 4% of the time, Pallas kernels for 0%

profile of v1, /device:TPU:0, one launch (start us, length us, event | category | flops | bytes accessed | tf_op | source)
XLA Modules:
  0.0 730.5 jit_solution(112409107268396334)
XLA Ops:
  8.0 1.8 bitcast_dynamic-update-slice_fusion.2
  9.9 1.8 bitcast_dynamic-update-slice_fusion.1
  11.7 1.9 bitcast_dynamic-update-slice_fusion
  13.6 1.8 convert_dynamic-update-slice_fusion.2
  15.4 2.8 convert_dynamic-update-slice_fusion.1
  18.3 1.6 convert_dynamic-update-slice_fusion
  25.3 3.5 constant_dynamic-slice_fusion
  31.8 165.5 %all-gather.5.cloned.1.call-done = f32[9280,768]{1,0:T(8,128)} async-done(((f32[2320,768]{1,0:T(8,128)}), f32[9280,768]{1,0:T(8,128)}) %all-gather.5.cloned.1.call-update) | async-done | bytes 28508176 | tf_op jit(solution)/shard_map/all_gather | solution.py:441
  197.3 1.5 slice_reduce_fusion
  199.7 10.2 %convert.16 = bf16[4,2320,768]{2,1,0:T(8,128)(2,1)S(1)} convert(f32[4,2320,768]{2,1,0:T(8,128)} %bitcast.37) | non-fusion elementwise | flops 7127040 | bytes 42762240 | tf_op jit(solution)/shard_map/convert.11
  209.9 5.1 copy-done
  215.0 1.5 fusion.1
  216.5 8.0 %fusion = (bf16[4,768,768]{2,1,0:T(8,128)(2,1)}, bf16[4,768,768]{2,1,0:T(8,128)(2,1)}) fusion(bf16[4,2320,768]{2,1,0:T(8,128)(2,1)} %copy-done), kind=kLoop, calls=%fused_computation.26 | loop fusion | bytes 18874368 | tf_op jit(solution)/shard_map/slice | solution.py:445
  224.5 1.3 stack_reshape_squeeze.7
  227.1 2.0 pad_maximum_fusion.2.wqkv
  229.1 2.0 concatenate.20.vec
  231.1 88.7 %forward.1 = (bf16[24,2,272,272]{3,2,1,0:T(8,128)(2,1)}, bf16[1088,768]{1,0:T(8,128)(2,1)}, bf16[1088,768]{1,0:T(8,128)(2,1)}, bf16[1088,768]{1,0:T(8,128)(2,1)}...) custom-call(s32[4]{0:T(128)} %dynamic_slice.9.meta, ...), custom_call_target="tpu_custom_call" | custom-call | tf_op jit(solution)/shard_map/forward/pallas_call | solution.py:389
  319.9 89.1 %backward.1 = (f32[1088,768]{1,0:T(8,128)}, f32[2,768,768]{2,1,0:T(8,128)}, f32[2,784,768]{2,1,0:T(8,128)}) custom-call(s32[4]{0:T(128)} %dynamic_slice.9.meta, bf16[1088,768]{1,0:T(8,128)(2,1)} %bitcast.42, bf16[1088,768]{1,0:T(8,128)(2,1)} %bitcast.40, bf16[2304,768]{1,0:T(8,128)(2,1)} %pad_maximum_fusion.2.wqkv, bf16[768,768]{1,0:T(8,128)(2,1)} %bitcast.45, ...), custom_call_target="tpu_custom_call" | custom-call | tf_op jit(solution)/shard_map/backward/pallas_call | solution.py:415
  409.0 10.2 %pad_maximum_fusion = f32[2,2320,768]{2,1,0:T(8,128)} fusion(f32[2,784,768]{2,1,0:T(8,128)} %get-tuple-element.80, f32[2,768,768]{2,1,0:T(8,128)} %get-tuple-element.79, f32[2,768,768]{2,1,0:T(8,128)} %get-tuple-element.78), kind=kLoop, calls=%fused_computation | loop fusion | flops 7127040 | bytes 28508160 | tf_op jit(solution)/shard_map/concatenate | solution.py:455
  419.3 1.9 copy-done.1
  421.2 5.8 pad_maximum_fusion.1
  427.1 15.8 %reduce-scatter.2.cloned.1.call-done = f32[1,2320,768]{2,1,0:T(8,128)} async-done(((f32[2,2320,768]{2,1,0:T(8,128)}), f32[1,2320,768]{2,1,0:T(8,128)}) %reduce-scatter.2.cloned.1.call-update) | async-done | bytes 7127056 | tf_op jit(solution)/shard_map/reduce_scatter | solution.py:456
  442.9 28.6 %all-gather.7.cloned.1.call-done = f32[4,1088,768]{2,1,0:T(8,128)} async-done(((f32[2,1088,768]{2,1,0:T(8,128)}), f32[4,1088,768]{2,1,0:T(8,128)}) %all-gather.7.cloned.1.call-update) | async-done | bytes 13369360 | tf_op jit(solution)/shard_map/all_gather | solution.py:453
  471.5 3.2 slice.233
  474.7 3.3 slice.203
  478.6 4.9 copy.55
  483.7 2.3 copy.54
  486.0 226.9 %all-reduce.5.cloned.1.call-done = f32[2320,768]{1,0:T(8,128)} async-done(((f32[2320,768]{1,0:T(8,128)}), f32[2320,768]{1,0:T(8,128)}) %all-reduce.5.cloned.1.call-update) | async-done | bytes 7127056 | tf_op jit(solution)/shard_map/psum | solution.py:457
  712.9 1.4 fusion.3
  714.3 1.8 slice_reduce_fusion.2
  716.1 3.0 fusion.4
  719.2 4.9 fusion.2
  (57 shorter events, 12.3 us)
Async XLA Ops:
  7.2 11.0 %copy-start.2 = (bf16[768,768]{1,0:T(8,128)(2,1)S(1)}, bf16[768,768]{1,0:T(8,128)(2,1)}, u32[]{:S(2)}) copy-start(bf16[768,768]{1,0:T(8,128)(2,1)} %param.36) | copy-start | bytes 3538948
  7.2 190.1 %all-gather.5.cloned.1.call-start = ((), (), s32[]{:S(2)}) async-start(), calls=%async_computation.3 | async-start | bytes 35635200 | tf_op jit(solution)/shard_map/all_gather | solution.py:441
  9.8 10.0 %copy-start.12 = (f32[192]{0:T(256)S(1)}, f32[192]{0:T(256)}, u32[]{:S(2)}) copy-start(f32[192]{0:T(256)} %param.31) | copy-start | bytes 2308
  9.8 10.2 %copy-start.13 = (f32[192]{0:T(256)S(1)}, f32[192]{0:T(256)}, u32[]{:S(2)}) copy-start(f32[192]{0:T(256)} %param.32) | copy-start | bytes 2308
  18.2 3.0 copy-start.6
  18.2 3.6 copy-start.7
  18.2 4.1 copy-start.8
  18.2 4.7 copy-start.9
  18.2 5.3 copy-start.10
  18.2 5.9 copy-start.11
  18.3 6.4 copy-start.14
  19.8 5.4 copy-start.3
  21.1 421.8 %reduce-scatter.2.cloned.1.call-start = ((), (), s32[]{:S(2)}) async-start(), calls=%async_computation.1 | async-start | bytes 21381120 | tf_op jit(solution)/shard_map/reduce_scatter | solution.py:456
  209.9 5.1 copy-start
  226.5 2.6 copy-start.5
  227.1 2.0 copy-start.4
  419.3 1.9 copy-start.1
  419.3 52.2 %all-gather.7.cloned.1.call-start = ((), (), s32[]{:S(2)}) async-start(), calls=%async_computation.4 | async-start | bytes 20054016 | tf_op jit(solution)/shard_map/all_gather | solution.py:453
  427.0 285.9 %all-reduce.5.cloned.1.call-start = ((), (), s32[]{:S(2)}) async-start(), calls=%async_computation.2 | async-start | bytes 14254080 | tf_op jit(solution)/shard_map/psum | solution.py:457
Sparse Core Ops, SparseCore 0:
  21.2 175.9 all-gather.4
  419.4 23.4 reduce-scatter.1
  444.5 26.8 all-gather.6
  475.7 237.2 all-reduce.4

commit v2 on v1

v2 whole, which is shorter than its diff:
```python
import math

import jax
import jax.numpy as jnp
from jax import lax
from jax.experimental import pallas as pl
from jax.experimental.pallas import tpu as pltpu
from jax.sharding import PartitionSpec as P

HEAD_DIM = 64
EPS = 1e-05
MESH = pl.DeviceIdType.MESH
f32 = jnp.float32
bf16 = jnp.bfloat16
VMEM_LIMIT = 61 << 20
RING = 8
CH = 64
TAIL_P = 0.24
TAIL = (
    0.08952743306829739,
    0.15551359433427508,
    -0.15404885518029288,
    0.6255903019940591,
    -0.6460706945688248,
    0.5545739487327468,
    -0.12508572868970558,
)
INV_SQRT_2PI = 1.0 / math.sqrt(2.0 * math.pi)
HALF_LOG2E = -0.5 / math.log(2.0)


def mm(a, b):
    return lax.dot_general(a, b, (((1,), (0,)), ((), ())), preferred_element_type=f32)


def mmt(a, b):
    return lax.dot_general(a, b, (((1,), (1,)), ((), ())), preferred_element_type=f32)


def tmm(a, b):
    return lax.dot_general(a, b, (((0,), (0,)), ((), ())), preferred_element_type=f32)


def loop(n, fn):
    def body(i, carry):
        fn(i)
        return carry

    lax.fori_loop(0, n, body, 0)


def al(i, step):
    return pl.ds(pl.multiple_of(i * step, step), step)


def centred(x):
    d = x.shape[-1]
    mu = jnp.sum(x, -1, keepdims=True) * (1.0 / d)
    xm = x - mu
    var = jnp.sum(xm * xm, -1, keepdims=True) * (1.0 / d)
    r = lax.rsqrt(var + EPS)
    return xm * r, r


def gelu_pair(v):
    d = 1.0 + TAIL_P * jnp.abs(v)
    t = pltpu.reciprocal(d, approx=True)
    t = t * (2.0 - d * t)
    e = jnp.exp2(HALF_LOG2E * (v * v))
    acc = TAIL[6] * t + TAIL[5]
    for k in range(4, -1, -1):
        acc = acc * t + TAIL[k]
    q = (acc * t) * e
    cdf = jnp.where(v < 0, q, 1.0 - q)
    return v * cdf, cdf + (v * e) * INV_SQRT_2PI


def fold8(x):
    return jnp.sum(x.reshape(x.shape[0] // 8, 8, x.shape[1]), 0)


class Dims:
    def __init__(self, tokens, w_up, n_t):
        self.samples, self.length, self.d = tokens.shape
        self.ns = self.samples // 2
        self.r = -(-self.length // 16) * 16
        self.rows = self.ns * self.r
        self.f = w_up.shape[1]
        self.ff = self.f * n_t
        self.n_t = n_t
        self.heads = self.d // HEAD_DIM
        self.pairs = self.heads // 2
        self.hw = self.d // n_t


class Links:
    def __init__(self, n_dp):
        self.n_dp = n_dp
        self.dp = lax.axis_index("dp")
        self.t = lax.axis_index("tensor")
        self.y, self.c = self.t // 2, lax.rem(self.t, 2)
        self.z, self.x = self.dp // 2, lax.rem(self.dp, 2)
        self.length = n_dp // 2
        self.sib = (self.dp, 2 * self.y + 1 - self.c)
        self.ypart = (self.dp, 2 * (1 - self.y) + self.c)
        self.t_sib = 2 * self.y + 1 - self.c
        self.t_y = 2 * (1 - self.y) + self.c
        self.t_ysib = 2 * (1 - self.y) + 1 - self.c
        g = lax.rem(self.dp, RING)
        half = RING // 2
        zz, xx = g // 2, lax.rem(g, 2)
        self.pos = jnp.where(xx == 0, zz, RING - 1 - zz)
        base = self.dp - g

        def at(pos):
            pos = lax.rem(pos + RING, RING)
            local = jnp.where(pos < half, 2 * pos, 2 * (RING - 1 - pos) + 1)
            return (base + local, self.t)

        self.step = 1 - 2 * self.c
        self.ahead, self.behind = at(self.pos + self.step), at(self.pos - self.step)

    def piece(self, offset):
        return lax.rem(self.pos + offset * self.step + RING, RING)


def rcopy(src, dst, ssem, rsem, dev):
    return pltpu.make_async_remote_copy(src_ref=src, dst_ref=dst, send_sem=ssem, recv_sem=rsem, device_id=dev, device_id_type=MESH)


def enter(devs):
    bar = pltpu.get_barrier_semaphore()
    for d in devs:
        pl.semaphore_signal(bar, inc=1, device_id=d, device_id_type=MESH)
    pl.semaphore_wait(bar, len(devs))


class Gather:
    def __init__(self, ln, src, out, direct, ssem, rsem):
        self.ln, self.src, self.out, self.direct = ln, src, out, direct
        self.ssem, self.rsem = ssem, rsem
        self.rows = src.shape[0]
        self.piece_rows = (self.rows - direct) // RING

    def at(self, ref, offset):
        return ref.at[pl.ds(pl.multiple_of(self.direct + self.ln.piece(offset) * self.piece_rows, 8), self.piece_rows)]

    def copy(self, src, dst, k, dev):
        return rcopy(src, dst, self.ssem.at[k], self.rsem.at[k], dev)

    def landed(self, view, k):
        rcopy(view, view, self.ssem.at[k], self.rsem.at[k], self.ln.sib).wait_recv()

    def spread_y(self):
        return self.copy(self.at(self.src, 0), self.at(self.out.at[self.ln.t], 0), 0, self.ln.ypart)

    def direct_y(self):
        d = pl.ds(0, self.direct)
        return self.copy(self.src.at[d], self.out.at[self.ln.t].at[d], 1, self.ln.ypart)

    def whole_sib(self):
        return self.copy(self.src, self.out.at[self.ln.t], 2, self.ln.sib)

    def start_y(self):
        self.spread_y().start()
        self.direct_y().start()

    def start_sib(self):
        self.whole_sib().start()

    def wait_sib(self):
        self.landed(self.out.at[self.ln.t_sib], 2)

    def to_sib(self, offset):
        v = self.at(self.out.at[self.ln.t_y], offset)
        return self.copy(v, v, 11 + 4 + offset, self.ln.sib)

    def direct_sib(self):
        v = self.out.at[self.ln.t_y].at[pl.ds(0, self.direct)]
        return self.copy(v, v, 10, self.ln.sib)

    def ring_ahead(self, s):
        v = self.at(self.out.at[self.ln.t_y], -s)
        return self.copy(v, v, 3 + s, self.ln.ahead)

    def ring_behind(self, s):
        v = self.at(self.out.at[self.ln.t_y], s)
        return self.copy(v, v, 7 + s, self.ln.behind)

    def tick(self, i):
        ln, out = self.ln, self.out.at[self.ln.t_y]
        if i == 0:
            self.landed(self.at(out, 0), 0)
            self.ring_ahead(0).start()
            self.ring_behind(0).start()
            self.to_sib(0).start()
            return
        s = i - 1
        self.landed(self.at(out, -s - 1), 3 + s)
        if s < 3:
            self.ring_ahead(s + 1).start()
            self.landed(self.at(out, s + 1), 7 + s)
            if s < 2:
                self.ring_behind(s + 1).start()
        self.to_sib(-s - 1).start()
        if s < 3:
            self.to_sib(s + 1).start()
        if i == 4:
            self.landed(out.at[pl.ds(0, self.direct)], 1)
            self.direct_sib().start()

    def finish(self):
        ln, out = self.ln, self.out.at[self.ln.t_ysib]
        for offset in range(-4, 4):
            v = out.at[pl.ds(pl.multiple_of(self.direct + lax.rem(ln.pos - offset * ln.step + RING, RING) * self.piece_rows, 8), self.piece_rows)]
            self.landed(v, 11 + 4 + offset)
        self.landed(out.at[pl.ds(0, self.direct)], 10)

    def drain(self):
        cps = [self.spread_y(), self.direct_y(), self.whole_sib(), self.direct_sib()]
        cps += [self.ring_ahead(s) for s in range(4)] + [self.ring_behind(s) for s in range(3)]
        cps += [self.to_sib(o) for o in range(-4, 4)]
        for cp in cps:
            cp.wait_send()


GATHER_SEMS = 19


def keep_of(meta, base, s, r0, n):
    rows = lax.broadcasted_iota(jnp.int32, (n, 1), 0) + r0
    return jnp.where(rows == 1, meta[base + s].astype(f32), 1.0)


def row_chunks(dm):
    out, r = [], 0
    while r < dm.r:
        n = min(CH, dm.r - r)
        out.append((r, n))
        r += n
    return out


def forward_kernel(dm, n_dp, *refs):
    (meta, wq, wk, wv, wo_s, wup_s, wdn_s, bias, g1_r, s1_r, g2_r, s2_r, bo_r, tokens, cotan) = refs[:15]
    (ga, gu, n32, p_hbm, o_wqkv, o_wo, o_bias, o_tok, o_cot, o_normed, o_q8, o_kk, o_vv, o_mixt, o_n2, o_act, o_gp, o_mid, d_own, d_sib) = refs[15:35]
    (tok3, cot3, tok, cot, wqkv, wo, wup, normed, q8, kk, vv, mixt, n2, act, gp, mid, dwd, pbuf, tmp, bbuf, bqv) = refs[35:56]
    psem, tsem, lsem, osem, ssa, rsa, ssu, rsu, ssd, rsd = refs[56:]
    R, D, NS, hw, f = dm.r, dm.d, dm.ns, dm.hw, dm.f
    ln = Links(n_dp)
    y, c, t = ln.y, ln.c, ln.t
    base = c * NS

    def row(ref):
        return ref[...].reshape(1, D)

    loads = []
    for s in range(NS):
        loads.append(pltpu.make_async_copy(tokens.at[base + s], tok3.at[s], lsem.at[s]))
    for s in range(NS):
        loads.append(pltpu.make_async_copy(cotan.at[base + s], cot3.at[s], lsem.at[NS + s]))
    for cp in loads:
        cp.start()
    outs = []

    def put(src, dst):
        cp = pltpu.make_async_copy(src, dst, osem.at[len(outs)])
        cp.start()
        outs.append(cp)

    mid[0:16, :] = bias[...]
    bbuf[t] = bias[...]
    for i, w in enumerate((wq, wk, wv)):
        wt = w[...].astype(f32).T
        mid[16 + i * hw : 16 + (i + 1) * hw, :] = wt
        wqkv[pl.ds(pl.multiple_of(i * D + t * hw, 16), hw), :] = wt.astype(bf16)
    mid[16 + 3 * hw : 16 + 4 * hw, :] = wo_s[...].astype(f32)
    wo[al(t, hw), :] = wo_s[...]
    enter((ln.ypart, ln.sib, ln.ahead, ln.behind))
    g_a = Gather(ln, mid.at[pl.ds(0, D + 16)], ga, 16 + D // 3, ssa, rsa)
    g_u = Gather(ln, dwd.at[0], gu, D // 3, ssu, rsu)
    g_a.start_y()
    g_a.start_sib()

    def widen(i):
        rs = al(i, 64)
        dwd[0, rs, :] = wup_s[rs, :].astype(f32)
        dwd[1, rs, :] = wdn_s[rs, :].astype(f32)
        wup[c, rs, :] = wup_s[rs, :]

    loop(f // 64, widen)
    put(dwd.at[1], n32)
    g_u.start_sib()

    for cp in loads:
        cp.wait()
    g1, s1, g2, s2, bo = (row(r) for r in (g1_r, s1_r, g2_r, s2_r, bo_r))
    full = dm.length // 16 * 16

    def pad_rows(s):
        for src, dst in ((tok3, tok), (cot3, cot)):
            for r in range(0, full, 64):
                n = min(64, full - r)
                dst[pl.ds(pl.multiple_of(s * R + r, 16), n), :] = src[s, r : r + n, :]
            last = pl.ds(pl.multiple_of(s * R + full, 16), R - full)
            dst[last, :] = jnp.zeros((R - full, D), bf16)
            if dm.length > full:
                dst[pl.ds(pl.multiple_of(s * R + full, 16), dm.length - full), :] = src[s, full : dm.length, :]

    loop(NS, pad_rows)
    put(tok, o_tok)
    put(cot, o_cot)

    def ln1(s):
        for r, n in row_chunks(dm):
            rs = pl.ds(pl.multiple_of(s * R + r, 16), n)
            x = tok[rs, :].astype(f32)
            if r == 0:
                x = x * keep_of(meta, base, s, r, n)
            xh, _ = centred(x)
            normed[rs, :] = (xh * g1 + s1).astype(bf16)

    loop(NS, ln1)
    put(normed, o_normed)

    def fetch(src, k):
        cp = pltpu.make_async_copy(src, tmp.at[k], tsem.at[k])
        cp.start()
        return cp

    def take_a(tp):
        dsts = [(wqkv, i * D + tp * hw) for i in range(3)] + [(wo, tp * hw)]
        cb = pltpu.make_async_copy(ga.at[tp, pl.ds(0, 16)], bbuf.at[tp], tsem.at[2])
        cb.start()
        cps = [fetch(ga.at[tp, pl.ds(16, hw)], 0)]
        for i, (ref, r0) in enumerate(dsts):
            if i < 3:
                cps.append(fetch(ga.at[tp, pl.ds(16 + (i + 1) * hw, hw)], (i + 1) % 2))
            cps[i].wait()
            ref[pl.ds(pl.multiple_of(r0, 16), hw), :] = tmp[i % 2].astype(bf16)
        cb.wait()

    lane = lax.broadcasted_iota(jnp.int32, (1, 128), 1)
    masks = (lane < HEAD_DIM, lane >= HEAD_DIM)
    hp = dm.pairs // 2
    tail = R - 16
    live = lax.broadcasted_iota(jnp.int32, (16, 1), 0) < dm.length - tail

    def project(hf):
        for i in range(2):
            b = bbuf[2 * hf + i]
            bqv[0:1, i * hw : (i + 1) * hw] = b[1:2, 0:hw]
            bqv[1:2, i * hw : (i + 1) * hw] = b[1:2, hw : 2 * hw]
        cs = al(hf, 2 * hw)

        def one(s):
            rs = al(s, R)
            n = normed[rs, :]
            w = [wqkv[pl.ds(pl.multiple_of(i * D + hf * 2 * hw, 128), 2 * hw), :] for i in range(3)]
            q8[rs, cs] = (mmt(n, w[0]) + bqv[0:1, : 2 * hw]).astype(bf16) * jnp.bfloat16(0.125)
            kk[rs, cs] = mmt(n, w[1]).astype(bf16)
            vv[rs, cs] = (mmt(n, w[2]) + bqv[1:2, : 2 * hw]).astype(bf16)

        loop(NS, one)

    def p_copy(hf, i):
        slot = lax.rem(i, 2)
        return pltpu.make_async_copy(pbuf.at[slot], p_hbm.at[(i // hp) * dm.pairs + hf * hp + lax.rem(i, hp)], psem.at[slot])

    def attend(hf, ticks):
        total = NS * hp

        def one(i):
            s, p = i // hp, hf * hp + lax.rem(i, hp)
            slot = lax.rem(i, 2)
            rs, cs = al(s, R), al(p, 128)
            for k, fn in ticks:
                pl.when(i == k)(fn)

            @pl.when(i >= 2)
            def _():
                p_copy(hf, i - 2).wait()

            q, k, v = q8[rs, cs], kk[rs, cs], vv[rs, cs]
            for h in range(2):
                st = mmt(jnp.where(masks[h], k, jnp.bfloat16(0)), q)
                sa = st[:tail]
                sb = jnp.where(live, st[tail:], -1e30)
                m = jnp.maximum(jnp.max(sa, 0, keepdims=True), jnp.max(sb, 0, keepdims=True))
                ea, eb = jnp.exp(sa - m), jnp.exp(sb - m)
                inv = 1.0 / (jnp.sum(ea, 0, keepdims=True) + jnp.sum(eb, 0, keepdims=True))
                pbuf[slot, h, :tail, :] = (ea * inv).astype(bf16)
                pbuf[slot, h, tail:, :] = (eb * inv).astype(bf16)
                o = tmm(v, pbuf[slot, h])
                hr = pl.ds(pl.multiple_of(p * 128 + h * HEAD_DIM, HEAD_DIM), HEAD_DIM)
                mixt[s, hr, :] = o[h * HEAD_DIM : (h + 1) * HEAD_DIM].astype(bf16)
            p_copy(hf, i).start()

        loop(total, one)
        p_copy(hf, total - 2).wait()
        p_copy(hf, total - 1).wait()

    g_a.wait_sib()
    take_a(ln.t_sib)
    project(y)
    g_a.tick(0)
    attend(y, [(2, lambda: g_a.tick(1)), (10, lambda: g_a.tick(2))])
    g_a.tick(3)
    g_a.tick(4)
    g_u.start_y()
    g_a.finish()
    take_a(ln.t_y)
    take_a(ln.t_ysib)
    put(wqkv, o_wqkv)
    put(wo, o_wo)
    put(bbuf, o_bias)
    project(1 - y)
    put(q8, o_q8)
    put(kk, o_kk)
    put(vv, o_vv)
    g_u.tick(0)
    attend(1 - y, [(2, lambda: g_u.tick(1)), (10, lambda: g_u.tick(2))])
    put(mixt, o_mixt)
    g_a.drain()

    def outp(s):
        rs = al(s, R)
        mid[rs, :] = tmm(mixt[s], wo[...])

    loop(NS, outp)

    def ln2(s):
        for r, n in row_chunks(dm):
            rs = pl.ds(pl.multiple_of(s * R + r, 16), n)
            x = tok[rs, :].astype(f32)
            if r == 0:
                x = x * keep_of(meta, base, s, r, n)
            m = x + (mid[rs, :] + bo)
            mid[rs, :] = m
            xh, _ = centred(m)
            n2[rs, :] = (xh * g2 + s2).astype(bf16)

    loop(NS, ln2)
    put(mid, o_mid)
    put(n2, o_n2)
    g_u.tick(3)
    g_u.wait_sib()
    cps = [fetch(gu.at[ln.t_sib, pl.ds(0, hw)], 0)]
    for i in range(4):
        if i < 3:
            cps.append(fetch(gu.at[ln.t_sib, pl.ds((i + 1) * hw, hw)], (i + 1) % 2))
        cps[i].wait()
        wup[1 - c, i * hw : (i + 1) * hw, :] = tmp[i % 2].astype(bf16)
    ft = f // 256

    def mlp(i):
        s, j = i // (2 * ft), lax.rem(i, 2 * ft)
        rs, sh, cs = al(s, R), j // ft, al(lax.rem(j, ft), 256)
        h = mm(n2[rs, :], wup[sh, :, cs]) + bbuf[2 * y + sh, 0:1, cs]
        a, g = gelu_pair(h)
        act[rs, al(j, 256)] = a.astype(bf16)
        gp[rs, al(j, 256)] = g.astype(bf16)

    loop(NS * 2 * ft, mlp)
    put(act, o_act)
    put(gp, o_gp)
    g_u.tick(4)
    g_u.finish()
    g_u.drain()
    outs[0].wait()

    def dwdn(i):
        sh, j = i // ft, lax.rem(i, ft)
        dwd[sh, al(j, 256), :] = tmm(act[:, al(i, 256)], cot[...])

    loop(2 * ft, dwdn)
    put(dwd.at[c], d_own)
    cp = rcopy(dwd.at[1 - c], d_sib, ssd.at[0], rsd.at[0], ln.sib)
    cp.start()
    cp.wait()
    for cp in outs[1:]:
        cp.wait()


V = pl.BlockSpec(memory_space=pltpu.VMEM)
ANY = pl.BlockSpec(memory_space=pl.ANY)
SM = pl.BlockSpec(memory_space=pltpu.SMEM)


def forward_call(dm, n_dp, small, big):
    M, D, f = dm.rows, dm.d, dm.f
    sds, vm, dma = jax.ShapeDtypeStruct, pltpu.VMEM, pltpu.SemaphoreType.DMA
    row = sds((M, D), bf16)
    wide = sds((M, 2 * f), bf16)
    sq = sds((D, f), f32)
    outs = [sds((dm.n_t, D + 16, D), f32), sds((dm.n_t, D, f), f32), sds((f, D), f32), sds((dm.ns * dm.pairs, 2, dm.r, dm.r), bf16), sds((3 * D, D), bf16), sds((D, D), bf16), sds((dm.n_t, 16, D), f32)]
    outs += [row] * 6 + [sds((dm.ns, D, dm.r), bf16), row, wide, wide, sds((M, D), f32), sds((f, D), f32), sds((f, D), f32)]
    scratch = [vm((dm.ns, dm.length, D), bf16)] * 2 + [vm((M, D), bf16)] * 2 + [vm((3 * D, D), bf16), vm((D, D), bf16), vm((2, D, f), bf16)]
    scratch += [vm((M, D), bf16)] * 4 + [vm((dm.ns, D, dm.r), bf16), vm((M, D), bf16), vm((M, 2 * f), bf16), vm((M, 2 * f), bf16), vm((M, D), f32), vm((2, f, D), f32)]
    scratch += [vm((2, 2, dm.r, dm.r), bf16), vm((2, dm.hw, D), f32), vm((dm.n_t, 16, D), f32), vm((8, D), f32)]
    scratch += [dma((2,)), dma((3,)), dma((2 * dm.ns,)), dma((20,)), dma((GATHER_SEMS,)), dma((GATHER_SEMS,)), dma((GATHER_SEMS,)), dma((GATHER_SEMS,)), dma((1,)), dma((1,))]

    def kern(*refs):
        forward_kernel(dm, n_dp, *refs)

    return pl.pallas_call(
        kern,
        out_shape=outs,
        in_specs=[SM] + [V] * (len(small) - 1) + [ANY] * len(big),
        out_specs=[ANY] * len(outs),
        scratch_shapes=scratch,
        compiler_params=pltpu.CompilerParams(vmem_limit_bytes=VMEM_LIMIT, collective_id=1, has_side_effects=True),
        name="forward",
    )(*small, *big)


class Reduce:
    KINDS = 9

    def __init__(self, ln, own, sib, rz, rx, fin, vin, vout, lsem, ssem, rsem, n_sub, n_arrays):
        self.ln, self.own, self.sibling, self.rz, self.rx, self.fin = ln, own, sib, rz, rx, fin
        self.vin, self.vout, self.lsem, self.ssem, self.rsem = vin, vout, lsem, ssem, rsem
        self.n_sub, self.total = n_sub, n_sub * n_arrays
        self.block = own.shape[1] // 4
        self.pr = self.block // n_sub
        L, z = ln.length, ln.z
        self.L = L
        self.far = (L - 1 - z, z)
        self.waves = self.total + 2 * L

    def view(self, ref, q, b):
        return ref.at[q // self.n_sub, pl.ds(pl.multiple_of(b * self.block + lax.rem(q, self.n_sub) * self.pr, 8), self.pr)]

    def parent(self, d):
        return (2 * (self.ln.z + (-1 if d == 0 else 1)) + self.ln.x, self.ln.t)

    def child(self, d):
        return (2 * (self.ln.z + (1 if d == 0 else -1)) + self.ln.x, self.ln.t)

    def partner(self):
        return (2 * self.ln.z + 1 - self.ln.x, self.ln.t)

    def local(self, src, i, j):
        return pltpu.make_async_copy(src, self.vin.at[i, j], self.lsem.at[i, j])

    def landed(self, view, q, kind):
        rcopy(view, view, self.ssem.at[0, 0], self.rsem.at[q, kind], self.ln.sib).wait_recv()

    def ok(self, q):
        return (q >= 0) & (q < self.total)

    def send(self, src, dst, slot, k, q, kind, dev):
        return rcopy(src, dst, self.ssem.at[slot, k], self.rsem.at[q, kind], dev)

    def wave(self, tau, start=True):
        ln, L = self.ln, self.L
        slot = lax.rem(tau, 2)
        col = ln.x
        leaf = 1 - ln.x

        def each(fn):
            return fn

        q = tau
        b = leaf

        @pl.when(self.ok(q))
        def _():
            v, o = self.vin, self.vout.at[slot, 0]
            if start:
                a, s = self.local(self.view(self.own, q, b), 0, 0), self.local(self.view(self.sibling, q, b), 0, 1)
                a.start()
                s.start()
                a.wait()
                s.wait()
                o[...] = v[0, 0] + v[0, 1]
            cp = self.send(o, self.view(self.rx, q, b), slot, 0, q, 0, self.partner())
            cp.start() if start else cp.wait_send()

        k = jnp.where(col == 0, self.far[0], self.far[1])
        z = ln.z
        up = (2 * (z + (2 * col - 1)) + ln.x, ln.t)
        down = (2 * (z + (1 - 2 * col)) + ln.x, ln.t)
        q1 = tau - 1 - k

        @pl.when(self.ok(q1))
        def _():
            v, o = self.vin, self.vout.at[slot, 1]
            if start:
                a, s = self.local(self.view(self.own, q1, col), 1, 0), self.local(self.view(self.sibling, q1, col), 1, 1)
                a.start()
                s.start()
                xv = self.view(self.rx, q1, col)
                self.landed(xv, q1, 0)
                x = self.local(xv, 1, 2)
                x.start()

                @pl.when(k > 0)
                def _():
                    zv = self.view(self.rz, q1, col)
                    self.landed(zv, q1, 1)
                    g = self.local(zv, 1, 3)
                    g.start()
                    g.wait()

                a.wait()
                s.wait()
                x.wait()
                o[...] = (v[1, 0] + v[1, 1]) + v[1, 2]

                @pl.when(k > 0)
                def _():
                    o[...] += v[1, 3]

            @pl.when(k < L - 1)
            def _():
                cp = self.send(o, self.view(self.rz, q1, col), slot, 1, q1, 1, up)
                cp.start() if start else cp.wait_send()

            @pl.when(k == L - 1)
            def _():
                fv = self.view(self.fin, q1, col)
                cps = [pltpu.make_async_copy(o, fv, self.lsem.at[4, slot]), self.send(o, fv, slot, 2, q1, 5, down), self.send(o, fv, slot, 3, q1, 6, self.partner())]
                for cp in cps:
                    cp.start() if start else (cp.wait() if cp is cps[0] else cp.wait_send())

        for d in range(2):
            kd = self.far[d]
            q2 = tau - 1 - kd
            bz = 2 + d

            @pl.when(self.ok(q2))
            def _():
                v, o = self.vin, self.vout.at[slot, 2 + d]
                if start:
                    a, s = self.local(self.view(self.own, q2, bz), 2, 2 * d), self.local(self.view(self.sibling, q2, bz), 2, 2 * d + 1)
                    a.start()
                    s.start()

                    @pl.when(kd > 0)
                    def _():
                        zv = self.view(self.rz, q2, bz)
                        self.landed(zv, q2, 2 + d)
                        g = self.local(zv, 3, d)
                        g.start()
                        g.wait()

                    a.wait()
                    s.wait()
                    o[...] = v[2, 2 * d] + v[2, 2 * d + 1]

                    @pl.when(kd > 0)
                    def _():
                        o[...] += v[3, d]

                @pl.when(kd < L - 1)
                def _():
                    cp = self.send(o, self.view(self.rz, q2, bz), slot, 4 + 3 * d, q2, 2 + d, self.parent(d))
                    cp.start() if start else cp.wait_send()

                @pl.when(kd == L - 1)
                def _():
                    xv, fv, tot = self.view(self.rx, q2, bz), self.view(self.fin, q2, bz), self.vout.at[slot, 4]
                    cp = self.send(o, xv, slot, 5 + 3 * d, q2, 4, self.partner())
                    if start:
                        cp.start()
                        self.landed(xv, q2, 4)
                        x = self.local(xv, 3, 2)
                        x.start()
                        x.wait()
                        tot[...] = o[...] + v[3, 2]
                    else:
                        cp.wait_send()
                    cps = [pltpu.make_async_copy(tot, fv, self.lsem.at[4, 2 + slot]), self.send(tot, fv, slot, 6 + 3 * d, q2, 7 + d, self.child(d))]
                    for cp in cps:
                        cp.start() if start else (cp.wait() if cp is cps[0] else cp.wait_send())

        r = L - 1 - k
        q3 = tau - L - r

        @pl.when(self.ok(q3) & (r > 0))
        def _():
            fv = self.view(self.fin, q3, col)
            if start:
                self.landed(fv, q3, 5)

            @pl.when(k > 0)
            def _():
                cp = self.send(fv, fv, slot, 10, q3, 5, down)
                cp.start() if start else cp.wait_send()

            cp = self.send(fv, fv, slot, 11, q3, 6, self.partner())
            cp.start() if start else cp.wait_send()

        for d in range(2):
            kd = self.far[d]
            r = L - 1 - kd
            q4 = tau - L - r

            @pl.when(self.ok(q4) & (r > 0))
            def _():
                fv = self.view(self.fin, q4, 2 + d)
                if start:
                    self.landed(fv, q4, 7 + d)

                @pl.when(kd > 0)
                def _():
                    cp = self.send(fv, fv, slot, 12 + d, q4, 7 + d, self.child(d))
                    cp.start() if start else cp.wait_send()

    def step(self, tau):
        self.wave(tau - 2, start=False)
        self.wave(tau)

    def steps(self, t0, t1):
        def body(tau, carry):
            self.step(tau)
            return carry

        lax.fori_loop(t0, t1, body, 0)

    def finish(self):
        self.wave(self.waves - 2, start=False)
        self.wave(self.waves - 1, start=False)

        def body(q, carry):
            self.landed(self.view(self.fin, q, 1 - self.ln.x), q, 6)
            return carry

        lax.fori_loop(0, self.total, body, 0)


N_SUB = 4


def backward_kernel(dm, n_dp, *refs):
    (meta, wdn_s, g1_r, g2_r, bd_r, n32, gu, p_hbm, i_wqkv, i_wo, i_bias, i_tok, i_cot, i_normed, i_q8, i_kk, i_vv, i_mixt, i_n2, i_act, i_gp, i_mid, d_own, d_sib, wup_s) = refs[:25]
    (fin, sm_out, lo32, gt32, gn_h, own, sibl, rz, rx) = refs[25:34]
    (wqkv, wo, wup, wdn, tok, cot, normed, q8, kk, vv, mixt, n2, gp, act, mid, gn, dwa, acc, pbuf, tmp, bbuf, vin, vout, small, sland) = refs[34:59]
    psem, tsem, lsem, osem, nss, nrs, xss, xrs, rls, rss, rrs, sss, srs = refs[59:]
    R, D, NS, hw, f = dm.r, dm.d, dm.ns, dm.hw, dm.f
    ln = Links(n_dp)
    y, c, t = ln.y, ln.c, ln.t
    base = c * NS
    nt, ft = D // 256, f // 256

    srcs = (i_gp, i_act, i_n2, i_cot, i_bias, i_mid, i_wqkv, i_wo, i_mixt, i_q8, i_kk, i_vv, i_normed, i_tok, wup_s)
    dsts = (gp.at[:, pl.ds(0, 2 * f)], act, n2, cot, bbuf, mid, wqkv, wo, mixt, q8, kk, vv, normed, tok, wup.at[t])
    ins = [pltpu.make_async_copy(a, b, lsem.at[i]) for i, (a, b) in enumerate(zip(srcs, dsts))]
    for cp in ins:
        cp.start()
    moved = [pltpu.make_async_copy(d_own, own.at[0], osem.at[0]), pltpu.make_async_copy(d_sib, sibl.at[0], osem.at[1])]
    for cp in moved:
        cp.start()
    bar = pltpu.get_barrier_semaphore()
    group = ln.dp - lax.rem(ln.dp, n_dp)
    for dev in (ln.ypart, ln.sib):
        pl.semaphore_signal(bar, inc=1, device_id=dev, device_id_type=MESH)

    def greet(i, carry):
        pl.semaphore_signal(bar, inc=1, device_id=(lax.rem(ln.dp + i, n_dp), t), device_id_type=MESH)
        return carry

    lax.fori_loop(1, n_dp, greet, 0)
    pl.semaphore_wait(bar, 2 + n_dp - 1)
    red = Reduce(ln, own, sibl, rz, rx, fin, vin, vout, rls, rss, rrs, N_SUB, 3)
    pending = []

    third = f // 3
    for i in range(3):
        v = pl.ds(i * third, third)
        cp = rcopy(n32.at[v], gn_h.at[t, v], nss.at[i], nrs.at[i], ln.ypart)
        cp.start()
        pending.append(cp)
    cp = rcopy(n32, gn_h.at[t], nss.at[3], nrs.at[3], ln.sib)
    cp.start()
    pending.append(cp)

    def landed(view, sem):
        rcopy(view, view, nss.at[0], sem, ln.sib).wait_recv()

    def pass_on(i):
        v = gn_h.at[ln.t_y, pl.ds(i * third, third)]
        landed(v, nrs.at[i])
        cp = rcopy(v, v, nss.at[4 + i], nrs.at[4 + i], ln.sib)
        cp.start()
        pending.append(cp)

    def narrow(src, put):
        n = src.shape[0] // 4
        cps = []
        for i in range(4):
            cps.append(pltpu.make_async_copy(src.at[pl.ds(i * n, n)], tmp.at[i % 2], tsem.at[i % 2]))
            if i == 0:
                cps[0].start()
        for i in range(4):
            if i < 3:
                cps[i + 1].start()
            cps[i].wait()
            put(i * n, n, tmp[i % 2].astype(bf16))

    def put_dn(ts):
        def put(r, n, v):
            wdn[pl.ds(pl.multiple_of(ts * f + r, 16), n), :] = v

        return put

    def put_up(ts):
        def put(r, n, v):
            wup[ts, r : r + n, :] = v

        return put

    wdn[al(t, f), :] = wdn_s[...]
    narrow(gu.at[ln.t_sib], put_up(ln.t_sib))
    landed(gn_h.at[ln.t_sib], nrs.at[3])
    narrow(gn_h.at[ln.t_sib], put_dn(ln.t_sib))
    for i in range(4):
        ins[i].wait()
    acc[...] = jnp.zeros_like(acc)

    def unit(j):
        half = j // (2 * ft)
        hf = jnp.where(half == 0, y, 1 - y)
        return 2 * hf + lax.rem(j, 2 * ft) // ft, lax.rem(j, ft)

    def grad_hidden(half):
        def one(i):
            s, j = i // (2 * ft), half * 2 * ft + lax.rem(i, 2 * ft)
            sh, k = unit(j)
            rs, cs = al(s, R), al(j, 256)
            ga = mmt(cot[rs, :], wdn[pl.ds(pl.multiple_of(sh * f + k * 256, 256), 256), :])
            gp[rs, cs] = (ga * gp[rs, cs].astype(f32)).astype(bf16)

        loop(NS * 2 * ft, one)

    grad_hidden(0)

    def dwup(i):
        sh, j = i // nt, lax.rem(i, nt)
        for n in range(ft):
            dwa[pl.ds(pl.multiple_of(i * 256, 256), 256), n * 256 : n * 256 + 256] = tmm(n2[:, al(j, 256)], gp[:, al(sh * ft + n, 256)])

    loop(2 * nt, dwup)
    up_own = pltpu.make_async_copy(dwa.at[al(c, D)], own.at[1], osem.at[2])
    up_own.start()
    up_sib = rcopy(dwa.at[al(1 - c, D)], sibl.at[1], xss.at[0], xrs.at[0], ln.sib)
    up_sib.start()
    for cp in moved:
        cp.wait()
    red.steps(0, 1)
    ones = jnp.ones((8, dm.rows), bf16)
    for sh in range(2):
        acc[6 + sh, :, :f] = mm(ones, gp[:, sh * f : (sh + 1) * f]) * 0.125

    bd = bd_r[...].reshape(1, D)
    ins[4].wait()
    ins[5].wait()

    def lo_own(s):
        rs = al(s, R)
        gn[rs, :] = mid[rs, :] + bd + mm(act[rs, :], wdn[al(y, 2 * f), :])

    loop(NS, lo_own)
    ins[14].wait()
    narrow(gu.at[ln.t_y], put_up(ln.t_y))
    narrow(gu.at[ln.t_ysib], put_up(ln.t_ysib))
    red.steps(1, 2)

    def mlp(i):
        s, j = i // (2 * ft), lax.rem(i, 2 * ft)
        sh, k = unit(2 * ft + j)
        rs, cs = al(s, R), al(k, 256)
        h = mm(n2[rs, :], wup[sh, :, cs]) + bbuf[sh, 0:1, cs]
        a, g = gelu_pair(h)
        act[rs, al(j, 256)] = a.astype(bf16)
        gp[rs, al(2 * ft + j, 256)] = g.astype(bf16)

    loop(NS * 2 * ft, mlp)
    red.steps(2, 3)
    up_own.wait()
    up_sib.wait()
    pass_on(0)
    red.steps(3, 4)
    pass_on(1)
    red.steps(4, 5)
    pass_on(2)
    narrow(gn_h.at[ln.t_y], put_dn(ln.t_y))
    for i in range(3):
        v = gn_h.at[ln.t_ysib, pl.ds(i * third, third)]
        landed(v, nrs.at[4 + i])
    narrow(gn_h.at[ln.t_ysib], put_dn(ln.t_ysib))
    grad_hidden(1)
    red.steps(5, 6)
    for cp in ins[6:]:
        if cp is not ins[14]:
            cp.wait()

    def gnorm2(s):
        rs = al(s, R)
        tot = None
        for half in range(2):
            for i in range(2):
                sh = 2 * (y if half == 0 else 1 - y) + i
                k = half * 2 + i
                p = mmt(gp[rs, k * f : (k + 1) * f], wup[sh])
                tot = p if tot is None else tot + p
        lo = gn[rs, :] + mm(act[rs, :], wdn[al(1 - y, 2 * f), :])
        dwa[rs, :] = lo
        gn[rs, :] = tot

    loop(NS, gnorm2)
    lo_copies = []
    for s in range(NS):
        v = dwa.at[pl.ds(s * R, R)]
        lo_copies.append((pltpu.make_async_copy(v, lo32.at[base + s], osem.at[3 + s]), rcopy(v, lo32.at[base + s], xss.at[1 + s], xrs.at[1 + s], ln.sib)))
        for cp in lo_copies[-1]:
            cp.start()
    red.steps(6, 7)
    g2 = g2_r[...].reshape(1, D)
    g1 = g1_r[...].reshape(1, D)

    def ln2b(i):
        rs = pl.ds(pl.multiple_of(i * CH, CH), CH)
        xh, r = centred(mid[rs, :])
        go = gn[rs, :]
        co = cot[rs, :].astype(f32)
        g = go * g2
        gx = g * xh
        gm = co + r * (g - jnp.sum(g, -1, keepdims=True) * (1.0 / D) - xh * (jnp.sum(gx, -1, keepdims=True) * (1.0 / D)))
        mid[rs, :] = gm
        gl = gm.astype(bf16)
        act[rs, 0:D] = gl
        acc[0] += fold8(co)
        acc[1] += fold8(gl.astype(f32))
        acc[4] += fold8(go * xh)
        acc[5] += fold8(go)

    loop(dm.rows // CH, ln2b)

    def gmixf(s):
        rs = al(s, R)
        act[rs, D : 2 * D] = mmt(act[rs, 0:D], wo[...]).astype(bf16)

    loop(NS, gmixf)
    own_h = al(y, 2 * hw)

    def over_samples(fn):
        tot = None
        for s in range(NS):
            p = fn(s)
            tot = p if tot is None else tot + p
        return tot

    for a, b in lo_copies:
        a.wait()
        b.wait()

    for n in range(nt):
        cc = slice(n * 256, n * 256 + 256)
        p = over_samples(lambda s: mm(mixt[s, own_h, :], act[s * R : s * R + R, cc]))
        for sh in range(2):
            dwa[sh * D + 3 * hw : sh * D + 4 * hw, cc] = p[sh * hw : (sh + 1) * hw]
    red.steps(7, 8)
    lane = lax.broadcasted_iota(jnp.int32, (1, 128), 1)
    masks = (lane < HEAD_DIM, lane >= HEAD_DIM)
    total = NS * dm.pairs

    def p_copy(i):
        slot = lax.rem(i, 2)
        return pltpu.make_async_copy(p_hbm.at[i], pbuf.at[slot], psem.at[slot])

    p_copy(0).start()

    def attn(i):
        s, p = i // dm.pairs, lax.rem(i, dm.pairs)
        slot = lax.rem(i, 2)
        rs, cs = al(s, R), al(p, 128)

        @pl.when(i + 1 < total)
        def _():
            p_copy(i + 1).start()

        p_copy(i).wait()
        q, k, v, do = q8[rs, cs], kk[rs, cs], vv[rs, cs], act[rs, pl.ds(pl.multiple_of(D + p * 128, 128), 128)]
        dv, dk = [], []
        for h in range(2):
            pt = pbuf[slot, h]
            pf = pt.astype(f32)
            dp = mmt(jnp.where(masks[h], v, jnp.bfloat16(0)), do)
            dsum = jnp.sum(pf * dp, 0, keepdims=True)
            ds = (pf * (dp - dsum)).astype(bf16)
            dv.append(mm(pt, do))
            dk.append(mm(ds, q))
            o = tmm(k, ds)
            hr = pl.ds(pl.multiple_of(p * 128 + h * HEAD_DIM, HEAD_DIM), HEAD_DIM)
            mixt[s, hr, :] = (o[h * HEAD_DIM : (h + 1) * HEAD_DIM] * 0.125).astype(bf16)
        kk[rs, cs] = jnp.where(masks[0], dk[0], dk[1]).astype(bf16)
        vv[rs, cs] = jnp.where(masks[0], dv[0], dv[1]).astype(bf16)

    loop(total, attn)
    for n in range(nt):
        cc = slice(n * 256, n * 256 + 256)
        p = over_samples(lambda s: mm(mixt[s, own_h, :], normed[s * R : s * R + R, cc]))
        tk = tmm(kk[:, own_h], normed[:, cc])
        tv = tmm(vv[:, own_h], normed[:, cc])
        for sh in range(2):
            h = slice(sh * hw, (sh + 1) * hw)
            dwa[sh * D : sh * D + hw, cc] = p[h]
            dwa[sh * D + hw : sh * D + 2 * hw, cc] = tk[h]
            dwa[sh * D + 2 * hw : sh * D + 3 * hw, cc] = tv[h]
    a_own = pltpu.make_async_copy(dwa.at[al(c, D)], own.at[2], osem.at[2])
    a_own.start()
    a_sib = rcopy(dwa.at[al(1 - c, D)], sibl.at[2], xss.at[5], xrs.at[5], ln.sib)
    a_sib.start()
    onesr = jnp.ones((8, R), bf16)
    acc[8, :, 0 : 2 * hw] = over_samples(lambda s: mmt(onesr, mixt[s, own_h, :])) * 0.125
    acc[9, :, 0 : 2 * hw] = mm(ones, vv[:, own_h]) * 0.125
    a_own.wait()
    a_sib.wait()
    red.steps(8, 9)

    def gnorm1(s):
        rs = al(s, R)
        gn[rs, :] = tmm(mixt[s], wqkv[0:D, :]) + mm(kk[rs, :], wqkv[D : 2 * D, :]) + mm(vv[rs, :], wqkv[2 * D : 3 * D, :])

    loop(NS, gnorm1)

    def ln1b(s):
        for r0, n in row_chunks(dm):
            rs = pl.ds(pl.multiple_of(s * R + r0, 16), n)
            x = tok[rs, :].astype(f32)
            keep = keep_of(meta, base, s, r0, n) if r0 == 0 else None
            xh, r = centred(x if keep is None else x * keep)
            go = gn[rs, :]
            g = go * g1
            gx = g * xh
            gi = r * (g - jnp.sum(g, -1, keepdims=True) * (1.0 / D) - xh * (jnp.sum(gx, -1, keepdims=True) * (1.0 / D)))
            o = mid[rs, :] + gi
            mid[rs, :] = o if keep is None else o * keep
            acc[2] += fold8(go * xh)
            acc[3] += fold8(go)

    loop(NS, ln1b)
    gt_copies = []
    for s in range(NS):
        v = mid.at[pl.ds(s * R, R)]
        gt_copies.append((pltpu.make_async_copy(v, gt32.at[base + s], osem.at[3 + s]), rcopy(v, gt32.at[base + s], xss.at[6 + s], xrs.at[6 + s], ln.sib)))
        for cp in gt_copies[-1]:
            cp.start()

    tot = jnp.sum(acc[...], 1)
    for sh in range(2):
        small[sh, 0:6, :] = tot[0:6]
        small[sh, 6:7, :] = tot[6 + sh : 7 + sh]
        small[sh, 7:8, 0:hw] = tot[8:9, sh * hw : (sh + 1) * hw]
        small[sh, 7:8, hw : 2 * hw] = tot[9:10, sh * hw : (sh + 1) * hw]
        small[sh, 7:8, 2 * hw :] = jnp.zeros((1, D - 2 * hw), f32)
    cp = rcopy(small.at[1 - c], small.at[2], xss.at[10], xrs.at[10], ln.sib)
    cp.start()
    cp.wait()
    sland[ln.dp] = small[c] + small[2]

    def peer(i):
        d = lax.rem(ln.dp + i, n_dp)
        return rcopy(sland.at[ln.dp], sland.at[ln.dp], sss.at[d], srs.at[ln.dp], (d, t))

    def spread(i, carry):
        peer(i).start()
        return carry

    lax.fori_loop(1, n_dp, spread, 0)
    red.steps(9, red.waves)
    red.finish()

    def gathered(i, carry):
        peer(i).wait_send()
        d = lax.rem(ln.dp + i, n_dp)
        rcopy(sland.at[d], sland.at[d], sss.at[d], srs.at[d], (d, t)).wait_recv()
        return carry

    lax.fori_loop(1, n_dp, gathered, 0)
    sm_out[...] = lax.fori_loop(1, n_dp, lambda i, v: v + sland[i], sland[0])
    for a, b in gt_copies:
        a.wait()
        b.wait()
    for cp in pending:
        cp.wait_send()


def backward_call(dm, n_dp, small, big):
    M, D, f = dm.rows, dm.d, dm.f
    sds, vm, dma = jax.ShapeDtypeStruct, pltpu.VMEM, pltpu.SemaphoreType.DMA
    st = sds((3, D, D), f32)
    outs = [st, sds((8, D), f32), sds((dm.samples, dm.r, D), f32), sds((dm.samples, dm.r, D), f32), sds((dm.n_t, f, D), f32), st, st, st, st]
    row, wide = vm((M, D), bf16), vm((M, 2 * f), bf16)
    pr = D // 4 // N_SUB
    scratch = [vm((3 * D, D), bf16), vm((D, D), bf16), vm((dm.n_t, D, f), bf16), vm((dm.ff, D), bf16)] + [row] * 6
    scratch += [vm((dm.ns, D, dm.r), bf16), row, vm((M, dm.ff), bf16), wide, vm((M, D), f32), vm((M, D), f32), vm((2 * D, D), f32), vm((10, 8, D), f32)]
    scratch += [vm((2, 2, dm.r, dm.r), bf16), vm((2, f // 4, D), f32), vm((dm.n_t, 16, D), f32), vm((4, 4, pr, D), f32), vm((2, 5, pr, D), f32), vm((3, 8, D), f32), vm((n_dp, 8, D), f32)]
    nq = 3 * N_SUB
    scratch += [dma((2,)), dma((2,)), dma((15,)), dma((7,)), dma((7,)), dma((7,)), dma((11,)), dma((11,)), dma((5, 4)), dma((2, 14)), dma((nq, Reduce.KINDS)), dma((n_dp,)), dma((n_dp,))]

    def kern(*refs):
        backward_kernel(dm, n_dp, *refs)

    return pl.pallas_call(
        kern,
        out_shape=outs,
        in_specs=[SM] + [V] * (len(small) - 1) + [ANY] * len(big),
        out_specs=[ANY, V] + [ANY] * 7,
        scratch_shapes=scratch,
        compiler_params=pltpu.CompilerParams(vmem_limit_bytes=VMEM_LIMIT, collective_id=2, has_side_effects=True),
        name="backward",
    )(*small, *big)


def shards(tokens, metadata, cotangent, w_query, w_key, w_value, w_out, b_query, b_value, b_out, w_up, b_up, w_down, b_down, gain_one, shift_one, gain_two, shift_two, n_dp, n_t):
    dm = Dims(tokens, w_up, n_t)
    D, hw, f = dm.d, dm.hw, dm.f
    bias = jnp.concatenate([b_up, b_query, b_value, jnp.zeros((16 * D - f - 2 * hw,), f32)]).reshape(16, D)
    small = (metadata, w_query, w_key, w_value, w_out, w_up, w_down, bias, gain_one, shift_one, gain_two, shift_two, b_out)
    (_, gu, n32, p, wqkv, wo, bb, tok, cot, normed, q8, kk, vv, mixt, n2, act, gp, mid, d_own, d_sib) = forward_call(dm, n_dp, small, (tokens, cotangent))
    small = (metadata, w_down, gain_one, gain_two, b_down)
    fin, sm, lo, gt, *_ = backward_call(dm, n_dp, small, (n32, gu, p, wqkv, wo, bb, tok, cot, normed, q8, kk, vv, mixt, n2, act, gp, mid, d_own, d_sib, w_up))
    a_ = fin[2]
    return (
        lo[:, : dm.length].astype(bf16),
        gt[:, : dm.length],
        a_[0:hw].T,
        a_[hw : 2 * hw].T,
        a_[2 * hw : 3 * hw].T,
        a_[3 * hw : 4 * hw],
        sm[7, :hw],
        sm[7, hw : 2 * hw],
        sm[1],
        fin[1],
        sm[6],
        fin[0],
        sm[0],
        sm[2],
        sm[3],
        sm[4],
        sm[5],
    )


def solution(mesh):
    n_dp, n_t = mesh.shape["dp"], mesh.shape["tensor"]
    rows, cols, vec, rep = P("dp", None, None), P(None, "tensor"), P("tensor"), P()
    srow = P("tensor", None)

    def run(*args):
        return shards(*args, n_dp=n_dp, n_t=n_t)

    return jax.shard_map(
        run,
        mesh=mesh,
        in_specs=(rows, P("dp"), rows, cols, cols, cols, srow, vec, vec, rep, cols, vec, srow, rep, rep, rep, rep, rep),
        out_specs=(rows, rows, cols, cols, cols, srow, vec, vec, rep, cols, vec, srow, rep, rep, rep, rep, rep),
        check_vma=False,
    )
```

time: 732 us -> 555 us (0.76)
  waiting for transfers between devices: 437 us -> 0 us
  Pallas kernels: 178 us -> 520 us
  other arithmetic: 40 us -> 0.01 us
  local copies, waits for them, and re-layouts: 61.7 us -> 31.5 us
  between operations: 14 us -> 0.72 us
    pallas_call x2, Pallas kernels: 178 us -> 520 us  [the longest x1 416 us: backward_call(): pl.pallas_call(kern, out_shape=outs, in_specs=[SM] + [V] * (len(small) -...]
    psum x1 -> x0, waiting for transfers between devices: 227 us -> none  [shards(): dw = lax.psum(dw[...], 'dp')]
    all_gather x2 -> x0, waiting for transfers between devices: 194 us -> none  [the longest x1 165 us: shards(): g = lax.all_gather(own, 'tensor')]
    slice x9 -> x2, local copies, waits for them, and re-layouts: 24.1 us -> 3.87 us  [the longest x1 3.31 us: shards(): lo[:, :dm.length].astype(bf16)]
    another operation x2 -> x0, other arithmetic: 16 us -> none
    reduce_scatter x1 -> x0, waiting for transfers between devices: 15.8 us -> none  [shards(): lax.psum_scatter(dw, 'tensor', axis_index_groups=sib, scatter_dimension=0)]
    concatenate x2 -> x0, other arithmetic: 12.2 us -> none  [the longest x1 10.2 us: shards(): dw = jnp.concatenate([dwd, dwu, dwa], 1)]
    unnamed x6 -> x1, other arithmetic: 11.7 us -> 0.01 us
  transfers between devices with their start and end apart: 4 -> 0, of which waited for: 4 -> 0; matrix products, arithmetic and copies ran while one was open for 4% -> 0% of each run, Pallas kernels for 0% -> 0%
where the time goes in v2:
time: 555 us; the launch traced here: 553 us
  Pallas kernels  520 us (94%)
  local copies, waits for them, and re-layouts  31.5 us (6%)
    pallas_call x1, Pallas kernels, backward_call(): pl.pallas_call(kern, out_shape=outs, in_specs=[SM] + [V] * (len(small) -...  416 us
    pallas_call x1, Pallas kernels, forward_call(): pl.pallas_call(kern, out_shape=outs, in_specs=[SM] + [V] * (len(small) -...  104 us
    unnamed x17, local copies, waits for them, and re-layouts  20.8 us

profile of v2, /device:TPU:0, one launch (start us, length us, event | category | flops | bytes accessed | tf_op | source)
XLA Modules:
  0.0 552.6 jit_solution(10546793138961601762)
XLA Ops:
  0.7 0.8 concatenate.3
  1.5 0.6 reshape.41.refs_7_
  2.1 1.9 copy.35.refs_1_
  4.0 1.9 copy.36.refs_2_
  5.8 1.9 copy.37.refs_3_
  7.7 0.0 copy-start.1
  7.7 4.4 copy.38.refs_13_
  12.1 0.0 copy-done.1
  12.1 2.3 copy.39.refs_14_
  14.4 104.4 %forward.1 = (f32[4,784,768]{2,1,0:T(8,128)}, f32[4,768,768]{2,1,0:T(8,128)}, f32[768,768]{1,0:T(8,128)}, bf16[24,2,272,272]{3,2,1,0:T(8,128)(2,1)}, bf16[2304,7...) custom-call(s32[8]{0:T(128)} %refs_0_.3, ...), custom_call_target="tpu_custom_call" | custom-call | tf_op jit(solution)/shard_map/forward/pallas_call | solution.py:506
  118.8 416.0 %backward.1 = (f32[3,768,768]{2,1,0:T(8,128)}, f32[8,768]{1,0:T(8,128)}, f32[8,272,768]{2,1,0:T(8,128)}, f32[8,272,768]{2,1,0:T(8,128)}, f32[4,768,768]{2,1,0:T(...) custom-call(s32[8]{0:T(128)} %refs_0_.3, ...), custom_call_target="tpu_custom_call" | custom-call | tf_op jit(solution)/shard_map/backward/pallas_call | solution.py:1107
  534.8 0.0 copy-start
  534.8 3.3 slice.105
  538.1 0.0 copy-start.2
  538.1 2.3 copy.40
  540.4 0.0 copy-done.2
  540.4 0.6 fusion
  541.0 0.7 slice_reduce_fusion
  541.7 0.0 copy-done
  541.7 0.0 slice-start
  541.7 1.4 slice_bitcast_fusion.2
  543.1 0.0 slice-start.1
  543.1 2.7 slice_bitcast_fusion
  545.8 0.0 slice-done
  545.8 1.5 slice-done.1
  547.4 0.6 slice.70
  547.9 4.7 copy.41
  (2 shorter events, 0.0 us)
Async XLA Ops:
  7.7 4.4 copy-start.1
  534.8 6.9 %copy-start = (f32[3,768,768]{2,1,0:T(8,128)S(1)}, f32[3,768,768]{2,1,0:T(8,128)}, u32[]{:S(2)}) copy-start(f32[3,768,768]{2,1,0:T(8,128)} %get-tuple-element.61) | copy-start | bytes 21233668
  538.1 2.3 copy-start.2
  541.7 4.2 slice-start
  543.1 4.2 slice-start.1

commit v3 on v2

v3 whole, which is shorter than its diff:
```python
import math

import jax
import jax.numpy as jnp
from jax import lax
from jax.experimental import pallas as pl
from jax.experimental.pallas import tpu as pltpu
from jax.sharding import PartitionSpec as P

HEAD_DIM = 64
EPS = 1e-05
MESH = pl.DeviceIdType.MESH
f32 = jnp.float32
bf16 = jnp.bfloat16
VMEM_LIMIT = 63 << 20
RING = 8
CH = 64
TAIL_P = 0.24
TAIL = (
    0.08952743306829739,
    0.15551359433427508,
    -0.15404885518029288,
    0.6255903019940591,
    -0.6460706945688248,
    0.5545739487327468,
    -0.12508572868970558,
)
INV_SQRT_2PI = 1.0 / math.sqrt(2.0 * math.pi)
HALF_LOG2E = -0.5 / math.log(2.0)


def mm(a, b):
    return lax.dot_general(a, b, (((1,), (0,)), ((), ())), preferred_element_type=f32)


def mmt(a, b):
    return lax.dot_general(a, b, (((1,), (1,)), ((), ())), preferred_element_type=f32)


def tmm(a, b):
    return lax.dot_general(a, b, (((0,), (0,)), ((), ())), preferred_element_type=f32)


def loop(n, fn):
    def body(i, carry):
        fn(i)
        return carry

    lax.fori_loop(0, n, body, 0)


def al(i, step):
    return pl.ds(pl.multiple_of(i * step, step), step)


def centred(x):
    d = x.shape[-1]
    mu = jnp.sum(x, -1, keepdims=True) * (1.0 / d)
    xm = x - mu
    var = jnp.sum(xm * xm, -1, keepdims=True) * (1.0 / d)
    r = lax.rsqrt(var + EPS)
    return xm * r, r


def gelu_pair(v):
    d = 1.0 + TAIL_P * jnp.abs(v)
    t = pltpu.reciprocal(d, approx=True)
    t = t * (2.0 - d * t)
    e = jnp.exp2(HALF_LOG2E * (v * v))
    acc = TAIL[6] * t + TAIL[5]
    for k in range(4, -1, -1):
        acc = acc * t + TAIL[k]
    q = (acc * t) * e
    cdf = jnp.where(v < 0, q, 1.0 - q)
    return v * cdf, cdf + (v * e) * INV_SQRT_2PI


def fold8(x):
    return jnp.sum(x.reshape(x.shape[0] // 8, 8, x.shape[1]), 0)


class Dims:
    def __init__(self, tokens, w_up, n_t):
        self.samples, self.length, self.d = tokens.shape
        self.ns = self.samples // 2
        self.r = -(-self.length // 16) * 16
        self.rows = self.ns * self.r
        self.f = w_up.shape[1]
        self.ff = self.f * n_t
        self.n_t = n_t
        self.heads = self.d // HEAD_DIM
        self.pairs = self.heads // 2
        self.hw = self.d // n_t


class Links:
    def __init__(self, n_dp):
        self.n_dp = n_dp
        self.dp = lax.axis_index("dp")
        self.t = lax.axis_index("tensor")
        self.y, self.c = self.t // 2, lax.rem(self.t, 2)
        self.z, self.x = self.dp // 2, lax.rem(self.dp, 2)
        self.length = n_dp // 2
        self.sib = (self.dp, 2 * self.y + 1 - self.c)
        self.ypart = (self.dp, 2 * (1 - self.y) + self.c)
        self.t_sib = 2 * self.y + 1 - self.c
        self.t_y = 2 * (1 - self.y) + self.c
        self.t_ysib = 2 * (1 - self.y) + 1 - self.c
        g = lax.rem(self.dp, RING)
        half = RING // 2
        zz, xx = g // 2, lax.rem(g, 2)
        self.pos = jnp.where(xx == 0, zz, RING - 1 - zz)
        base = self.dp - g

        def at(pos):
            pos = lax.rem(pos + RING, RING)
            local = jnp.where(pos < half, 2 * pos, 2 * (RING - 1 - pos) + 1)
            return (base + local, self.t)

        self.step = 1 - 2 * self.c
        self.ahead, self.behind = at(self.pos + self.step), at(self.pos - self.step)

    def piece(self, offset):
        return lax.rem(self.pos + offset * self.step + RING, RING)


def rcopy(src, dst, ssem, rsem, dev):
    return pltpu.make_async_remote_copy(src_ref=src, dst_ref=dst, send_sem=ssem, recv_sem=rsem, device_id=dev, device_id_type=MESH)


def enter(devs):
    bar = pltpu.get_barrier_semaphore()
    for d in devs:
        pl.semaphore_signal(bar, inc=1, device_id=d, device_id_type=MESH)
    pl.semaphore_wait(bar, len(devs))


class Gather:
    def __init__(self, ln, src, out, direct, ssem, rsem):
        self.ln, self.src, self.out, self.direct = ln, src, out, direct
        self.ssem, self.rsem = ssem, rsem
        self.passed = self.passed_sib = False
        self.rows = src.shape[0]
        self.piece_rows = (self.rows - direct) // RING

    def at(self, ref, offset):
        return ref.at[pl.ds(pl.multiple_of(self.direct + self.ln.piece(offset) * self.piece_rows, 8), self.piece_rows)]

    def copy(self, src, dst, k, dev):
        return rcopy(src, dst, self.ssem.at[k], self.rsem.at[k], dev)

    def landed(self, view, k):
        rcopy(view, view, self.ssem.at[k], self.rsem.at[k], self.ln.sib).wait_recv()

    def spread_y(self):
        return self.copy(self.at(self.src, 0), self.at(self.out.at[self.ln.t], 0), 0, self.ln.ypart)

    def direct_y(self):
        d = pl.ds(0, self.direct)
        return self.copy(self.src.at[d], self.out.at[self.ln.t].at[d], 1, self.ln.ypart)

    def whole_sib(self):
        return self.copy(self.src, self.out.at[self.ln.t], 2, self.ln.sib)

    def start_y(self):
        self.spread_y().start()
        self.direct_y().start()

    def start_sib(self):
        self.whole_sib().start()

    def wait_sib(self):
        self.landed(self.out.at[self.ln.t_sib], 2)

    def to_sib(self, offset):
        v = self.at(self.out.at[self.ln.t_y], offset)
        return self.copy(v, v, 11 + 4 + offset, self.ln.sib)

    def direct_sib(self):
        v = self.out.at[self.ln.t_y].at[pl.ds(0, self.direct)]
        return self.copy(v, v, 10, self.ln.sib)

    def ring_ahead(self, s):
        v = self.at(self.out.at[self.ln.t_y], -s)
        return self.copy(v, v, 3 + s, self.ln.ahead)

    def ring_behind(self, s):
        v = self.at(self.out.at[self.ln.t_y], s)
        return self.copy(v, v, 7 + s, self.ln.behind)

    def tick(self, i):
        ln, out = self.ln, self.out.at[self.ln.t_y]
        if i == 0:
            self.landed(self.at(out, 0), 0)
            self.ring_ahead(0).start()
            self.ring_behind(0).start()
            self.to_sib(0).start()
            return
        s = i - 1
        self.landed(self.at(out, -s - 1), 3 + s)
        if s < 3:
            self.ring_ahead(s + 1).start()
            self.landed(self.at(out, s + 1), 7 + s)
            if s < 2:
                self.ring_behind(s + 1).start()
        self.to_sib(-s - 1).start()
        if s < 3:
            self.to_sib(s + 1).start()
        if i == 4:
            self.direct_landed()

    def direct_landed(self):
        if not self.passed:
            self.passed = True
            self.landed(self.out.at[self.ln.t_y].at[pl.ds(0, self.direct)], 1)
            self.direct_sib().start()

    def direct_sib_landed(self):
        if not self.passed_sib:
            self.passed_sib = True
            self.landed(self.out.at[self.ln.t_ysib].at[pl.ds(0, self.direct)], 10)

    def finish(self):
        ln, out = self.ln, self.out.at[self.ln.t_ysib]
        for offset in range(-4, 4):
            v = out.at[pl.ds(pl.multiple_of(self.direct + lax.rem(ln.pos - offset * ln.step + RING, RING) * self.piece_rows, 8), self.piece_rows)]
            self.landed(v, 11 + 4 + offset)
        self.direct_sib_landed()

    def drain(self):
        cps = [self.spread_y(), self.direct_y(), self.whole_sib(), self.direct_sib()]
        cps += [self.ring_ahead(s) for s in range(4)] + [self.ring_behind(s) for s in range(3)]
        cps += [self.to_sib(o) for o in range(-4, 4)]
        for cp in cps:
            cp.wait_send()


GATHER_SEMS = 19


def keep_of(meta, base, s, r0, n):
    rows = lax.broadcasted_iota(jnp.int32, (n, 1), 0) + r0
    return jnp.where(rows == 1, meta[base + s].astype(f32), 1.0)


def row_chunks(dm):
    out, r = [], 0
    while r < dm.r:
        n = min(CH, dm.r - r)
        out.append((r, n))
        r += n
    return out


def forward_kernel(dm, n_dp, *refs):
    (meta, wq, wk, wv, wo_s, wup_s, wdn_s, bup_r, bq_r, bv_r, g1_r, s1_r, g2_r, s2_r, bo_r, tokens, cotan) = refs[:17]
    (gu, gn_h, n32, p_hbm, o_wqkv, o_wo, o_bias, o_tok, o_cot, o_normed, o_q8, o_kk, o_vv, o_mixt, o_n2, o_act, o_gp, o_mid, d_own, d_sib) = refs[17:37]
    (tok3, cot3, tok, cot, wqkv, wo, wup, normed, q8, kk, vv, mixt, n2, act, gp, mid, dwd, pbuf, tmp, bbuf, bqv, ga, ustage) = refs[37:60]
    psem, tsem, lsem, osem, ssa, rsa, ssu, rsu, ssn, rsn, ssd, rsd = refs[60:]
    R, D, NS, hw, f = dm.r, dm.d, dm.ns, dm.hw, dm.f
    ln = Links(n_dp)
    y, c, t = ln.y, ln.c, ln.t
    base = c * NS

    def row(ref):
        return ref[...].reshape(1, D)

    loads = [pltpu.make_async_copy(tokens, tok3, lsem.at[0]), pltpu.make_async_copy(cotan, cot3, lsem.at[1])]
    for cp in loads:
        cp.start()
    outs = []

    def put(src, dst):
        cp = pltpu.make_async_copy(src, dst, osem.at[len(outs)])
        cp.start()
        outs.append(cp)

    own_a = mid.at[pl.ds(0, 16 + 3 * hw)]
    mid[0:16, :] = jnp.zeros((16, D), f32)
    mid[0:1, 0:f] = bup_r[...].reshape(1, f)
    mid[1:2, 0:hw] = bq_r[...].reshape(1, hw)
    mid[1:2, hw : 2 * hw] = bv_r[...].reshape(1, hw)
    bbuf[t] = mid[0:16, :]
    for i, w in enumerate((wq, wk, wv)):
        mid[16 + i * hw : 16 + (i + 1) * hw, :] = w[...].astype(f32)
        wqkv[pl.ds(pl.multiple_of(i * D + t * hw, 16), hw), :] = w[...]
    wo[al(t, hw), :] = wo_s[...]
    g_a = Gather(ln, own_a, ga, 16 + hw, ssa, rsa)
    g_u = Gather(ln, ustage, gu, hw + D // 3, ssu, rsu)
    g_n = Gather(ln, n32, gn_h, D // 3, ssn, rsn)
    enter((ln.ypart, ln.sib, ln.ahead, ln.behind))
    g_a.start_y()
    g_a.start_sib()
    ustage[0:hw, :] = wo_s[...].astype(f32)

    def widen(i):
        rs = al(i, 64)
        ustage[pl.ds(pl.multiple_of(hw + i * 64, 64), 64), :] = wup_s[rs, :].astype(f32)
        dwd[1, rs, :] = wdn_s[rs, :].astype(f32)
        wup[c, rs, :] = wup_s[rs, :]

    loop(D // 64, widen)
    put(dwd.at[1], n32)
    g_u.spread_y().start()
    outs[0].wait()
    g_n.spread_y().start()
    g_u.direct_y().start()
    g_n.direct_y().start()
    g_u.start_sib()
    g_n.start_sib()

    for cp in loads:
        cp.wait()
    g1, s1, g2, s2, bo = (row(r) for r in (g1_r, s1_r, g2_r, s2_r, bo_r))
    grp = dm.length // 32
    rest, pad = dm.length - grp * 32, R - grp * 32

    def selection(n_out, n_in):
        r = lax.broadcasted_iota(jnp.int32, (NS * n_out, n_in * 2 * NS), 0)
        col = lax.broadcasted_iota(jnp.int32, (NS * n_out, n_in * 2 * NS), 1)
        hit = (col == lax.rem(r, n_out) * (2 * NS) + base + r // n_out) & (lax.rem(r, n_out) < n_in)
        return jnp.where(hit, 1.0, 0.0).astype(bf16)

    sel = selection(32, 32)

    def regroup(g):
        for src, dst in ((tok3, tok), (cot3, cot)):
            v = src[al(g, 32)].astype(f32).reshape(32 * 2 * NS, D).astype(bf16)
            o = mm(sel, v).astype(bf16)
            for s in range(NS):
                dst[pl.ds(pl.multiple_of(s * R + g * 32, 16), 32), :] = o[s * 32 : (s + 1) * 32]

    loop(grp, regroup)
    if pad:
        sel_end = selection(pad, rest)
        for src, dst in ((tok3, tok), (cot3, cot)):
            v = src[grp * 32 : grp * 32 + rest].astype(f32).reshape(rest * 2 * NS, D).astype(bf16)
            o = mm(sel_end, v).astype(bf16)
            for s in range(NS):
                dst[s * R + grp * 32 : (s + 1) * R, :] = o[s * pad : (s + 1) * pad]
    put(tok, o_tok)
    put(cot, o_cot)

    def ln1(s):
        for r, n in row_chunks(dm):
            rs = pl.ds(pl.multiple_of(s * R + r, 16), n)
            x = tok[rs, :].astype(f32)
            if r == 0:
                x = x * keep_of(meta, base, s, r, n)
            xh, _ = centred(x)
            normed[rs, :] = (xh * g1 + s1).astype(bf16)

    loop(NS, ln1)
    put(normed, o_normed)

    def fetch(src, k):
        cp = pltpu.make_async_copy(src, tmp.at[k], tsem.at[k])
        cp.start()
        return cp

    def take_a(tp):
        bbuf[tp] = ga[tp, 0:16, :]
        for i in range(3):
            wqkv[pl.ds(pl.multiple_of(i * D + tp * hw, 16), hw), :] = ga[tp, 16 + i * hw : 16 + (i + 1) * hw, :].astype(bf16)

    lane = lax.broadcasted_iota(jnp.int32, (1, 128), 1)
    masks = (lane < HEAD_DIM, lane >= HEAD_DIM)
    hp = dm.pairs // 2
    tail = R - 16
    live = lax.broadcasted_iota(jnp.int32, (16, 1), 0) < dm.length - tail

    def project(hf):
        for i in range(2):
            b = bbuf[2 * hf + i]
            bqv[0:1, i * hw : (i + 1) * hw] = b[1:2, 0:hw]
            bqv[1:2, i * hw : (i + 1) * hw] = b[1:2, hw : 2 * hw]
        cs = al(hf, 2 * hw)

        def one(s):
            rs = al(s, R)
            n = normed[rs, :]
            w = [wqkv[pl.ds(pl.multiple_of(i * D + hf * 2 * hw, 128), 2 * hw), :] for i in range(3)]
            q8[rs, cs] = (mmt(n, w[0]) + bqv[0:1, : 2 * hw]).astype(bf16) * jnp.bfloat16(0.125)
            kk[rs, cs] = mmt(n, w[1]).astype(bf16)
            vv[rs, cs] = (mmt(n, w[2]) + bqv[1:2, : 2 * hw]).astype(bf16)

        loop(NS, one)

    def p_copy(hf, i):
        slot = lax.rem(i, 2)
        return pltpu.make_async_copy(pbuf.at[slot], p_hbm.at[(i // hp) * dm.pairs + hf * hp + lax.rem(i, hp)], psem.at[slot])

    def attend(hf, ticks):
        total = NS * hp

        def one(i):
            s, p = i // hp, hf * hp + lax.rem(i, hp)
            slot = lax.rem(i, 2)
            rs, cs = al(s, R), al(p, 128)
            for k, fn in ticks:
                pl.when(i == k)(fn)

            @pl.when(i >= 2)
            def _():
                p_copy(hf, i - 2).wait()

            q, k, v = q8[rs, cs], kk[rs, cs], vv[rs, cs]
            for h in range(2):
                st = mmt(jnp.where(masks[h], k, jnp.bfloat16(0)), q)
                sa = st[:tail]
                sb = jnp.where(live, st[tail:], -1e30)
                m = jnp.maximum(jnp.max(sa, 0, keepdims=True), jnp.max(sb, 0, keepdims=True))
                ea, eb = jnp.exp(sa - m), jnp.exp(sb - m)
                inv = 1.0 / (jnp.sum(ea, 0, keepdims=True) + jnp.sum(eb, 0, keepdims=True))
                pbuf[slot, h, :tail, :] = (ea * inv).astype(bf16)
                pbuf[slot, h, tail:, :] = (eb * inv).astype(bf16)
                o = tmm(v, pbuf[slot, h])
                hr = pl.ds(pl.multiple_of(p * 128 + h * HEAD_DIM, HEAD_DIM), HEAD_DIM)
                mixt[s, hr, :] = o[h * HEAD_DIM : (h + 1) * HEAD_DIM].astype(bf16)
            p_copy(hf, i).start()

        loop(total, one)
        p_copy(hf, total - 2).wait()
        p_copy(hf, total - 1).wait()

    g_a.wait_sib()
    take_a(ln.t_sib)
    g_a.tick(0)
    project(y)
    g_a.tick(1)
    attend(y, [(3, lambda: g_a.tick(2)), (9, lambda: g_a.tick(3))])
    g_a.tick(4)
    g_a.finish()
    take_a(ln.t_y)
    take_a(ln.t_ysib)
    put(wqkv, o_wqkv)
    put(bbuf, o_bias)
    g_u.tick(0)
    project(1 - y)
    put(q8, o_q8)
    put(kk, o_kk)
    put(vv, o_vv)
    attend(1 - y, [(2, lambda: g_u.tick(1)), (9, lambda: g_u.tick(2))])
    g_u.tick(3)
    put(mixt, o_mixt)
    g_a.drain()
    g_u.direct_landed()
    wo_rows = [fetch(gu.at[tp, pl.ds(0, hw)], i) for i, tp in enumerate((ln.t_y,))]
    g_u.wait_sib()
    wo_rows.append(fetch(gu.at[ln.t_sib, pl.ds(0, hw)], 1))
    g_u.direct_sib_landed()
    wo_rows.append(fetch(gu.at[ln.t_ysib, pl.ds(0, hw)], 2))
    for i, tp in enumerate((ln.t_y, ln.t_sib, ln.t_ysib)):
        wo_rows[i].wait()
        wo[al(tp, hw), :] = tmp[i].astype(bf16)
    put(wo, o_wo)
    ups = [fetch(gu.at[ln.t_sib, pl.ds((i + 1) * hw, hw)], i) for i in range(4)]

    def outp(s):
        rs = al(s, R)
        mid[rs, :] = tmm(mixt[s], wo[...])

    loop(NS, outp)

    def ln2(s):
        for r, n in row_chunks(dm):
            rs = pl.ds(pl.multiple_of(s * R + r, 16), n)
            x = tok[rs, :].astype(f32)
            if r == 0:
                x = x * keep_of(meta, base, s, r, n)
            m = x + (mid[rs, :] + bo)
            mid[rs, :] = m
            xh, _ = centred(m)
            n2[rs, :] = (xh * g2 + s2).astype(bf16)

    g_u.tick(4)
    g_n.tick(0)
    loop(NS, ln2)
    put(mid, o_mid)
    put(n2, o_n2)
    for i in range(4):
        ups[i].wait()
        wup[1 - c, i * hw : (i + 1) * hw, :] = tmp[i].astype(bf16)
    ft = f // 256

    def mlp(i):
        for k, n in ((7, 1), (14, 2), (21, 3)):
            pl.when(i == k)(lambda: g_n.tick(n))
        s, j = i // (2 * ft), lax.rem(i, 2 * ft)
        rs, sh, cs = al(s, R), j // ft, al(lax.rem(j, ft), 256)
        h = mm(n2[rs, :], wup[sh, :, cs]) + bbuf[2 * y + sh, 0:1, cs]
        a, g = gelu_pair(h)
        act[rs, al(j, 256)] = a.astype(bf16)
        gp[rs, al(j, 256)] = g.astype(bf16)

    loop(NS * 2 * ft, mlp)
    put(act, o_act)
    put(gp, o_gp)

    def dwdn(sh):
        def one(j):
            dwd[sh, al(j, 256), :] = tmm(act[:, al(sh * ft + j, 256)], cot[...])

        loop(ft, one)

    dwdn(1 - c)
    ex = rcopy(dwd.at[1 - c], d_sib, ssd.at[0], rsd.at[0], ln.sib)
    ex.start()
    g_n.tick(4)
    dwdn(c)
    put(dwd.at[c], d_own)
    g_u.finish()
    g_n.wait_sib()
    g_n.finish()
    g_u.drain()
    g_n.drain()
    ex.wait()
    for cp in outs[1:]:
        cp.wait()


V = pl.BlockSpec(memory_space=pltpu.VMEM)
ANY = pl.BlockSpec(memory_space=pl.ANY)
SM = pl.BlockSpec(memory_space=pltpu.SMEM)


def forward_call(dm, n_dp, small, big):
    M, D, f = dm.rows, dm.d, dm.f
    sds, vm, dma = jax.ShapeDtypeStruct, pltpu.VMEM, pltpu.SemaphoreType.DMA
    row = sds((M, D), bf16)
    wide = sds((M, 2 * f), bf16)
    sq = sds((D, f), f32)
    outs = [sds((dm.n_t, D + dm.hw, f), f32), sds((dm.n_t, f, D), f32), sds((f, D), f32), sds((dm.ns * dm.pairs, 2, dm.r, dm.r), bf16), sds((3 * D, D), bf16), sds((D, D), bf16), sds((dm.n_t, 16, D), f32)]
    outs += [row] * 6 + [sds((dm.ns, D, dm.r), bf16), row, wide, wide, sds((M, D), f32), sds((f, D), f32), sds((f, D), f32)]
    scratch = [vm((dm.length, 2 * dm.ns, D), bf16)] * 2 + [vm((M, D), bf16)] * 2 + [vm((3 * D, D), bf16), vm((D, D), bf16), vm((2, D, f), bf16)]
    scratch += [vm((M, D), bf16)] * 4 + [vm((dm.ns, D, dm.r), bf16), vm((M, D), bf16), vm((M, 2 * f), bf16), vm((M, 2 * f), bf16), vm((M, D), f32), vm((2, f, D), f32)]
    scratch += [vm((2, 2, dm.r, dm.r), bf16), vm((4, dm.hw, D), f32), vm((dm.n_t, 16, D), f32), vm((8, D), f32), vm((dm.n_t, 16 + 3 * dm.hw, D), f32), vm((dm.hw + D, D), f32)]
    scratch += [dma((2,)), dma((4,)), dma((2,)), dma((20,)), *([dma((GATHER_SEMS,))] * 6), dma((1,)), dma((1,))]

    def kern(*refs):
        forward_kernel(dm, n_dp, *refs)

    return pl.pallas_call(
        kern,
        out_shape=outs,
        in_specs=[SM] + [V] * (len(small) - 1) + [ANY] * len(big),
        out_specs=[ANY] * len(outs),
        scratch_shapes=scratch,
        compiler_params=pltpu.CompilerParams(vmem_limit_bytes=VMEM_LIMIT, collective_id=1, has_side_effects=True),
        name="forward",
    )(*small, *big)


class Reduce:
    KINDS = 7

    @staticmethod
    def scratch(n_arrays, n_sub, rows, width):
        pr, nq = rows // 4 // n_sub, n_arrays * n_sub
        vm, dma = pltpu.VMEM, pltpu.SemaphoreType.DMA
        return [vm((2, 2, 4 * pr, width), f32), vm((2, 7 * pr, width), f32), vm((nq, 5 * pr, width), f32), dma((2, 3, 2)), dma((2, 2)), dma((2, 11)), dma((nq, Reduce.KINDS))]

    def __init__(self, ln, head, own, sib, fin, first, n_arrays, n_sub, vin, vout, land, lsem, fsem, ssem, rsem):
        self.ln, self.head, self.own, self.sibling, self.fin, self.first = ln, head, own, sib, fin, first
        self.vin, self.vout, self.land, self.lsem, self.fsem, self.ssem, self.rsem = vin, vout, land, lsem, fsem, ssem, rsem
        self.n_sub, self.total = n_sub, n_sub * n_arrays
        self.pr = own.shape[1] // 4 // n_sub
        L, z, x = ln.length, ln.z, ln.x
        self.L = L
        self.waves = self.total + 2 * L - 1
        up = 2 * x - 1
        self.k = ((1 - x) * (L - 1 - z) + x * z, x * (L - 1 - z) + (1 - x) * z)
        self.up = ((2 * (z + up) + x, ln.t), (2 * (z - up) + x, ln.t))
        self.down = (self.up[1], self.up[0])
        self.partner = (2 * z + 1 - x, ln.t)
        self.parts = ((2 * x, 2), (2 * (1 - x) + 1, 1), (2 * (1 - x), 1))

    def rows(self, q, job, part=0, n=None):
        first, count = self.parts[job]
        r0 = lax.rem(q, self.n_sub) * 4 + first + part
        return pl.ds(pl.multiple_of(r0 * self.pr, 8), (n or count) * self.pr)

    def view(self, ref, q, job, part=0, n=None):
        return ref.at[self.first + q // self.n_sub, self.rows(q, job, part, n)]

    def box(self, q, part, n=1):
        return self.land.at[q, pl.ds(part * self.pr, n * self.pr)]

    def landed(self, view, q, kind):
        rcopy(view, view, self.ssem.at[0, 0], self.rsem.at[q, kind], self.ln.sib).wait_recv()

    def ok(self, q):
        return (q >= 0) & (q < self.total)

    def slabs(self, tau):
        return (tau - 1 - self.k[0], tau - 1 - self.k[1], tau)

    def loads(self, tau, job, views):
        par = lax.rem(tau, 2)
        n = self.parts[job][1] * self.pr
        at = pl.ds((0, 2, 3)[job] * self.pr, n)
        return [pltpu.make_async_copy(v, self.vin.at[par, i, at], self.lsem.at[par, job, i]) for i, v in enumerate(views)]

    def prefetch(self, tau):
        for job, q in enumerate(self.slabs(tau)):

            def start(refs):
                for cp in self.loads(tau, job, refs):
                    cp.start()

            @pl.when(self.ok(q))
            def _():
                pair = [self.view(r, q, job) for r in (self.own, self.sibling)]
                if self.head is None:
                    start(pair)
                    return
                pl.when(q < self.n_sub)(lambda: start([r.at[self.rows(q, job)] for r in self.head]))
                pl.when(q >= self.n_sub)(lambda: start(pair))

    def send(self, src, dst, slot, k, q, kind, dev):
        return rcopy(src, dst, self.ssem.at[slot, k], self.rsem.at[q, kind], dev)

    def wave(self, tau, start=True):
        L, pr = self.L, self.pr
        slot = lax.rem(tau, 2)
        q_both, q_one, q_leaf = self.slabs(tau)

        def run(*cps):
            for cp in cps:
                cp.start() if start else cp.wait_send()

        def out(part, n=1):
            return self.vout.at[slot, pl.ds(part * pr, n * pr)]

        def summed(job, q):
            for cp in self.loads(tau, job, [self.view(r, q, job) for r in (self.own, self.sibling)]):
                cp.wait()
            a = (0, 2, 3)[job] * pr
            n = self.parts[job][1] * pr
            return self.vin[slot, 0, a : a + n] + self.vin[slot, 1, a : a + n]

        @pl.when(self.ok(q_leaf))
        def _():
            o = out(3)
            if start:
                o[...] = summed(2, q_leaf)
            run(self.send(o, self.box(q_leaf, 3), slot, 0, q_leaf, 0, self.partner))

        for i in range(2):
            k = self.k[i]
            r = L - 1 - k
            q = tau - L - r

            @pl.when(self.ok(q) & (r > 0))
            def _():
                fv = self.view(self.fin, q, i)
                if start:
                    self.landed(fv, q, 4 if i == 0 else 6)

                @pl.when(k > 0)
                def _():
                    run(self.send(fv, fv, slot, 8 if i == 0 else 10, q, 4 if i == 0 else 6, self.down[i]))

                if i == 0:
                    fx = self.view(self.fin, q, 0, 0, 1)
                    run(self.send(fx, fx, slot, 9, q, 5, self.partner))

        for i, q in ((0, q_both), (1, q_one)):
            k = self.k[i]
            n, part = (2, 0) if i == 0 else (1, 2)

            @pl.when(self.ok(q))
            def _():
                o = out(part, n)
                if start:
                    v = summed(i, q)
                    if i == 0:
                        self.landed(self.box(q, 3), q, 0)
                        o[0:pr] = v[0:pr] + self.land[q, 3 * pr : 4 * pr]
                        o[pr : 2 * pr] = v[pr : 2 * pr]
                    else:
                        o[...] = v

                    @pl.when(k > 0)
                    def _():
                        self.landed(self.box(q, part, n), q, 1 + i)
                        o[...] += self.land[q, part * pr : (part + n) * pr]

                @pl.when(k < L - 1)
                def _():
                    run(self.send(o, self.box(q, part, n), slot, 1 if i == 0 else 5, q, 1 + i, self.up[i]))

                @pl.when(k == L - 1)
                def _():
                    z = out(part + n - 1)
                    tot = out(4 + 2 * i, n)
                    run(self.send(z, self.box(q, 4), slot, 4 if i == 0 else 6, q, 3, self.partner))
                    if start:
                        if i == 0:
                            tot[0:pr] = o[0:pr]
                        self.landed(self.box(q, 4), q, 3)
                        tot[(n - 1) * pr : n * pr] = z[...] + self.land[q, 4 * pr : 5 * pr]
                    fv = self.view(self.fin, q, i)
                    run(self.send(tot, fv, slot, 2 if i == 0 else 7, q, 4 if i == 0 else 6, self.down[i]))
                    if i == 0:
                        run(self.send(out(4), self.view(self.fin, q, 0, 0, 1), slot, 3, q, 5, self.partner))
                    cp = pltpu.make_async_copy(tot, fv, self.fsem.at[i, slot])
                    cp.start() if start else cp.wait()

    def step(self, tau):
        self.wave(tau - 2, start=False)
        self.wave(tau)

    def steps(self, t0, t1):
        def body(tau, carry):
            self.prefetch(tau + 1)
            self.step(tau)
            return carry

        lax.fori_loop(t0, t1, body, 0)

    def finish(self):
        self.wave(self.waves - 2, start=False)
        self.wave(self.waves - 1, start=False)

        def body(q, carry):
            self.landed(self.view(self.fin, q, 2), q, 5)
            return carry

        lax.fori_loop(0, self.total, body, 0)


N_SUB = (4, 4)


def backward_kernel(dm, n_dp, *refs):
    (meta, g1_r, g2_r, bd_r, wdn_s, gn_h, gu, p_hbm, i_wqkv, i_wo, i_bias, i_tok, i_cot, i_normed, i_q8, i_kk, i_vv, i_mixt, i_n2, i_act, i_gp, i_mid, d_own, d_sib, wup_s) = refs[:25]
    (fin, sm_out, lo32, gt32, own, sibl, sland) = refs[25:32]
    (wqkv, wo, wup, wdn, cot, mixt, n2, gp, act, mid, gn, dwa, acc, pbuf, tmp, bbuf, small) = refs[32:49]
    psem, tsem, lsem, osem, xss, xrs, sss, srs = refs[49:57]
    red_a, red_b = refs[57:64], refs[64:71]
    R, D, NS, hw, f = dm.r, dm.d, dm.ns, dm.hw, dm.f
    ln = Links(n_dp)
    y, c, t = ln.y, ln.c, ln.t
    base = c * NS
    nt, ft = D // 256, f // 256

    srcs = (i_gp, i_n2, i_cot, wdn_s, i_act, i_bias, i_mid, wup_s, i_wqkv, i_wo, i_mixt)
    dsts = (gp.at[:, pl.ds(0, 2 * f)], n2, cot, wdn.at[al(t, f)], act, bbuf, mid, wup.at[t], wqkv, wo, mixt)
    ins = [pltpu.make_async_copy(a, b, lsem.at[i]) for i, (a, b) in enumerate(zip(srcs, dsts))]
    late = [pltpu.make_async_copy(a, gp.at[:, pl.ds(i * D, D)], lsem.at[11 + i]) for i, a in enumerate((i_q8, i_kk, i_vv, i_normed))]
    late.append(pltpu.make_async_copy(i_tok, n2, lsem.at[15]))
    for cp in ins:
        cp.start()
    bar = pltpu.get_barrier_semaphore()
    group = ln.dp - lax.rem(ln.dp, n_dp)
    for dev in (ln.ypart, ln.sib):
        pl.semaphore_signal(bar, inc=1, device_id=dev, device_id_type=MESH)

    def greet(i, carry):
        pl.semaphore_signal(bar, inc=1, device_id=(lax.rem(ln.dp + i, n_dp), t), device_id_type=MESH)
        return carry

    lax.fori_loop(1, n_dp, greet, 0)
    pl.semaphore_wait(bar, 2 + n_dp - 1)
    red = Reduce(ln, (d_own, d_sib), own, sibl, fin, 0, 2, N_SUB[0], *red_a)
    last = Reduce(ln, None, own, sibl, fin, 2, 1, N_SUB[1], *red_b)
    def narrow(src, put):
        n = src.shape[0] // 256
        cps = [pltpu.make_async_copy(src.at[pl.ds(i * 256, 256)], tmp.at[i % 2], tsem.at[i % 2]) for i in range(n)]
        for cp in cps[:2]:
            cp.start()
        for i, cp in enumerate(cps):
            cp.wait()
            put(i * 256, 256, tmp[i % 2].astype(bf16))
            if i + 2 < n:
                cps[i + 2].start()

    def put_dn(ts, r0=0):
        def put(r, n, v):
            wdn[pl.ds(pl.multiple_of(ts * f + r0 + r, 16), n), :] = v

        return put

    def put_up(ts):
        def put(r, n, v):
            wup[ts, r : r + n, :] = v

        return put

    red.prefetch(0)
    red.step(0)
    red.prefetch(1)
    narrow(gn_h.at[ln.t_sib], put_dn(ln.t_sib))
    for cp in ins[:4]:
        cp.wait()
    acc[...] = jnp.zeros_like(acc)

    def unit(j):
        half = j // (2 * ft)
        hf = jnp.where(half == 0, y, 1 - y)
        return 2 * hf + lax.rem(j, 2 * ft) // ft, lax.rem(j, ft)

    def grad_hidden(n, block):
        def one(i):
            s, j = i // n, block(lax.rem(i, n))
            sh, k = unit(j)
            rs, cs = al(s, R), al(j, 256)
            ga = mmt(cot[rs, :], wdn[pl.ds(pl.multiple_of(sh * f + k * 256, 256), 256), :])
            gp[rs, cs] = (ga * gp[rs, cs].astype(f32)).astype(bf16)

        loop(NS * n, one)

    grad_hidden(2 * ft, lambda j: j)
    red.step(1)
    red.prefetch(2)

    def dwup(i):
        sh, j = i // nt, lax.rem(i, nt)
        for n in range(ft):
            dwa[pl.ds(pl.multiple_of(i * 256, 256), 256), n * 256 : n * 256 + 256] = tmm(n2[:, al(j, 256)], gp[:, al(sh * ft + n, 256)])

    loop(2 * nt, dwup)
    up_own = pltpu.make_async_copy(dwa.at[al(c, D)], own.at[1], osem.at[2])
    up_own.start()
    up_sib = rcopy(dwa.at[al(1 - c, D)], sibl.at[1], xss.at[0], xrs.at[0], ln.sib)
    up_sib.start()
    red.step(2)
    red.prefetch(3)
    ones = jnp.ones((8, dm.rows), bf16)
    for sh in range(2):
        acc[6 + sh, :, :f] = mm(ones, gp[:, sh * f : (sh + 1) * f]) * 0.125

    bd = bd_r[...].reshape(1, D)
    for cp in ins[4:]:
        cp.wait()

    def lo_own(s):
        rs = al(s, R)
        gn[rs, :] = mid[rs, :] + bd + mm(act[rs, :], wdn[al(y, 2 * f), :])

    loop(NS, lo_own)
    narrow(gu.at[ln.t_y, pl.ds(hw, D)], put_up(ln.t_y))
    narrow(gu.at[ln.t_ysib, pl.ds(hw, D)], put_up(ln.t_ysib))
    red.step(3)
    up_own.wait()
    up_sib.wait()
    red.prefetch(4)

    def mlp(i):
        pl.when(i == NS * ft)(lambda: red.steps(4, 5))
        s, j = i // (2 * ft), lax.rem(i, 2 * ft)
        sh, k = unit(2 * ft + j)
        rs, cs = al(s, R), al(k, 256)
        h = mm(n2[rs, :], wup[sh, :, cs]) + bbuf[sh, 0:1, cs]
        a, g = gelu_pair(h)
        act[rs, al(j, 256)] = a.astype(bf16)
        gp[rs, al(2 * ft + j, 256)] = g.astype(bf16)

    loop(NS * 2 * ft, mlp)
    narrow(gn_h.at[ln.t_y], put_dn(ln.t_y))
    red.steps(5, 6)
    narrow(gn_h.at[ln.t_ysib], put_dn(ln.t_ysib))
    narrow(gu.at[ln.t_sib, pl.ds(hw, D)], put_up(ln.t_sib))
    grad_hidden(2 * ft, lambda j: 2 * ft + j)
    red.steps(6, 7)

    def gnorm2(s):
        rs = al(s, R)
        tot = None
        for half in range(2):
            for i in range(2):
                sh = 2 * (y if half == 0 else 1 - y) + i
                k = half * 2 + i
                p = mmt(gp[rs, k * f : (k + 1) * f], wup[sh])
                tot = p if tot is None else tot + p
        lo = gn[rs, :] + mm(act[rs, :], wdn[al(1 - y, 2 * f), :])
        dwa[rs, :] = lo
        gn[rs, :] = tot

    loop(NS, gnorm2)
    lo_copies = []
    for s in range(NS):
        v = dwa.at[pl.ds(s * R, R)]
        lo_copies.append((pltpu.make_async_copy(v, lo32.at[base + s], osem.at[3 + s]), rcopy(v, lo32.at[base + s], xss.at[1 + s], xrs.at[1 + s], ln.sib)))
        for cp in lo_copies[-1]:
            cp.start()
    for cp in late:
        cp.start()
    q8, kk, vv, normed = (gp.at[:, pl.ds(i * D, D)] for i in range(4))
    tok = n2
    red.steps(7, 8)
    g2 = g2_r[...].reshape(1, D)
    g1 = g1_r[...].reshape(1, D)

    def ln2b(i):
        rs = pl.ds(pl.multiple_of(i * CH, CH), CH)
        xh, r = centred(mid[rs, :])
        go = gn[rs, :]
        co = cot[rs, :].astype(f32)
        g = go * g2
        gx = g * xh
        gm = co + r * (g - jnp.sum(g, -1, keepdims=True) * (1.0 / D) - xh * (jnp.sum(gx, -1, keepdims=True) * (1.0 / D)))
        mid[rs, :] = gm
        gl = gm.astype(bf16)
        act[rs, 0:D] = gl
        acc[0] += fold8(co)
        acc[1] += fold8(gl.astype(f32))
        acc[4] += fold8(go * xh)
        acc[5] += fold8(go)

    loop(dm.rows // CH, ln2b)

    def gmixf(s):
        rs = al(s, R)
        act[rs, D : 2 * D] = mmt(act[rs, 0:D], wo[...]).astype(bf16)

    loop(NS, gmixf)
    own_h = al(y, 2 * hw)

    def over_samples(fn):
        tot = None
        for s in range(NS):
            p = fn(s)
            tot = p if tot is None else tot + p
        return tot

    for a, b in lo_copies:
        a.wait()
        b.wait()

    for n in range(nt):
        cc = slice(n * 256, n * 256 + 256)
        p = over_samples(lambda s: mm(mixt[s, own_h, :], act[s * R : s * R + R, cc]))
        for sh in range(2):
            dwa[sh * D + 3 * hw : sh * D + 4 * hw, cc] = p[sh * hw : (sh + 1) * hw]
    red.steps(8, 9)
    for cp in late:
        cp.wait()
    lane = lax.broadcasted_iota(jnp.int32, (1, 128), 1)
    masks = (lane < HEAD_DIM, lane >= HEAD_DIM)
    total, hp = NS * dm.pairs, dm.pairs // 2

    def place(i):
        j = lax.rem(i, NS * hp)
        half = i // (NS * hp)
        hf = y + half * (1 - 2 * y)
        return j // hp, hf * hp + lax.rem(j, hp)

    def p_copy(i):
        slot = lax.rem(i, 2)
        s, p = place(i)
        return pltpu.make_async_copy(p_hbm.at[s * dm.pairs + p], pbuf.at[slot], psem.at[slot])

    p_copy(0).start()

    def attn(i):
        s, p = place(i)
        slot = lax.rem(i, 2)
        rs, cs = al(s, R), al(p, 128)

        @pl.when(i + 1 < total)
        def _():
            p_copy(i + 1).start()

        p_copy(i).wait()
        q, k, v, do = q8[rs, cs], kk[rs, cs], vv[rs, cs], act[rs, pl.ds(pl.multiple_of(D + p * 128, 128), 128)]
        dv, dk = [], []
        for h in range(2):
            pt = pbuf[slot, h]
            pf = pt.astype(f32)
            dp = mmt(jnp.where(masks[h], v, jnp.bfloat16(0)), do)
            dsum = jnp.sum(pf * dp, 0, keepdims=True)
            ds = (pf * (dp - dsum)).astype(bf16)
            dv.append(mm(pt, do))
            dk.append(mm(ds, q))
            o = tmm(k, ds)
            hr = pl.ds(pl.multiple_of(p * 128 + h * HEAD_DIM, HEAD_DIM), HEAD_DIM)
            mixt[s, hr, :] = (o[h * HEAD_DIM : (h + 1) * HEAD_DIM] * 0.125).astype(bf16)
        kk[rs, cs] = jnp.where(masks[0], dk[0], dk[1]).astype(bf16)
        vv[rs, cs] = jnp.where(masks[0], dv[0], dv[1]).astype(bf16)

    def attend(i0, i1, between):
        def one(i, carry):
            attn(i)
            for k, fn in between:
                pl.when(i == k)(fn)
            return carry

        lax.fori_loop(i0, i1, one, 0)

    half = NS * hp
    attend(0, half, [(half // 3, lambda: red.steps(9, 10)), (half * 2 // 3, lambda: red.steps(10, 11))])
    for n in range(nt):
        cc = slice(n * 256, n * 256 + 256)
        p = over_samples(lambda s: mm(mixt[s, own_h, :], normed[s * R : s * R + R, cc]))
        tk = tmm(kk[:, own_h], normed[:, cc])
        tv = tmm(vv[:, own_h], normed[:, cc])
        for sh in range(2):
            h = slice(sh * hw, (sh + 1) * hw)
            dwa[sh * D : sh * D + hw, cc] = p[h]
            dwa[sh * D + hw : sh * D + 2 * hw, cc] = tk[h]
            dwa[sh * D + 2 * hw : sh * D + 3 * hw, cc] = tv[h]
    a_own = pltpu.make_async_copy(dwa.at[al(c, D)], own.at[2], osem.at[2])
    a_own.start()
    a_sib = rcopy(dwa.at[al(1 - c, D)], sibl.at[2], xss.at[5], xrs.at[5], ln.sib)
    a_sib.start()
    onesr = jnp.ones((8, R), bf16)
    acc[8, :, 0 : 2 * hw] = over_samples(lambda s: mmt(onesr, mixt[s, own_h, :])) * 0.125
    acc[9, :, 0 : 2 * hw] = mm(ones, vv[:, own_h]) * 0.125
    red.steps(11, 12)
    a_own.wait()
    a_sib.wait()
    last.prefetch(0)
    attend(
        half,
        total,
        [
            (half + 1, lambda: last.steps(0, 1)),
            (half * 4 // 3, lambda: red.steps(12, red.waves - 1)),
            (half * 5 // 3, lambda: last.steps(1, 2)),
        ],
    )
    red.steps(red.waves - 1, red.waves)
    red.finish()
    last.steps(2, 3)

    def gnorm1(s):
        rs = al(s, R)
        gn[rs, :] = tmm(mixt[s], wqkv[0:D, :]) + mm(kk[rs, :], wqkv[D : 2 * D, :]) + mm(vv[rs, :], wqkv[2 * D : 3 * D, :])

    loop(NS, gnorm1)
    last.steps(3, 4)

    def ln1b(s):
        for r0, n in row_chunks(dm):
            rs = pl.ds(pl.multiple_of(s * R + r0, 16), n)
            x = tok[rs, :].astype(f32)
            keep = keep_of(meta, base, s, r0, n) if r0 == 0 else None
            xh, r = centred(x if keep is None else x * keep)
            go = gn[rs, :]
            g = go * g1
            gx = g * xh
            gi = r * (g - jnp.sum(g, -1, keepdims=True) * (1.0 / D) - xh * (jnp.sum(gx, -1, keepdims=True) * (1.0 / D)))
            o = mid[rs, :] + gi
            mid[rs, :] = o if keep is None else o * keep
            acc[2] += fold8(go * xh)
            acc[3] += fold8(go)

    loop(NS, ln1b)
    gt_copies = []
    for s in range(NS):
        v = mid.at[pl.ds(s * R, R)]
        gt_copies.append((pltpu.make_async_copy(v, gt32.at[base + s], osem.at[3 + s]), rcopy(v, gt32.at[base + s], xss.at[6 + s], xrs.at[6 + s], ln.sib)))
        for cp in gt_copies[-1]:
            cp.start()

    tot = jnp.sum(acc[...], 1)
    for sh in range(2):
        small[sh, 0:6, :] = tot[0:6]
        small[sh, 6:7, :] = tot[6 + sh : 7 + sh]
        small[sh, 7:8, 0:hw] = tot[8:9, sh * hw : (sh + 1) * hw]
        small[sh, 7:8, hw : 2 * hw] = tot[9:10, sh * hw : (sh + 1) * hw]
        small[sh, 7:8, 2 * hw :] = jnp.zeros((1, D - 2 * hw), f32)
    cp = rcopy(small.at[1 - c], small.at[2], xss.at[10], xrs.at[10], ln.sib)
    cp.start()
    cp.wait()
    small[2] = small[c] + small[2]
    mine = sland.at[al(ln.dp, 8)]
    kept = pltpu.make_async_copy(small.at[2], mine, osem.at[0])
    kept.start()

    def peer(i):
        d = lax.rem(ln.dp + i, n_dp)
        return rcopy(small.at[2], mine, sss.at[d], srs.at[ln.dp], (d, t))

    def spread(i, carry):
        peer(i).start()
        return carry

    lax.fori_loop(1, n_dp, spread, 0)
    last.steps(4, last.waves)
    last.finish()

    def gathered(i, carry):
        peer(i).wait_send()
        d = lax.rem(ln.dp + i, n_dp)
        theirs = sland.at[al(d, 8)]
        rcopy(theirs, theirs, sss.at[d], srs.at[d], (d, t)).wait_recv()
        return carry

    lax.fori_loop(1, n_dp, gathered, 0)
    kept.wait()
    back = pltpu.make_async_copy(sland, dwa.at[pl.ds(0, 8 * n_dp)], osem.at[0])
    back.start()
    back.wait()
    sm_out[...] = lax.fori_loop(1, n_dp, lambda i, v: v + dwa[al(i, 8), :], dwa[0:8, :])
    for a, b in gt_copies:
        a.wait()
        b.wait()


def backward_call(dm, n_dp, small, big):
    M, D, f = dm.rows, dm.d, dm.f
    sds, vm, dma = jax.ShapeDtypeStruct, pltpu.VMEM, pltpu.SemaphoreType.DMA
    st = sds((3, D, D), f32)
    outs = [st, sds((8, D), f32), sds((dm.samples, dm.r, D), f32), sds((dm.samples, dm.r, D), f32), st, st, sds((8 * n_dp, D), f32)]
    row, wide = vm((M, D), bf16), vm((M, 2 * f), bf16)
    scratch = [vm((3 * D, D), bf16), vm((D, D), bf16), vm((dm.n_t, D, f), bf16), vm((dm.ff, D), bf16), row]
    scratch += [vm((dm.ns, D, dm.r), bf16), row, vm((M, dm.ff), bf16), wide, vm((M, D), f32), vm((M, D), f32), vm((2 * D, D), f32), vm((10, 8, D), f32)]
    scratch += [vm((2, 2, dm.r, dm.r), bf16), vm((2, 256, D), f32), vm((dm.n_t, 16, D), f32), vm((3, 8, D), f32)]
    scratch += [dma((2,)), dma((2,)), dma((16,)), dma((7,)), dma((11,)), dma((11,)), dma((n_dp,)), dma((n_dp,))]
    scratch += Reduce.scratch(2, N_SUB[0], D, D) + Reduce.scratch(1, N_SUB[1], D, D)

    def kern(*refs):
        backward_kernel(dm, n_dp, *refs)

    return pl.pallas_call(
        kern,
        out_shape=outs,
        in_specs=[SM] + [V] * (len(small) - 1) + [ANY] * len(big),
        out_specs=[ANY, V] + [ANY] * 5,
        scratch_shapes=scratch,
        compiler_params=pltpu.CompilerParams(vmem_limit_bytes=VMEM_LIMIT, collective_id=2, has_side_effects=True),
        name="backward",
    )(*small, *big)


def shards(tokens, metadata, cotangent, w_query, w_key, w_value, w_out, b_query, b_value, b_out, w_up, b_up, w_down, b_down, gain_one, shift_one, gain_two, shift_two, n_dp, n_t):
    dm = Dims(tokens, w_up, n_t)
    D, hw, f = dm.d, dm.hw, dm.f
    small = (metadata, w_query.T, w_key.T, w_value.T, w_out, w_up, w_down, b_up, b_query, b_value, gain_one, shift_one, gain_two, shift_two, b_out)
    (gu, gnw, _, p, wqkv, wo, bb, tok, cot, normed, q8, kk, vv, mixt, n2, act, gp, mid, d_own, d_sib) = forward_call(dm, n_dp, small, (tokens.transpose(1, 0, 2), cotangent.transpose(1, 0, 2)))
    small = (metadata, gain_one, gain_two, b_down)
    fin, sm, lo, gt, *_ = backward_call(dm, n_dp, small, (w_down, gnw, gu, p, wqkv, wo, bb, tok, cot, normed, q8, kk, vv, mixt, n2, act, gp, mid, d_own, d_sib, w_up))
    a_ = fin[2]
    return (
        lo[:, : dm.length].astype(bf16),
        gt[:, : dm.length],
        a_[0:hw].T,
        a_[hw : 2 * hw].T,
        a_[2 * hw : 3 * hw].T,
        a_[3 * hw : 4 * hw],
        sm[7, :hw],
        sm[7, hw : 2 * hw],
        sm[1],
        fin[1],
        sm[6],
        fin[0],
        sm[0],
        sm[2],
        sm[3],
        sm[4],
        sm[5],
    )


def solution(mesh):
    n_dp, n_t = mesh.shape["dp"], mesh.shape["tensor"]
    rows, cols, vec, rep = P("dp", None, None), P(None, "tensor"), P("tensor"), P()
    srow = P("tensor", None)

    def run(*args):
        return shards(*args, n_dp=n_dp, n_t=n_t)

    return jax.shard_map(
        run,
        mesh=mesh,
        in_specs=(rows, P("dp"), rows, cols, cols, cols, srow, vec, vec, rep, cols, vec, srow, rep, rep, rep, rep, rep),
        out_specs=(rows, rows, cols, cols, cols, srow, vec, vec, rep, cols, vec, srow, rep, rep, rep, rep, rep),
        check_vma=False,
    )
```

time: 555 us -> 365 us (0.66)
  Pallas kernels: 520 us -> 345 us
  local copies, waits for them, and re-layouts: 31.5 us -> 17.8 us
    pallas_call x1, Pallas kernels: 416 us -> 247 us  [backward_call(): pl.pallas_call(kern, out_shape=outs, in_specs=[SM] + [V] * (len(small) -...]
    unnamed x17 -> x10, local copies, waits for them, and re-layouts: 20.8 us -> 8.48 us
    pallas_call x1, Pallas kernels: 104 us -> 98 us  [forward_call(): pl.pallas_call(kern, out_shape=outs, in_specs=[SM] + [V] * (len(small) -...]
where the time goes in v3:
time: 365 us; the launch traced here: 364 us
  Pallas kernels  345 us (95%)
  local copies, waits for them, and re-layouts  17.8 us (5%)
    pallas_call x1, Pallas kernels, backward_call(): pl.pallas_call(kern, out_shape=outs, in_specs=[SM] + [V] * (len(small) -...  247 us
    pallas_call x1, Pallas kernels, forward_call(): pl.pallas_call(kern, out_shape=outs, in_specs=[SM] + [V] * (len(small) -...  98 us
    unnamed x10, local copies, waits for them, and re-layouts  8.48 us

profile of v3, /device:TPU:0, one launch (start us, length us, event | category | flops | bytes accessed | tf_op | source)
XLA Modules:
  0.0 363.9 jit_solution(4228184388091544957)
XLA Ops:
  0.7 98.0 %forward.1 = (f32[4,960,768]{2,1,0:T(8,128)}, f32[4,768,768]{2,1,0:T(8,128)}, f32[768,768]{1,0:T(8,128)}, bf16[24,2,272,272]{3,2,1,0:T(8,128)(2,1)}, bf16[2304,7...) custom-call(s32[8]{0:T(128)} %refs_0_.3, ...), custom_call_target="tpu_custom_call" | custom-call | tf_op jit(solution)/shard_map/forward/pallas_call | solution.py:543
  98.6 247.4 %backward.1 = (f32[3,768,768]{2,1,0:T(8,128)}, f32[8,768]{1,0:T(8,128)}, f32[8,272,768]{2,1,0:T(8,128)}, f32[8,272,768]{2,1,0:T(8,128)}, f32[3,768,768]{2,1,0:T(...) custom-call(s32[8]{0:T(128)} %refs_0_.3, f32[768]{0:T(1024)} %refs_1_.1, f32[768]{0:T(1024)} %refs_2_.1, f32[768]{0:T(1024)} %refs_3_.1, ...), custom_call_target="tpu_custom_call" | custom-call | tf_op jit(solution)/shard_map/backward/pallas_call | solution.py:1118
  346.1 0.0 copy-start
  346.1 3.3 slice.105
  349.4 0.0 copy-start.1
  349.4 2.3 copy.35
  351.7 0.0 copy-done.1
  351.7 0.6 fusion
  352.3 0.7 slice_reduce_fusion
  353.0 0.0 copy-done
  353.0 0.0 slice-start
  353.0 1.4 slice_bitcast_fusion.2
  354.4 0.0 slice-start.1
  354.4 2.7 slice_bitcast_fusion
  357.1 0.0 slice-done
  357.1 1.5 slice-done.1
  358.7 0.6 slice.70
  359.2 4.7 %copy.36 = f32[8,258,768]{2,0,1:T(8,128)} copy(f32[8,258,768]{2,1,0:T(8,128)S(1)} %slice.70) | data formatting | bytes 12681216
  (1 shorter events, 0.0 us)
Async XLA Ops:
  346.1 6.9 %copy-start = (f32[3,768,768]{2,1,0:T(8,128)S(1)}, f32[3,768,768]{2,1,0:T(8,128)}, u32[]{:S(2)}) copy-start(f32[3,768,768]{2,1,0:T(8,128)} %get-tuple-element.61) | copy-start | bytes 21233668
  349.4 2.3 copy-start.1
  353.0 4.2 %slice-start = ((s8[6684672]{0:T(1024)(128)(4,1)}), s8[4194304]{0:T(1024)(128)(4,1)S(1)}, s32[]{:S(2)}) async-start(s8[6684672]{0:T(1024)(128)(4,1)} %bitcast.25), calls=%async_computation | async-start | bytes 8388608
  354.4 4.2 %slice-start.1 = ((s8[6684672]{0:T(1024)(128)(4,1)}), s8[2490368]{0:T(1024)(128)(4,1)S(1)}, s32[]{:S(2)}) async-start(s8[6684672]{0:T(1024)(128)(4,1)} %bitcast.25), calls=%async_computation.1 | async-start | bytes 4980736

commit v4 on v3

--- a/solution.py
+++ b/solution.py
@@ -84,6 +84,7 @@
         self.samples, self.length, self.d = tokens.shape
         self.ns = self.samples // 2
         self.r = -(-self.length // 16) * 16
+        self.rp = -(-self.r // 128) * 128
         self.rows = self.ns * self.r
         self.f = w_up.shape[1]
         self.ff = self.f * n_t
@@ -206,8 +207,6 @@
         self.to_sib(-s - 1).start()
         if s < 3:
             self.to_sib(s + 1).start()
-        if i == 4:
-            self.direct_landed()
 
     def direct_landed(self):
         if not self.passed:
@@ -254,9 +253,9 @@
 
 def forward_kernel(dm, n_dp, *refs):
     (meta, wq, wk, wv, wo_s, wup_s, wdn_s, bup_r, bq_r, bv_r, g1_r, s1_r, g2_r, s2_r, bo_r, tokens, cotan) = refs[:17]
-    (gu, gn_h, n32, p_hbm, o_wqkv, o_wo, o_bias, o_tok, o_cot, o_normed, o_q8, o_kk, o_vv, o_mixt, o_n2, o_act, o_gp, o_mid, d_own, d_sib) = refs[17:37]
-    (tok3, cot3, tok, cot, wqkv, wo, wup, normed, q8, kk, vv, mixt, n2, act, gp, mid, dwd, pbuf, tmp, bbuf, bqv, ga, ustage) = refs[37:60]
-    psem, tsem, lsem, osem, ssa, rsa, ssu, rsu, ssn, rsn, ssd, rsd = refs[60:]
+    (gu, gn_h, n32, p_hbm, o_wqkv, o_wo, o_wup, o_bias, o_tok, o_cot, o_normed, o_q8, o_kk, o_vv, o_mixt, o_n2, o_act, o_gp, o_mid, d_own, d_sib) = refs[17:38]
+    (tok3, cot3, tok, cot, wqkv, wo, wup, normed, q8, kk, vv, mixt, n2, act, gp, mid, dwd, pbuf, tmp, bbuf, bqv, ga, ustage) = refs[38:61]
+    psem, tsem, lsem, osem, ssa, rsa, ssu, rsu, ssn, rsn, ssd, rsd = refs[61:]
     R, D, NS, hw, f = dm.r, dm.d, dm.ns, dm.hw, dm.f
     ln = Links(n_dp)
     y, c, t = ln.y, ln.c, ln.t
@@ -287,7 +286,7 @@
     wo[al(t, hw), :] = wo_s[...]
     g_a = Gather(ln, own_a, ga, 16 + hw, ssa, rsa)
     g_u = Gather(ln, ustage, gu, hw + D // 3, ssu, rsu)
-    g_n = Gather(ln, n32, gn_h, D // 3, ssn, rsn)
+    g_n = Gather(ln, n32, gn_h, D // 4, ssn, rsn)
     enter((ln.ypart, ln.sib, ln.ahead, ln.behind))
     g_a.start_y()
     g_a.start_sib()
@@ -412,9 +411,9 @@
                 m = jnp.maximum(jnp.max(sa, 0, keepdims=True), jnp.max(sb, 0, keepdims=True))
                 ea, eb = jnp.exp(sa - m), jnp.exp(sb - m)
                 inv = 1.0 / (jnp.sum(ea, 0, keepdims=True) + jnp.sum(eb, 0, keepdims=True))
-                pbuf[slot, h, :tail, :] = (ea * inv).astype(bf16)
-                pbuf[slot, h, tail:, :] = (eb * inv).astype(bf16)
-                o = tmm(v, pbuf[slot, h])
+                pbuf[slot, h * R : h * R + tail, 0:R] = (ea * inv).astype(bf16)
+                pbuf[slot, h * R + tail : (h + 1) * R, 0:R] = (eb * inv).astype(bf16)
+                o = tmm(v, pbuf[slot, h * R : (h + 1) * R, 0:R])
                 hr = pl.ds(pl.multiple_of(p * 128 + h * HEAD_DIM, HEAD_DIM), HEAD_DIM)
                 mixt[s, hr, :] = o[h * HEAD_DIM : (h + 1) * HEAD_DIM].astype(bf16)
             p_copy(hf, i).start()
@@ -430,6 +429,7 @@
     g_a.tick(1)
     attend(y, [(3, lambda: g_a.tick(2)), (9, lambda: g_a.tick(3))])
     g_a.tick(4)
+    g_a.direct_landed()
     g_a.finish()
     take_a(ln.t_y)
     take_a(ln.t_ysib)
@@ -440,8 +440,13 @@
     put(q8, o_q8)
     put(kk, o_kk)
     put(vv, o_vv)
-    attend(1 - y, [(2, lambda: g_u.tick(1)), (9, lambda: g_u.tick(2))])
-    g_u.tick(3)
+    g_n.tick(0)
+
+    def both(i):
+        g_u.tick(i)
+        g_n.tick(i)
+
+    attend(1 - y, [(2, lambda: both(1)), (10, lambda: both(2))])
     put(mixt, o_mixt)
     g_a.drain()
     g_u.direct_landed()
@@ -473,27 +478,28 @@
             xh, _ = centred(m)
             n2[rs, :] = (xh * g2 + s2).astype(bf16)
 
-    g_u.tick(4)
-    g_n.tick(0)
+    both(3)
     loop(NS, ln2)
     put(mid, o_mid)
     put(n2, o_n2)
     for i in range(4):
         ups[i].wait()
         wup[1 - c, i * hw : (i + 1) * hw, :] = tmp[i].astype(bf16)
+    put(wup, o_wup)
     ft = f // 256
+    tw = 384 if f % 384 == 0 else 256
+    mt = f // tw
 
     def mlp(i):
-        for k, n in ((7, 1), (14, 2), (21, 3)):
-            pl.when(i == k)(lambda: g_n.tick(n))
-        s, j = i // (2 * ft), lax.rem(i, 2 * ft)
-        rs, sh, cs = al(s, R), j // ft, al(lax.rem(j, ft), 256)
+        pl.when(i == NS * 2)(lambda: both(4))
+        s, j = i // (2 * mt), lax.rem(i, 2 * mt)
+        rs, sh, cs = al(s, R), j // mt, al(lax.rem(j, mt), tw)
         h = mm(n2[rs, :], wup[sh, :, cs]) + bbuf[2 * y + sh, 0:1, cs]
         a, g = gelu_pair(h)
-        act[rs, al(j, 256)] = a.astype(bf16)
-        gp[rs, al(j, 256)] = g.astype(bf16)
-
-    loop(NS * 2 * ft, mlp)
+        act[rs, al(j, tw)] = a.astype(bf16)
+        gp[rs, al(j, tw)] = g.astype(bf16)
+
+    loop(NS * 2 * mt, mlp)
     put(act, o_act)
     put(gp, o_gp)
 
@@ -506,10 +512,10 @@
     dwdn(1 - c)
     ex = rcopy(dwd.at[1 - c], d_sib, ssd.at[0], rsd.at[0], ln.sib)
     ex.start()
-    g_n.tick(4)
     dwdn(c)
     put(dwd.at[c], d_own)
     g_u.finish()
+    g_n.direct_landed()
     g_n.wait_sib()
     g_n.finish()
     g_u.drain()
@@ -530,11 +536,11 @@
     row = sds((M, D), bf16)
     wide = sds((M, 2 * f), bf16)
     sq = sds((D, f), f32)
-    outs = [sds((dm.n_t, D + dm.hw, f), f32), sds((dm.n_t, f, D), f32), sds((f, D), f32), sds((dm.ns * dm.pairs, 2, dm.r, dm.r), bf16), sds((3 * D, D), bf16), sds((D, D), bf16), sds((dm.n_t, 16, D), f32)]
+    outs = [sds((dm.n_t, D + dm.hw, f), f32), sds((dm.n_t, f, D), f32), sds((f, D), f32), sds((dm.ns * dm.pairs, 2 * dm.r, dm.rp), bf16), sds((3 * D, D), bf16), sds((D, D), bf16), sds((2, D, f), bf16), sds((dm.n_t, 16, D), f32)]
     outs += [row] * 6 + [sds((dm.ns, D, dm.r), bf16), row, wide, wide, sds((M, D), f32), sds((f, D), f32), sds((f, D), f32)]
     scratch = [vm((dm.length, 2 * dm.ns, D), bf16)] * 2 + [vm((M, D), bf16)] * 2 + [vm((3 * D, D), bf16), vm((D, D), bf16), vm((2, D, f), bf16)]
     scratch += [vm((M, D), bf16)] * 4 + [vm((dm.ns, D, dm.r), bf16), vm((M, D), bf16), vm((M, 2 * f), bf16), vm((M, 2 * f), bf16), vm((M, D), f32), vm((2, f, D), f32)]
-    scratch += [vm((2, 2, dm.r, dm.r), bf16), vm((4, dm.hw, D), f32), vm((dm.n_t, 16, D), f32), vm((8, D), f32), vm((dm.n_t, 16 + 3 * dm.hw, D), f32), vm((dm.hw + D, D), f32)]
+    scratch += [vm((2, 2 * dm.r, dm.rp), bf16), vm((4, dm.hw, D), f32), vm((dm.n_t, 16, D), f32), vm((8, D), f32), vm((dm.n_t, 16 + 3 * dm.hw, D), f32), vm((dm.hw + D, D), f32)]
     scratch += [dma((2,)), dma((4,)), dma((2,)), dma((20,)), *([dma((GATHER_SEMS,))] * 6), dma((1,)), dma((1,))]
 
     def kern(*refs):
@@ -560,14 +566,14 @@
         vm, dma = pltpu.VMEM, pltpu.SemaphoreType.DMA
         return [vm((2, 2, 4 * pr, width), f32), vm((2, 7 * pr, width), f32), vm((nq, 5 * pr, width), f32), dma((2, 3, 2)), dma((2, 2)), dma((2, 11)), dma((nq, Reduce.KINDS))]
 
-    def __init__(self, ln, head, own, sib, fin, first, n_arrays, n_sub, vin, vout, land, lsem, fsem, ssem, rsem):
-        self.ln, self.head, self.own, self.sibling, self.fin, self.first = ln, head, own, sib, fin, first
+    def __init__(self, ln, head, own, sib, fin, height, n_arrays, n_sub, vin, vout, land, lsem, fsem, ssem, rsem):
+        self.ln, self.head, self.own, self.sibling, self.fin = ln, head, own, sib, fin
         self.vin, self.vout, self.land, self.lsem, self.fsem, self.ssem, self.rsem = vin, vout, land, lsem, fsem, ssem, rsem
         self.n_sub, self.total = n_sub, n_sub * n_arrays
-        self.pr = own.shape[1] // 4 // n_sub
+        self.pr = height // 4 // n_sub
         L, z, x = ln.length, ln.z, ln.x
         self.L = L
-        self.waves = self.total + 2 * L - 1
+        self.waves = self.total + 2 * L
         up = 2 * x - 1
         self.k = ((1 - x) * (L - 1 - z) + x * z, x * (L - 1 - z) + (1 - x) * z)
         self.up = ((2 * (z + up) + x, ln.t), (2 * (z - up) + x, ln.t))
@@ -577,11 +583,10 @@
 
     def rows(self, q, job, part=0, n=None):
         first, count = self.parts[job]
-        r0 = lax.rem(q, self.n_sub) * 4 + first + part
-        return pl.ds(pl.multiple_of(r0 * self.pr, 8), (n or count) * self.pr)
+        return pl.ds(pl.multiple_of((q * 4 + first + part) * self.pr, 8), (n or count) * self.pr)
 
     def view(self, ref, q, job, part=0, n=None):
-        return ref.at[self.first + q // self.n_sub, self.rows(q, job, part, n)]
+        return ref.at[self.rows(q, job, part, n)]
 
     def box(self, q, part, n=1):
         return self.land.at[q, pl.ds(part * self.pr, n * self.pr)]
@@ -646,10 +651,30 @@
                 o[...] = summed(2, q_leaf)
             run(self.send(o, self.box(q_leaf, 3), slot, 0, q_leaf, 0, self.partner))
 
+        q_met = tau - L - 1
+        for i in range(2):
+            n, part = (2, 0) if i == 0 else (1, 2)
+
+            @pl.when(self.ok(q_met) & (self.k[i] == L - 1))
+            def _():
+                tot = out(4 + 2 * i, n)
+                if start:
+                    a = (part + n - 1) * pr
+                    self.landed(self.box(q_met, 4), q_met, 3)
+                    if i == 0:
+                        tot[0:pr] = self.vout[1 - slot, 0:pr]
+                    tot[(n - 1) * pr : n * pr] = self.vout[1 - slot, a : a + pr] + self.land[q_met, 4 * pr : 5 * pr]
+                fv = self.view(self.fin, q_met, i)
+                run(self.send(tot, fv, slot, 2 if i == 0 else 7, q_met, 4 if i == 0 else 6, self.down[i]))
+                if i == 0:
+                    run(self.send(out(4), self.view(self.fin, q_met, 0, 0, 1), slot, 3, q_met, 5, self.partner))
+                cp = pltpu.make_async_copy(tot, fv, self.fsem.at[i, slot])
+                cp.start() if start else cp.wait()
+
         for i in range(2):
             k = self.k[i]
             r = L - 1 - k
-            q = tau - L - r
+            q = tau - L - 1 - r
 
             @pl.when(self.ok(q) & (r > 0))
             def _():
@@ -692,20 +717,7 @@
 
                 @pl.when(k == L - 1)
                 def _():
-                    z = out(part + n - 1)
-                    tot = out(4 + 2 * i, n)
-                    run(self.send(z, self.box(q, 4), slot, 4 if i == 0 else 6, q, 3, self.partner))
-                    if start:
-                        if i == 0:
-                            tot[0:pr] = o[0:pr]
-                        self.landed(self.box(q, 4), q, 3)
-                        tot[(n - 1) * pr : n * pr] = z[...] + self.land[q, 4 * pr : 5 * pr]
-                    fv = self.view(self.fin, q, i)
-                    run(self.send(tot, fv, slot, 2 if i == 0 else 7, q, 4 if i == 0 else 6, self.down[i]))
-                    if i == 0:
-                        run(self.send(out(4), self.view(self.fin, q, 0, 0, 1), slot, 3, q, 5, self.partner))
-                    cp = pltpu.make_async_copy(tot, fv, self.fsem.at[i, slot])
-                    cp.start() if start else cp.wait()
+                    run(self.send(out(part + n - 1), self.box(q, 4), slot, 4 if i == 0 else 6, q, 3, self.partner))
 
     def step(self, tau):
         self.wave(tau - 2, start=False)
@@ -730,23 +742,25 @@
         lax.fori_loop(0, self.total, body, 0)
 
 
-N_SUB = (4, 4)
+N_SUB = 4
+PER = N_SUB // 4
+P_AHEAD = 8
 
 
 def backward_kernel(dm, n_dp, *refs):
-    (meta, g1_r, g2_r, bd_r, wdn_s, gn_h, gu, p_hbm, i_wqkv, i_wo, i_bias, i_tok, i_cot, i_normed, i_q8, i_kk, i_vv, i_mixt, i_n2, i_act, i_gp, i_mid, d_own, d_sib, wup_s) = refs[:25]
+    (meta, g1_r, g2_r, bd_r, wdn_s, gn_h, gu, p_hbm, i_wqkv, i_wo, i_wup, i_bias, i_tok, i_cot, i_normed, i_q8, i_kk, i_vv, i_mixt, i_n2, i_act, i_gp, i_mid, d_own, d_sib) = refs[:25]
     (fin, sm_out, lo32, gt32, own, sibl, sland) = refs[25:32]
-    (wqkv, wo, wup, wdn, cot, mixt, n2, gp, act, mid, gn, dwa, acc, pbuf, tmp, bbuf, small) = refs[32:49]
-    psem, tsem, lsem, osem, xss, xrs, sss, srs = refs[49:57]
-    red_a, red_b = refs[57:64], refs[64:71]
+    (wqkv, wo, wup, wdn, cot, mixt, n2, gp, act, mid, gn, dwa, acc, bbuf, small) = refs[32:47]
+    psem, tsem, lsem, osem, xss, xrs, sss, srs = refs[47:55]
+    red_a = refs[55:62]
     R, D, NS, hw, f = dm.r, dm.d, dm.ns, dm.hw, dm.f
     ln = Links(n_dp)
     y, c, t = ln.y, ln.c, ln.t
     base = c * NS
     nt, ft = D // 256, f // 256
 
-    srcs = (i_gp, i_n2, i_cot, wdn_s, i_act, i_bias, i_mid, wup_s, i_wqkv, i_wo, i_mixt)
-    dsts = (gp.at[:, pl.ds(0, 2 * f)], n2, cot, wdn.at[al(t, f)], act, bbuf, mid, wup.at[t], wqkv, wo, mixt)
+    srcs = (i_gp, i_n2, i_cot, wdn_s, i_act, i_bias, i_mid, i_wup, i_wqkv, i_wo, i_mixt)
+    dsts = (gp.at[:, pl.ds(0, 2 * f)], n2, cot, wdn.at[al(t, f)], act, bbuf, mid, wup.at[pl.ds(2 * y, 2)], wqkv, wo, mixt)
     ins = [pltpu.make_async_copy(a, b, lsem.at[i]) for i, (a, b) in enumerate(zip(srcs, dsts))]
     late = [pltpu.make_async_copy(a, gp.at[:, pl.ds(i * D, D)], lsem.at[11 + i]) for i, a in enumerate((i_q8, i_kk, i_vv, i_normed))]
     late.append(pltpu.make_async_copy(i_tok, n2, lsem.at[15]))
@@ -763,57 +777,43 @@
 
     lax.fori_loop(1, n_dp, greet, 0)
     pl.semaphore_wait(bar, 2 + n_dp - 1)
-    red = Reduce(ln, (d_own, d_sib), own, sibl, fin, 0, 2, N_SUB[0], *red_a)
-    last = Reduce(ln, None, own, sibl, fin, 2, 1, N_SUB[1], *red_b)
-    def narrow(src, put):
-        n = src.shape[0] // 256
-        cps = [pltpu.make_async_copy(src.at[pl.ds(i * 256, 256)], tmp.at[i % 2], tsem.at[i % 2]) for i in range(n)]
-        for cp in cps[:2]:
-            cp.start()
-        for i, cp in enumerate(cps):
-            cp.wait()
-            put(i * 256, 256, tmp[i % 2].astype(bf16))
-            if i + 2 < n:
-                cps[i + 2].start()
-
-    def put_dn(ts, r0=0):
-        def put(r, n, v):
-            wdn[pl.ds(pl.multiple_of(ts * f + r0 + r, 16), n), :] = v
-
-        return put
-
-    def put_up(ts):
-        def put(r, n, v):
-            wup[ts, r : r + n, :] = v
-
-        return put
+    red = Reduce(ln, (d_own, d_sib), own, sibl, fin, D, 3, N_SUB, *red_a)
+    def at(i):
+        red.steps(i * PER, (i + 1) * PER)
+
+    def stage(src, ref, r0, k):
+        return pltpu.make_async_copy(src, ref.at[pl.ds(r0, D)], tsem.at[k])
+
+    staged = [stage(gn_h.at[ln.t_sib], dwa, 0, 0), stage(gu.at[ln.t_y, pl.ds(hw, D)], dwa, D, 1), stage(gu.at[ln.t_ysib, pl.ds(hw, D)], gn, 0, 2)]
+    for cp in staged:
+        cp.start()
+
+    def narrow(cp, ref, r0, dst):
+        cp.wait()
+        for r in range(0, D, 128):
+            dst[r : r + 128, :] = ref[r0 + r : r0 + r + 128, :].astype(bf16)
 
     red.prefetch(0)
-    red.step(0)
-    red.prefetch(1)
-    narrow(gn_h.at[ln.t_sib], put_dn(ln.t_sib))
+    at(0)
+    narrow(staged[0], dwa, 0, wdn.at[al(ln.t_sib, f)])
     for cp in ins[:4]:
         cp.wait()
     acc[...] = jnp.zeros_like(acc)
 
-    def unit(j):
-        half = j // (2 * ft)
-        hf = jnp.where(half == 0, y, 1 - y)
-        return 2 * hf + lax.rem(j, 2 * ft) // ft, lax.rem(j, ft)
-
-    def grad_hidden(n, block):
+    def grad_hidden(half):
         def one(i):
-            s, j = i // n, block(lax.rem(i, n))
-            sh, k = unit(j)
-            rs, cs = al(s, R), al(j, 256)
-            ga = mmt(cot[rs, :], wdn[pl.ds(pl.multiple_of(sh * f + k * 256, 256), 256), :])
+            s, sh = i // 2, lax.rem(i, 2)
+            rs, cs = al(s, R), al(half * 2 + sh, f)
+            hf = y if half == 0 else 1 - y
+            ga = mmt(cot[rs, :], wdn[al(2 * hf + sh, f), :])
             gp[rs, cs] = (ga * gp[rs, cs].astype(f32)).astype(bf16)
 
-        loop(NS * n, one)
-
-    grad_hidden(2 * ft, lambda j: j)
-    red.step(1)
-    red.prefetch(2)
+        loop(NS * 2, one)
+
+    grad_hidden(0)
+    at(1)
+    narrow(staged[1], dwa, D, wup.at[ln.t_y])
+    narrow(staged[2], gn, 0, wup.at[ln.t_ysib])
 
     def dwup(i):
         sh, j = i // nt, lax.rem(i, nt)
@@ -821,12 +821,10 @@
             dwa[pl.ds(pl.multiple_of(i * 256, 256), 256), n * 256 : n * 256 + 256] = tmm(n2[:, al(j, 256)], gp[:, al(sh * ft + n, 256)])
 
     loop(2 * nt, dwup)
-    up_own = pltpu.make_async_copy(dwa.at[al(c, D)], own.at[1], osem.at[2])
+    up_own = pltpu.make_async_copy(dwa.at[al(c, D)], own.at[pl.ds(D, D)], osem.at[2])
     up_own.start()
-    up_sib = rcopy(dwa.at[al(1 - c, D)], sibl.at[1], xss.at[0], xrs.at[0], ln.sib)
+    up_sib = rcopy(dwa.at[al(1 - c, D)], sibl.at[pl.ds(D, D)], xss.at[0], xrs.at[0], ln.sib)
     up_sib.start()
-    red.step(2)
-    red.prefetch(3)
     ones = jnp.ones((8, dm.rows), bf16)
     for sh in range(2):
         acc[6 + sh, :, :f] = mm(ones, gp[:, sh * f : (sh + 1) * f]) * 0.125
@@ -840,30 +838,30 @@
         gn[rs, :] = mid[rs, :] + bd + mm(act[rs, :], wdn[al(y, 2 * f), :])
 
     loop(NS, lo_own)
-    narrow(gu.at[ln.t_y, pl.ds(hw, D)], put_up(ln.t_y))
-    narrow(gu.at[ln.t_ysib, pl.ds(hw, D)], put_up(ln.t_ysib))
-    red.step(3)
+    at(2)
     up_own.wait()
     up_sib.wait()
-    red.prefetch(4)
+    staged = [stage(gn_h.at[ln.t_y], dwa, 0, 0), stage(gn_h.at[ln.t_ysib], dwa, D, 1)]
+    for cp in staged:
+        cp.start()
+    tw = 384 if f % 384 == 0 else 256
+    mt = f // tw
 
     def mlp(i):
-        pl.when(i == NS * ft)(lambda: red.steps(4, 5))
-        s, j = i // (2 * ft), lax.rem(i, 2 * ft)
-        sh, k = unit(2 * ft + j)
-        rs, cs = al(s, R), al(k, 256)
+        pl.when(i == NS * mt)(lambda: at(3))
+        s, j = i // (2 * mt), lax.rem(i, 2 * mt)
+        sh = 2 * (1 - y) + j // mt
+        rs, cs = al(s, R), al(lax.rem(j, mt), tw)
         h = mm(n2[rs, :], wup[sh, :, cs]) + bbuf[sh, 0:1, cs]
         a, g = gelu_pair(h)
-        act[rs, al(j, 256)] = a.astype(bf16)
-        gp[rs, al(2 * ft + j, 256)] = g.astype(bf16)
-
-    loop(NS * 2 * ft, mlp)
-    narrow(gn_h.at[ln.t_y], put_dn(ln.t_y))
-    red.steps(5, 6)
-    narrow(gn_h.at[ln.t_ysib], put_dn(ln.t_ysib))
-    narrow(gu.at[ln.t_sib, pl.ds(hw, D)], put_up(ln.t_sib))
-    grad_hidden(2 * ft, lambda j: 2 * ft + j)
-    red.steps(6, 7)
+        act[rs, al(j, tw)] = a.astype(bf16)
+        gp[rs, al(2 * mt + j, tw)] = g.astype(bf16)
+
+    loop(NS * 2 * mt, mlp)
+    at(4)
+    narrow(staged[0], dwa, 0, wdn.at[al(ln.t_y, f)])
+    narrow(staged[1], dwa, D, wdn.at[al(ln.t_ysib, f)])
+    grad_hidden(1)
 
     def gnorm2(s):
         rs = al(s, R)
@@ -879,6 +877,26 @@
         gn[rs, :] = tot
 
     loop(NS, gnorm2)
+    at(5)
+    total, hp = NS * dm.pairs, dm.pairs // 2
+
+    def place(i):
+        j = lax.rem(i, NS * hp)
+        half = i // (NS * hp)
+        hf = y + half * (1 - 2 * y)
+        return j // hp, hf * hp + lax.rem(j, hp)
+
+    def p_slot(i):
+        k = lax.rem(i, P_AHEAD)
+        return k // 2, pl.ds(pl.multiple_of(lax.rem(k, 2) * dm.rp, 128), dm.rp)
+
+    def p_copy(i):
+        s, p = place(i)
+        k, cs = p_slot(i)
+        return pltpu.make_async_copy(p_hbm.at[s * dm.pairs + p], wup.at[k, pl.ds(0, 2 * R), cs], psem.at[lax.rem(i, P_AHEAD)])
+
+    for i in range(P_AHEAD - 1):
+        p_copy(i).start()
     lo_copies = []
     for s in range(NS):
         v = dwa.at[pl.ds(s * R, R)]
@@ -889,7 +907,6 @@
         cp.start()
     q8, kk, vv, normed = (gp.at[:, pl.ds(i * D, D)] for i in range(4))
     tok = n2
-    red.steps(7, 8)
     g2 = g2_r[...].reshape(1, D)
     g1 = g1_r[...].reshape(1, D)
 
@@ -916,6 +933,7 @@
         act[rs, D : 2 * D] = mmt(act[rs, 0:D], wo[...]).astype(bf16)
 
     loop(NS, gmixf)
+    at(6)
     own_h = al(y, 2 * hw)
 
     def over_samples(fn):
@@ -934,40 +952,24 @@
         p = over_samples(lambda s: mm(mixt[s, own_h, :], act[s * R : s * R + R, cc]))
         for sh in range(2):
             dwa[sh * D + 3 * hw : sh * D + 4 * hw, cc] = p[sh * hw : (sh + 1) * hw]
-    red.steps(8, 9)
     for cp in late:
         cp.wait()
     lane = lax.broadcasted_iota(jnp.int32, (1, 128), 1)
     masks = (lane < HEAD_DIM, lane >= HEAD_DIM)
-    total, hp = NS * dm.pairs, dm.pairs // 2
-
-    def place(i):
-        j = lax.rem(i, NS * hp)
-        half = i // (NS * hp)
-        hf = y + half * (1 - 2 * y)
-        return j // hp, hf * hp + lax.rem(j, hp)
-
-    def p_copy(i):
-        slot = lax.rem(i, 2)
-        s, p = place(i)
-        return pltpu.make_async_copy(p_hbm.at[s * dm.pairs + p], pbuf.at[slot], psem.at[slot])
-
-    p_copy(0).start()
-
     def attn(i):
         s, p = place(i)
-        slot = lax.rem(i, 2)
         rs, cs = al(s, R), al(p, 128)
-
-        @pl.when(i + 1 < total)
+        slab, pc = p_slot(i)
+
+        @pl.when(i + P_AHEAD - 1 < total)
         def _():
-            p_copy(i + 1).start()
+            p_copy(i + P_AHEAD - 1).start()
 
         p_copy(i).wait()
         q, k, v, do = q8[rs, cs], kk[rs, cs], vv[rs, cs], act[rs, pl.ds(pl.multiple_of(D + p * 128, 128), 128)]
         dv, dk = [], []
         for h in range(2):
-            pt = pbuf[slot, h]
+            pt = wup[slab, h * R : (h + 1) * R, pc][:, :R]
             pf = pt.astype(f32)
             dp = mmt(jnp.where(masks[h], v, jnp.bfloat16(0)), do)
             dsum = jnp.sum(pf * dp, 0, keepdims=True)
@@ -990,7 +992,12 @@
         lax.fori_loop(i0, i1, one, 0)
 
     half = NS * hp
-    attend(0, half, [(half // 3, lambda: red.steps(9, 10)), (half * 2 // 3, lambda: red.steps(10, 11))])
+
+    def seventh():
+        red.steps(7 * PER, 8 * PER - 1)
+        red.step(8 * PER - 1)
+
+    attend(0, half, [(half // 2, seventh)])
     for n in range(nt):
         cc = slice(n * 256, n * 256 + 256)
         p = over_samples(lambda s: mm(mixt[s, own_h, :], normed[s * R : s * R + R, cc]))
@@ -1001,36 +1008,28 @@
             dwa[sh * D : sh * D + hw, cc] = p[h]
             dwa[sh * D + hw : sh * D + 2 * hw, cc] = tk[h]
             dwa[sh * D + 2 * hw : sh * D + 3 * hw, cc] = tv[h]
-    a_own = pltpu.make_async_copy(dwa.at[al(c, D)], own.at[2], osem.at[2])
+    a_own = pltpu.make_async_copy(dwa.at[al(c, D)], own.at[pl.ds(2 * D, D)], osem.at[2])
     a_own.start()
-    a_sib = rcopy(dwa.at[al(1 - c, D)], sibl.at[2], xss.at[5], xrs.at[5], ln.sib)
+    a_sib = rcopy(dwa.at[al(1 - c, D)], sibl.at[pl.ds(2 * D, D)], xss.at[5], xrs.at[5], ln.sib)
     a_sib.start()
     onesr = jnp.ones((8, R), bf16)
     acc[8, :, 0 : 2 * hw] = over_samples(lambda s: mmt(onesr, mixt[s, own_h, :])) * 0.125
     acc[9, :, 0 : 2 * hw] = mm(ones, vv[:, own_h]) * 0.125
-    red.steps(11, 12)
+    third3 = NS * hp // 3
+    attend(half, half + third3, [])
     a_own.wait()
     a_sib.wait()
-    last.prefetch(0)
-    attend(
-        half,
-        total,
-        [
-            (half + 1, lambda: last.steps(0, 1)),
-            (half * 4 // 3, lambda: red.steps(12, red.waves - 1)),
-            (half * 5 // 3, lambda: last.steps(1, 2)),
-        ],
-    )
-    red.steps(red.waves - 1, red.waves)
-    red.finish()
-    last.steps(2, 3)
+    red.prefetch(8 * PER)
+    at(8)
+    attend(half + third3, total, [(half + 2 * third3, lambda: at(9))])
+    at(10)
 
     def gnorm1(s):
         rs = al(s, R)
         gn[rs, :] = tmm(mixt[s], wqkv[0:D, :]) + mm(kk[rs, :], wqkv[D : 2 * D, :]) + mm(vv[rs, :], wqkv[2 * D : 3 * D, :])
 
     loop(NS, gnorm1)
-    last.steps(3, 4)
+    at(11)
 
     def ln1b(s):
         for r0, n in row_chunks(dm):
@@ -1079,8 +1078,9 @@
         return carry
 
     lax.fori_loop(1, n_dp, spread, 0)
-    last.steps(4, last.waves)
-    last.finish()
+
+    red.steps(12 * PER, red.waves)
+    red.finish()
 
     def gathered(i, carry):
         peer(i).wait_send()
@@ -1103,14 +1103,14 @@
 def backward_call(dm, n_dp, small, big):
     M, D, f = dm.rows, dm.d, dm.f
     sds, vm, dma = jax.ShapeDtypeStruct, pltpu.VMEM, pltpu.SemaphoreType.DMA
-    st = sds((3, D, D), f32)
+    st = sds((3 * D, D), f32)
     outs = [st, sds((8, D), f32), sds((dm.samples, dm.r, D), f32), sds((dm.samples, dm.r, D), f32), st, st, sds((8 * n_dp, D), f32)]
     row, wide = vm((M, D), bf16), vm((M, 2 * f), bf16)
     scratch = [vm((3 * D, D), bf16), vm((D, D), bf16), vm((dm.n_t, D, f), bf16), vm((dm.ff, D), bf16), row]
     scratch += [vm((dm.ns, D, dm.r), bf16), row, vm((M, dm.ff), bf16), wide, vm((M, D), f32), vm((M, D), f32), vm((2 * D, D), f32), vm((10, 8, D), f32)]
-    scratch += [vm((2, 2, dm.r, dm.r), bf16), vm((2, 256, D), f32), vm((dm.n_t, 16, D), f32), vm((3, 8, D), f32)]
-    scratch += [dma((2,)), dma((2,)), dma((16,)), dma((7,)), dma((11,)), dma((11,)), dma((n_dp,)), dma((n_dp,))]
-    scratch += Reduce.scratch(2, N_SUB[0], D, D) + Reduce.scratch(1, N_SUB[1], D, D)
+    scratch += [vm((dm.n_t, 16, D), f32), vm((3, 8, D), f32)]
+    scratch += [dma((P_AHEAD,)), dma((3,)), dma((16,)), dma((7,)), dma((11,)), dma((11,)), dma((n_dp,)), dma((n_dp,))]
+    scratch += Reduce.scratch(3, N_SUB, D, D)
 
     def kern(*refs):
         backward_kernel(dm, n_dp, *refs)
@@ -1130,10 +1130,10 @@
     dm = Dims(tokens, w_up, n_t)
     D, hw, f = dm.d, dm.hw, dm.f
     small = (metadata, w_query.T, w_key.T, w_value.T, w_out, w_up, w_down, b_up, b_query, b_value, gain_one, shift_one, gain_two, shift_two, b_out)
-    (gu, gnw, _, p, wqkv, wo, bb, tok, cot, normed, q8, kk, vv, mixt, n2, act, gp, mid, d_own, d_sib) = forward_call(dm, n_dp, small, (tokens.transpose(1, 0, 2), cotangent.transpose(1, 0, 2)))
+    (gu, gnw, _, p, wqkv, wo, wu, bb, tok, cot, normed, q8, kk, vv, mixt, n2, act, gp, mid, d_own, d_sib) = forward_call(dm, n_dp, small, (tokens.transpose(1, 0, 2), cotangent.transpose(1, 0, 2)))
     small = (metadata, gain_one, gain_two, b_down)
-    fin, sm, lo, gt, *_ = backward_call(dm, n_dp, small, (w_down, gnw, gu, p, wqkv, wo, bb, tok, cot, normed, q8, kk, vv, mixt, n2, act, gp, mid, d_own, d_sib, w_up))
-    a_ = fin[2]
+    fin, sm, lo, gt, *_ = backward_call(dm, n_dp, small, (w_down, gnw, gu, p, wqkv, wo, wu, bb, tok, cot, normed, q8, kk, vv, mixt, n2, act, gp, mid, d_own, d_sib))
+    a_ = fin[2 * D :]
     return (
         lo[:, : dm.length].astype(bf16),
         gt[:, : dm.length],
@@ -1144,9 +1144,9 @@
         sm[7, :hw],
         sm[7, hw : 2 * hw],
         sm[1],
-        fin[1],
+        fin[D : 2 * D],
         sm[6],
-        fin[0],
+        fin[:D],
         sm[0],
         sm[2],
         sm[3],

time: 365 us -> 306 us (0.84)
  Pallas kernels: 345 us -> 287 us
    pallas_call x1, Pallas kernels: 247 us -> 193 us  [backward_call(): pl.pallas_call(kern, out_shape=outs, in_specs=[SM] + [V] * (len(small) -...]
    pallas_call x1, Pallas kernels: 98 us -> 94 us  [forward_call(): pl.pallas_call(kern, out_shape=outs, in_specs=[SM] + [V] * (len(small) -...]
where the time goes in v4:
time: 306 us
  Pallas kernels  287 us (94%)
  local copies, waits for them, and re-layouts  17.8 us (6%)
    pallas_call x1, Pallas kernels, backward_call(): pl.pallas_call(kern, out_shape=outs, in_specs=[SM] + [V] * (len(small) -...  193 us
    pallas_call x1, Pallas kernels, forward_call(): pl.pallas_call(kern, out_shape=outs, in_specs=[SM] + [V] * (len(small) -...  94 us
    unnamed x10, local copies, waits for them, and re-layouts  8.48 us

profile of v4, /device:TPU:0, one launch (start us, length us, event | category | flops | bytes accessed | tf_op | source)
XLA Modules:
  0.0 305.6 jit_solution(9005341950596260662)
XLA Ops:
  0.7 94.0 %forward.1 = (f32[4,960,768]{2,1,0:T(8,128)}, f32[4,768,768]{2,1,0:T(8,128)}, f32[768,768]{1,0:T(8,128)}, bf16[24,544,384]{2,1,0:T(8,128)(2,1)}, bf16[2304,768]{...) custom-call(s32[8]{0:T(128)} %refs_0_.3, ...), custom_call_target="tpu_custom_call" | custom-call | tf_op jit(solution)/shard_map/forward/pallas_call | solution.py:549
  94.6 193.1 %backward.1 = (f32[2304,768]{1,0:T(8,128)}, f32[8,768]{1,0:T(8,128)}, f32[8,272,768]{2,1,0:T(8,128)}, f32[8,272,768]{2,1,0:T(8,128)}, f32[2304,768]{1,0:T(8,128)...) custom-call(s32[8]{0:T(128)} %refs_0_.3, f32[768]{0:T(1024)} %refs_1_.1, f32[768]{0:T(1024)} %refs_2_.1, f32[768]{0:T(1024)} %refs_3_.1, ...), custom_call_target="tpu_custom_call" | custom-call | tf_op jit(solution)/shard_map/backward/pallas_call | solution.py:1118
  287.8 0.0 copy-start
  287.8 3.3 %slice.86 = bf16[8,258,768]{2,1,0:T(8,128)(2,1)S(1)} slice(f32[8,272,768]{2,1,0:T(8,128)} %get-tuple-element.61), slice={[0:8], [0:258], [0:768]} | slice | bytes 6340608 | tf_op jit(solution)/shard_map/slice | solution.py:1138
  291.1 0.0 copy-start.1
  291.1 2.3 copy.35
  293.4 0.0 copy-done.1
  293.4 0.6 fusion.2
  294.0 0.7 slice_reduce_fusion
  294.7 0.0 copy-done
  294.7 0.0 slice-start
  294.7 1.4 fusion.1
  296.1 0.0 slice-start.1
  296.1 2.7 fusion
  298.8 0.0 slice-done
  298.8 1.5 slice-done.1
  300.4 0.6 slice.58
  300.9 4.7 %copy.36 = f32[8,258,768]{2,0,1:T(8,128)} copy(f32[8,258,768]{2,1,0:T(8,128)S(1)} %slice.58) | data formatting | bytes 12681216
  (1 shorter events, 0.0 us)
Async XLA Ops:
  287.8 6.9 %copy-start = (f32[2304,768]{1,0:T(8,128)S(1)}, f32[2304,768]{1,0:T(8,128)}, u32[]{:S(2)}) copy-start(f32[2304,768]{1,0:T(8,128)} %get-tuple-element.63) | copy-start | bytes 21233668
  291.1 2.3 copy-start.1
  294.7 4.2 %slice-start = ((s8[6684672]{0:T(1024)(128)(4,1)}), s8[4194304]{0:T(1024)(128)(4,1)S(1)}, s32[]{:S(2)}) async-start(s8[6684672]{0:T(1024)(128)(4,1)} %bitcast.13), calls=%async_computation | async-start | bytes 8388608
  296.1 4.2 %slice-start.1 = ((s8[6684672]{0:T(1024)(128)(4,1)}), s8[2490368]{0:T(1024)(128)(4,1)S(1)}, s32[]{:S(2)}) async-start(s8[6684672]{0:T(1024)(128)(4,1)} %bitcast.13), calls=%async_computation.1 | async-start | bytes 4980736

commit v5 on v4

--- a/solution.py
+++ b/solution.py
@@ -137,8 +137,8 @@
 
 
 class Gather:
-    def __init__(self, ln, src, out, direct, ssem, rsem):
-        self.ln, self.src, self.out, self.direct = ln, src, out, direct
+    def __init__(self, ln, src, out, direct, ssem, rsem, head=0):
+        self.ln, self.src, self.out, self.direct, self.head = ln, src, out, direct, head
         self.ssem, self.rsem = ssem, rsem
         self.passed = self.passed_sib = False
         self.rows = src.shape[0]
@@ -157,8 +157,23 @@
         return self.copy(self.at(self.src, 0), self.at(self.out.at[self.ln.t], 0), 0, self.ln.ypart)
 
     def direct_y(self):
-        d = pl.ds(0, self.direct)
+        d = pl.ds(self.head, self.direct - self.head)
         return self.copy(self.src.at[d], self.out.at[self.ln.t].at[d], 1, self.ln.ypart)
+
+    def head_y(self):
+        d = pl.ds(0, self.head)
+        return self.copy(self.src.at[d], self.out.at[self.ln.t].at[d], 19, self.ln.ypart)
+
+    def head_sib(self):
+        v = self.out.at[self.ln.t_y].at[pl.ds(0, self.head)]
+        return self.copy(v, v, 20, self.ln.sib)
+
+    def head_landed(self):
+        self.landed(self.out.at[self.ln.t_y].at[pl.ds(0, self.head)], 19)
+        self.head_sib().start()
+
+    def head_sib_landed(self):
+        self.landed(self.out.at[self.ln.t_ysib].at[pl.ds(0, self.head)], 20)
 
     def whole_sib(self):
         return self.copy(self.src, self.out.at[self.ln.t], 2, self.ln.sib)
@@ -178,7 +193,7 @@
         return self.copy(v, v, 11 + 4 + offset, self.ln.sib)
 
     def direct_sib(self):
-        v = self.out.at[self.ln.t_y].at[pl.ds(0, self.direct)]
+        v = self.out.at[self.ln.t_y].at[pl.ds(self.head, self.direct - self.head)]
         return self.copy(v, v, 10, self.ln.sib)
 
     def ring_ahead(self, s):
@@ -211,13 +226,13 @@
     def direct_landed(self):
         if not self.passed:
             self.passed = True
-            self.landed(self.out.at[self.ln.t_y].at[pl.ds(0, self.direct)], 1)
+            self.landed(self.out.at[self.ln.t_y].at[pl.ds(self.head, self.direct - self.head)], 1)
             self.direct_sib().start()
 
     def direct_sib_landed(self):
         if not self.passed_sib:
             self.passed_sib = True
-            self.landed(self.out.at[self.ln.t_ysib].at[pl.ds(0, self.direct)], 10)
+            self.landed(self.out.at[self.ln.t_ysib].at[pl.ds(self.head, self.direct - self.head)], 10)
 
     def finish(self):
         ln, out = self.ln, self.out.at[self.ln.t_ysib]
@@ -227,14 +242,15 @@
         self.direct_sib_landed()
 
     def drain(self):
-        cps = [self.spread_y(), self.direct_y(), self.whole_sib(), self.direct_sib()]
+        cps = [self.head_y(), self.head_sib()] if self.head else []
+        cps += [self.spread_y(), self.direct_y(), self.whole_sib(), self.direct_sib()]
         cps += [self.ring_ahead(s) for s in range(4)] + [self.ring_behind(s) for s in range(3)]
         cps += [self.to_sib(o) for o in range(-4, 4)]
         for cp in cps:
             cp.wait_send()
 
 
-GATHER_SEMS = 19
+GATHER_SEMS = 21
 
 
 def keep_of(meta, base, s, r0, n):
@@ -285,7 +301,7 @@
         wqkv[pl.ds(pl.multiple_of(i * D + t * hw, 16), hw), :] = w[...]
     wo[al(t, hw), :] = wo_s[...]
     g_a = Gather(ln, own_a, ga, 16 + hw, ssa, rsa)
-    g_u = Gather(ln, ustage, gu, hw + D // 3, ssu, rsu)
+    g_u = Gather(ln, ustage, gu, hw + D // 3, ssu, rsu, hw)
     g_n = Gather(ln, n32, gn_h, D // 4, ssn, rsn)
     enter((ln.ypart, ln.sib, ln.ahead, ln.behind))
     g_a.start_y()
@@ -303,6 +319,7 @@
     g_u.spread_y().start()
     outs[0].wait()
     g_n.spread_y().start()
+    g_u.head_y().start()
     g_u.direct_y().start()
     g_n.direct_y().start()
     g_u.start_sib()
@@ -446,14 +463,14 @@
         g_u.tick(i)
         g_n.tick(i)
 
-    attend(1 - y, [(2, lambda: both(1)), (10, lambda: both(2))])
+    attend(1 - y, [(9, lambda: both(1))])
     put(mixt, o_mixt)
     g_a.drain()
-    g_u.direct_landed()
+    g_u.head_landed()
     wo_rows = [fetch(gu.at[tp, pl.ds(0, hw)], i) for i, tp in enumerate((ln.t_y,))]
     g_u.wait_sib()
     wo_rows.append(fetch(gu.at[ln.t_sib, pl.ds(0, hw)], 1))
-    g_u.direct_sib_landed()
+    g_u.head_sib_landed()
     wo_rows.append(fetch(gu.at[ln.t_ysib, pl.ds(0, hw)], 2))
     for i, tp in enumerate((ln.t_y, ln.t_sib, ln.t_ysib)):
         wo_rows[i].wait()
@@ -478,7 +495,7 @@
             xh, _ = centred(m)
             n2[rs, :] = (xh * g2 + s2).astype(bf16)
 
-    both(3)
+    both(2)
     loop(NS, ln2)
     put(mid, o_mid)
     put(n2, o_n2)
@@ -491,7 +508,7 @@
     mt = f // tw
 
     def mlp(i):
-        pl.when(i == NS * 2)(lambda: both(4))
+        pl.when(i == NS * 3)(lambda: both(3))
         s, j = i // (2 * mt), lax.rem(i, 2 * mt)
         rs, sh, cs = al(s, R), j // mt, al(lax.rem(j, mt), tw)
         h = mm(n2[rs, :], wup[sh, :, cs]) + bbuf[2 * y + sh, 0:1, cs]
@@ -512,8 +529,10 @@
     dwdn(1 - c)
     ex = rcopy(dwd.at[1 - c], d_sib, ssd.at[0], rsd.at[0], ln.sib)
     ex.start()
+    both(4)
     dwdn(c)
     put(dwd.at[c], d_own)
+    g_u.direct_landed()
     g_u.finish()
     g_n.direct_landed()
     g_n.wait_sib()

time: 306 us -> 294 us (0.961)
  Pallas kernels: 287 us -> 275 us
    pallas_call x1, Pallas kernels: 94 us -> 82.8 us  [forward_call(): pl.pallas_call(kern, out_shape=outs, in_specs=[SM] + [V] * (len(small) -...]
where the time goes in v5:
time: 294 us
  Pallas kernels  275 us (94%)
  local copies, waits for them, and re-layouts  17.8 us (6%)
    pallas_call x1, Pallas kernels, backward_call(): pl.pallas_call(kern, out_shape=outs, in_specs=[SM] + [V] * (len(small) -...  192 us
    pallas_call x1, Pallas kernels, forward_call(): pl.pallas_call(kern, out_shape=outs, in_specs=[SM] + [V] * (len(small) -...  82.8 us
    unnamed x10, local copies, waits for them, and re-layouts  8.48 us

profile of v5, /device:TPU:0, one launch (start us, length us, event | category | flops | bytes accessed | tf_op | source)
XLA Modules:
  0.0 293.8 jit_solution(12380862240166652631)
XLA Ops:
  0.7 82.8 %forward.1 = (f32[4,960,768]{2,1,0:T(8,128)}, f32[4,768,768]{2,1,0:T(8,128)}, f32[768,768]{1,0:T(8,128)}, bf16[24,544,384]{2,1,0:T(8,128)(2,1)}, bf16[2304,768]{...) custom-call(s32[8]{0:T(128)} %refs_0_.3, ...), custom_call_target="tpu_custom_call" | custom-call | tf_op jit(solution)/shard_map/forward/pallas_call | solution.py:568
  83.5 192.5 %backward.1 = (f32[2304,768]{1,0:T(8,128)}, f32[8,768]{1,0:T(8,128)}, f32[8,272,768]{2,1,0:T(8,128)}, f32[8,272,768]{2,1,0:T(8,128)}, f32[2304,768]{1,0:T(8,128)...) custom-call(s32[8]{0:T(128)} %refs_0_.3, f32[768]{0:T(1024)} %refs_1_.1, f32[768]{0:T(1024)} %refs_2_.1, f32[768]{0:T(1024)} %refs_3_.1, ...), custom_call_target="tpu_custom_call" | custom-call | tf_op jit(solution)/shard_map/backward/pallas_call | solution.py:1137
  275.9 0.0 copy-start
  276.0 3.3 %slice.86 = bf16[8,258,768]{2,1,0:T(8,128)(2,1)S(1)} slice(f32[8,272,768]{2,1,0:T(8,128)} %get-tuple-element.61), slice={[0:8], [0:258], [0:768]} | slice | bytes 6340608 | tf_op jit(solution)/shard_map/slice | solution.py:1157
  279.3 0.0 copy-start.1
  279.3 2.3 copy.35
  281.6 0.0 copy-done.1
  281.6 0.6 fusion.2
  282.2 0.7 slice_reduce_fusion
  282.9 0.0 copy-done
  282.9 0.0 slice-start
  282.9 1.4 fusion.1
  284.3 0.0 slice-start.1
  284.3 2.7 fusion
  287.0 0.0 slice-done
  287.0 1.5 slice-done.1
  288.5 0.6 slice.58
  289.1 4.7 %copy.36 = f32[8,258,768]{2,0,1:T(8,128)} copy(f32[8,258,768]{2,1,0:T(8,128)S(1)} %slice.58) | data formatting | bytes 12681216
  (1 shorter events, 0.0 us)
Async XLA Ops:
  275.9 6.9 %copy-start = (f32[2304,768]{1,0:T(8,128)S(1)}, f32[2304,768]{1,0:T(8,128)}, u32[]{:S(2)}) copy-start(f32[2304,768]{1,0:T(8,128)} %get-tuple-element.63) | copy-start | bytes 21233668
  279.3 2.3 copy-start.1
  282.9 4.2 %slice-start = ((s8[6684672]{0:T(1024)(128)(4,1)}), s8[4194304]{0:T(1024)(128)(4,1)S(1)}, s32[]{:S(2)}) async-start(s8[6684672]{0:T(1024)(128)(4,1)} %bitcast.13), calls=%async_computation | async-start | bytes 8388608
  284.3 4.2 %slice-start.1 = ((s8[6684672]{0:T(1024)(128)(4,1)}), s8[2490368]{0:T(1024)(128)(4,1)S(1)}, s32[]{:S(2)}) async-start(s8[6684672]{0:T(1024)(128)(4,1)} %bitcast.13), calls=%async_computation.1 | async-start | bytes 4980736

commit v6 on v5

--- a/solution.py
+++ b/solution.py
@@ -577,13 +577,13 @@
 
 
 class Reduce:
-    KINDS = 7
+    KINDS = 9
 
     @staticmethod
     def scratch(n_arrays, n_sub, rows, width):
         pr, nq = rows // 4 // n_sub, n_arrays * n_sub
         vm, dma = pltpu.VMEM, pltpu.SemaphoreType.DMA
-        return [vm((2, 2, 4 * pr, width), f32), vm((2, 7 * pr, width), f32), vm((nq, 5 * pr, width), f32), dma((2, 3, 2)), dma((2, 2)), dma((2, 11)), dma((nq, Reduce.KINDS))]
+        return [vm((2, 2, 4 * pr, width), f32), vm((2, 7 * pr, width), f32), vm((nq, 7 * pr, width), f32), dma((2, 3, 2)), dma((2, 2)), dma((2, 13)), dma((nq, Reduce.KINDS))]
 
     def __init__(self, ln, head, own, sib, fin, height, n_arrays, n_sub, vin, vout, land, lsem, fsem, ssem, rsem):
         self.ln, self.head, self.own, self.sibling, self.fin = ln, head, own, sib, fin
@@ -592,11 +592,19 @@
         self.pr = height // 4 // n_sub
         L, z, x = ln.length, ln.z, ln.x
         self.L = L
-        self.waves = self.total + 2 * L
-        up = 2 * x - 1
-        self.k = ((1 - x) * (L - 1 - z) + x * z, x * (L - 1 - z) + (1 - x) * z)
-        self.up = ((2 * (z + up) + x, ln.t), (2 * (z - up) + x, ln.t))
-        self.down = (self.up[1], self.up[0])
+        self.K = L // 2
+        self.waves = self.total + 2 * self.K + 2
+        rows = (L // 2 - 1 + x, L // 2 - x)
+        self.root = [z == r for r in rows]
+        self.from_above = [z == r + 1 for r in rows]
+        self.dist = [jnp.abs(z - r) for r in rows]
+        below = [(z < r).astype(jnp.int32) for r in rows]
+        at_root = [(z == r).astype(jnp.int32) for r in rows]
+        self.k = [o * self.K + (1 - o) * (b * z + (1 - b) * (L - 1 - z)) for o, b in zip(at_root, below)]
+        self.up = [(2 * (z + 2 * b - 1) + x, ln.t) for b in below]
+        self.down = [(2 * (z - 2 * b + 1) + x, ln.t) for b in below]
+        self.lower, self.higher = (2 * (z - 1) + x, ln.t), (2 * (z + 1) + x, ln.t)
+        self.has_lower, self.has_higher = z > 0, z < L - 1
         self.partner = (2 * z + 1 - x, ln.t)
         self.parts = ((2 * x, 2), (2 * (1 - x) + 1, 1), (2 * (1 - x), 1))
 
@@ -670,11 +678,11 @@
                 o[...] = summed(2, q_leaf)
             run(self.send(o, self.box(q_leaf, 3), slot, 0, q_leaf, 0, self.partner))
 
-        q_met = tau - L - 1
+        q_met = tau - self.K - 2
         for i in range(2):
             n, part = (2, 0) if i == 0 else (1, 2)
 
-            @pl.when(self.ok(q_met) & (self.k[i] == L - 1))
+            @pl.when(self.ok(q_met) & self.root[i])
             def _():
                 tot = out(4 + 2 * i, n)
                 if start:
@@ -684,7 +692,8 @@
                         tot[0:pr] = self.vout[1 - slot, 0:pr]
                     tot[(n - 1) * pr : n * pr] = self.vout[1 - slot, a : a + pr] + self.land[q_met, 4 * pr : 5 * pr]
                 fv = self.view(self.fin, q_met, i)
-                run(self.send(tot, fv, slot, 2 if i == 0 else 7, q_met, 4 if i == 0 else 6, self.down[i]))
+                pl.when(self.has_lower)(lambda: run(self.send(tot, fv, slot, 2 if i == 0 else 7, q_met, 4 if i == 0 else 6, self.lower)))
+                pl.when(self.has_higher)(lambda: run(self.send(tot, fv, slot, 11 + i, q_met, 4 if i == 0 else 6, self.higher)))
                 if i == 0:
                     run(self.send(out(4), self.view(self.fin, q_met, 0, 0, 1), slot, 3, q_met, 5, self.partner))
                 cp = pltpu.make_async_copy(tot, fv, self.fsem.at[i, slot])
@@ -692,10 +701,9 @@
 
         for i in range(2):
             k = self.k[i]
-            r = L - 1 - k
-            q = tau - L - 1 - r
-
-            @pl.when(self.ok(q) & (r > 0))
+            q = tau - self.K - 2 - self.dist[i]
+
+            @pl.when(self.ok(q) & ~self.root[i])
             def _():
                 fv = self.view(self.fin, q, i)
                 if start:
@@ -725,16 +733,23 @@
                     else:
                         o[...] = v
 
-                    @pl.when(k > 0)
+                    root = self.root[i]
+
+                    @pl.when((~root & (k > 0)) | (root & self.has_lower))
                     def _():
                         self.landed(self.box(q, part, n), q, 1 + i)
                         o[...] += self.land[q, part * pr : (part + n) * pr]
 
-                @pl.when(k < L - 1)
-                def _():
-                    run(self.send(o, self.box(q, part, n), slot, 1 if i == 0 else 5, q, 1 + i, self.up[i]))
-
-                @pl.when(k == L - 1)
+                    @pl.when(root & self.has_higher)
+                    def _():
+                        self.landed(self.box(q, 5, n), q, 7 + i)
+                        o[...] += self.land[q, 5 * pr : (5 + n) * pr]
+
+                up = 1 if i == 0 else 5
+                pl.when(~self.root[i] & ~self.from_above[i])(lambda: run(self.send(o, self.box(q, part, n), slot, up, q, 1 + i, self.up[i])))
+                pl.when(self.from_above[i])(lambda: run(self.send(o, self.box(q, 5, n), slot, up, q, 7 + i, self.up[i])))
+
+                @pl.when(self.root[i])
                 def _():
                     run(self.send(out(part + n - 1), self.box(q, 4), slot, 4 if i == 0 else 6, q, 3, self.partner))
 
@@ -952,7 +967,6 @@
         act[rs, D : 2 * D] = mmt(act[rs, 0:D], wo[...]).astype(bf16)
 
     loop(NS, gmixf)
-    at(6)
     own_h = al(y, 2 * hw)
 
     def over_samples(fn):
@@ -1016,7 +1030,7 @@
         red.steps(7 * PER, 8 * PER - 1)
         red.step(8 * PER - 1)
 
-    attend(0, half, [(half // 2, seventh)])
+    attend(0, half, [(half // 2, lambda: at(6))])
     for n in range(nt):
         cc = slice(n * 256, n * 256 + 256)
         p = over_samples(lambda s: mm(mixt[s, own_h, :], normed[s * R : s * R + R, cc]))
@@ -1031,6 +1045,7 @@
     a_own.start()
     a_sib = rcopy(dwa.at[al(1 - c, D)], sibl.at[pl.ds(2 * D, D)], xss.at[5], xrs.at[5], ln.sib)
     a_sib.start()
+    seventh()
     onesr = jnp.ones((8, R), bf16)
     acc[8, :, 0 : 2 * hw] = over_samples(lambda s: mmt(onesr, mixt[s, own_h, :])) * 0.125
     acc[9, :, 0 : 2 * hw] = mm(ones, vv[:, own_h]) * 0.125

time: 294 us -> 291 us (0.990)
  Pallas kernels: 275 us -> 272 us
where the time goes in v6:
time: 291 us
  Pallas kernels  272 us (93%)
  local copies, waits for them, and re-layouts  17.8 us (6%)
    pallas_call x1, Pallas kernels, backward_call(): pl.pallas_call(kern, out_shape=outs, in_specs=[SM] + [V] * (len(small) -...  190 us
    pallas_call x1, Pallas kernels, forward_call(): pl.pallas_call(kern, out_shape=outs, in_specs=[SM] + [V] * (len(small) -...  82.8 us
    unnamed x10, local copies, waits for them, and re-layouts  8.48 us

profile of v6, /device:TPU:0, one launch (start us, length us, event | category | flops | bytes accessed | tf_op | source)
XLA Modules:
  0.0 290.9 jit_solution(10112062462432338884)
XLA Ops:
  0.7 82.8 %forward.1 = (f32[4,960,768]{2,1,0:T(8,128)}, f32[4,768,768]{2,1,0:T(8,128)}, f32[768,768]{1,0:T(8,128)}, bf16[24,544,384]{2,1,0:T(8,128)(2,1)}, bf16[2304,768]{...) custom-call(s32[8]{0:T(128)} %refs_0_.3, ...), custom_call_target="tpu_custom_call" | custom-call | tf_op jit(solution)/shard_map/forward/pallas_call | solution.py:568
  83.5 189.6 %backward.1 = (f32[2304,768]{1,0:T(8,128)}, f32[8,768]{1,0:T(8,128)}, f32[8,272,768]{2,1,0:T(8,128)}, f32[8,272,768]{2,1,0:T(8,128)}, f32[2304,768]{1,0:T(8,128)...) custom-call(s32[8]{0:T(128)} %refs_0_.3, f32[768]{0:T(1024)} %refs_1_.1, f32[768]{0:T(1024)} %refs_2_.1, f32[768]{0:T(1024)} %refs_3_.1, ...), custom_call_target="tpu_custom_call" | custom-call | tf_op jit(solution)/shard_map/backward/pallas_call | solution.py:1152
  273.1 0.0 copy-start
  273.1 3.3 %slice.86 = bf16[8,258,768]{2,1,0:T(8,128)(2,1)S(1)} slice(f32[8,272,768]{2,1,0:T(8,128)} %get-tuple-element.61), slice={[0:8], [0:258], [0:768]} | slice | bytes 6340608 | tf_op jit(solution)/shard_map/slice | solution.py:1172
  276.4 0.0 copy-start.1
  276.4 2.3 copy.35
  278.7 0.0 copy-done.1
  278.7 0.6 fusion.2
  279.3 0.7 slice_reduce_fusion
  280.0 0.0 copy-done
  280.0 0.0 slice-start
  280.0 1.4 fusion.1
  281.4 0.0 slice-start.1
  281.4 2.7 fusion
  284.1 0.0 slice-done
  284.1 1.5 slice-done.1
  285.7 0.6 slice.58
  286.2 4.7 %copy.36 = f32[8,258,768]{2,0,1:T(8,128)} copy(f32[8,258,768]{2,1,0:T(8,128)S(1)} %slice.58) | data formatting | bytes 12681216
  (1 shorter events, 0.0 us)
Async XLA Ops:
  273.1 6.9 %copy-start = (f32[2304,768]{1,0:T(8,128)S(1)}, f32[2304,768]{1,0:T(8,128)}, u32[]{:S(2)}) copy-start(f32[2304,768]{1,0:T(8,128)} %get-tuple-element.63) | copy-start | bytes 21233668
  276.4 2.3 copy-start.1
  280.0 4.2 %slice-start = ((s8[6684672]{0:T(1024)(128)(4,1)}), s8[4194304]{0:T(1024)(128)(4,1)S(1)}, s32[]{:S(2)}) async-start(s8[6684672]{0:T(1024)(128)(4,1)} %bitcast.13), calls=%async_computation | async-start | bytes 8388608
  281.4 4.2 %slice-start.1 = ((s8[6684672]{0:T(1024)(128)(4,1)}), s8[2490368]{0:T(1024)(128)(4,1)S(1)}, s32[]{:S(2)}) async-start(s8[6684672]{0:T(1024)(128)(4,1)} %bitcast.13), calls=%async_computation.1 | async-start | bytes 4980736
